TPU v7x, 256 devices: a whole 4x4x8 slice. The times are simulated.
256 devices in a mesh: fov: 64 (over x, z, y_lo), row: 4 (over y_hi, core).
Axes of the slice: x: 4, y: 4 (y_hi: 2, y_lo: 2; y = y_hi * 2 + y_lo), z: 8, core: 2. Of those that a mesh axis runs over, the one named last changes fastest.
Arguments:
- frames: bfloat16 [64, 5, 512, 512], P('fov', None, 'row'), parts along dimension 0, may hold values from 0.01 to 13, as said below
- phase_offset: float32 [64], P('fov'), parts along dimension 0, may hold values from -3.140625 to 3.140625
- order_gain: float32 [64, 5], P('fov'), parts along dimension 0, may hold values from 0.5 to 2
- band_shift: int32 [64, 2], P('fov'), parts along dimension 0, may hold values from -96 to 96
Outputs:
- picture: float32 [65536, 1024], P(('fov', 'row')), parts along dimension 0
There are 64 independent parts, one for each index of `fov`. A program takes and returns all parts, laid end to end along the dimension named above; each array names one. Nothing has to cross between parts.
Inputs may be any that keep to these rules, and one draw needn't show every extreme that they name: `frames`: positive intensities. `band_shift`: offsets in frequency bins of the 1024-point grid, row component first.
All inputs are finite; a program needn't handle non-finite values.
Results may differ from a plain program's by a relative error of at most 0.0003.
Values sent between devices are 32-bit elements; how exact they have to be, the bound alone decides.
No kernel may reach another device: no remote copies, remote signals or barrier semaphores. Data moves between devices by JAX's collectives and lax.ppermute only.
A program may use at most 128 MiB of HBM per device.

v0:
```python
import functools
import math

import jax
import jax.numpy as jnp
import numpy as np
from jax import lax
from jax.experimental import pallas as pl
from jax.experimental.pallas import tpu as pltpu
from jax.sharding import PartitionSpec as P

wiener = 0.1
gain_out = 8.0
cut_share = 0.45
PIX = 512
GRID = 1024
PHASES = 5
PARTS = 4
ROWS = PIX // PARTS
MAIN = 64
FOLD = 48
COLS = MAIN + FOLD
EXT = 72


def split_np(array):
    hi = array.astype(jnp.bfloat16)
    lo = (array - hi.astype(np.float32)).astype(jnp.bfloat16)
    return hi, lo


def split(array):
    hi = array.astype(jnp.bfloat16)
    lo = (array - hi.astype(jnp.float32)).astype(jnp.bfloat16)
    return hi, lo


@functools.cache
def tables():
    index = np.arange(PIX)
    angle = 2.0 * np.pi * (np.outer(index, index) % PIX) / PIX
    cos_all = np.cos(angle).astype(np.float32)
    sin_all = np.sin(angle).astype(np.float32)
    sin_half = sin_all[: PIX // 2].copy()
    sin_half[0] = cos_all[PIX // 2]
    x_table = np.stack(
        [np.concatenate([cos_all[d : PIX // 2 : PARTS], sin_half[d::PARTS]]) for d in range(PARTS)]
    )
    y_table = np.stack(
        [
            np.stack([cos_all[s * ROWS : (s + 1) * ROWS], sin_all[s * ROWS : (s + 1) * ROWS]])
            for s in range(PARTS)
        ]
    )
    first = np.zeros((PARTS, 2, COLS, 128), np.float32)
    step = np.zeros((PARTS, 2, COLS, 128), np.float32)
    for s in range(PARTS):
        freq = column_freq_np(s)
        scale = gain_out / (GRID * GRID) * np.where(freq == 0, 1.0, 2.0)
        turn = 2.0 * np.pi * ((freq[:, None] * np.arange(128)[None, :]) % GRID) / GRID
        first[s, 0] = scale[:, None] * np.cos(turn)
        first[s, 1] = scale[:, None] * np.sin(turn)
        turn = 2.0 * np.pi * (freq % 8) / 8
        step[s, 0] = np.cos(turn)[:, None]
        step[s, 1] = np.sin(turn)[:, None]
    turn = 2.0 * np.pi * index / GRID
    odd = np.stack([np.cos(turn), np.sin(turn)]).astype(np.float32)
    return split_np(x_table), split_np(y_table), first, step, odd


def column_freq_np(d):
    main = 4 * np.arange(MAIN) + d
    fold = 4 * np.arange(16, 64) + d - PIX
    if d == 0:
        fold[0] = -PIX // 2
    return np.concatenate([main, fold])


def dot3(left, right, dims):
    lhs = jnp.concatenate([left[0], left[0], left[1]], axis=dims[0])
    rhs = jnp.concatenate([right[0], right[1], right[0]], axis=dims[1])
    return lax.dot_general(
        lhs, rhs, (((dims[0],), (dims[1],)), ((), ())), preferred_element_type=jnp.float32
    )


def turn_pair(steps):
    angle = (2.0 * math.pi / PIX) * ((steps + 256) % 512 - 256).astype(jnp.float32)
    return jnp.cos(angle), jnp.sin(angle)


def forward_kernel(place, shift, offset, totals, frames, x_hi, x_lo, *outs):
    rank = place[0]
    shift_y = shift[0, 0]
    shift_x = shift[0, 1]
    x_cos, x_sin = turn_pair(lax.broadcasted_iota(jnp.int32, (8, PIX), 1) * shift_x)
    row_at = lax.broadcasted_iota(jnp.int32, (ROWS, 128), 0) + rank * ROWS
    y_cos, y_sin = turn_pair(row_at * shift_y)
    x_cos, x_sin = x_cos[:1], x_sin[:1]
    y_cos, y_sin = y_cos[:, :1], y_sin[:, :1]
    turn_re = x_cos * y_cos - x_sin * y_sin
    turn_im = x_cos * y_sin + x_sin * y_cos
    twice_re = turn_re * turn_re - turn_im * turn_im
    twice_im = 2.0 * turn_re * turn_im
    phase_at = lax.broadcasted_iota(jnp.int32, (8, 128), 0).astype(jnp.float32)
    phase_at = (2.0 * math.pi / PHASES) * phase_at + offset[0]
    cos_one, sin_one = jnp.cos(phase_at), jnp.sin(phase_at)
    cos_two, sin_two = jnp.cos(2.0 * phase_at), jnp.sin(2.0 * phase_at)
    sums = [None] * 5
    for p in range(PHASES):
        weight = (PIX * PIX / PHASES) / jnp.full((1, 1), totals[0, p], jnp.float32)
        plane = weight * frames[0, p].astype(jnp.float32)
        at = (slice(p, p + 1), slice(0, 1))
        terms = [
            plane,
            plane * cos_one[at],
            plane * sin_one[at],
            plane * cos_two[at],
            plane * sin_two[at],
        ]
        sums = terms if p == 0 else [a + b for a, b in zip(sums, terms)]
    zero, one_re, one_im, two_re, two_im = sums
    planes = [
        zero,
        one_re * turn_re + one_im * turn_im,
        one_re * turn_im - one_im * turn_re,
        two_re * twice_re + two_im * twice_im,
        two_re * twice_im - two_im * twice_re,
    ]
    band = split(jnp.concatenate(planes, axis=0))
    table = (
        jnp.concatenate([x_hi[rank ^ k] for k in range(PARTS)], axis=0),
        jnp.concatenate([x_lo[rank ^ k] for k in range(PARTS)], axis=0),
    )
    spectra = dot3(table, band, (1, 1))
    for k in range(PARTS):
        for plane in range(5):
            outs[k][plane] = spectra[k * 128 : (k + 1) * 128, plane * ROWS : (plane + 1) * ROWS]


def middle_kernel(place, got0, got1, got2, got3, weights, y_hi, y_lo, odd, *outs):
    rank = place[0]
    blocks = (got0, got1, got2, got3)
    first_row = lax.broadcasted_iota(jnp.int32, (MAIN, PIX), 0) == 0
    lone = jnp.logical_and(first_row, jnp.full((MAIN, PIX), rank, jnp.int32) == 0)
    top = lax.broadcasted_iota(jnp.int32, (EXT - MAIN, PIX), 0) == 0

    def plane(index):
        whole = jnp.concatenate([b[index] for b in blocks], axis=1)
        sines = whole[MAIN:]
        extra = jnp.where(top, sines[: EXT - MAIN], 0.0)
        return whole[:MAIN], jnp.where(lone, 0.0, sines), extra

    real_rows = []
    imag_rows = []
    cos_r, sin_r, extra_r = plane(0)
    real_rows += [cos_r, extra_r]
    imag_rows += [-sin_r, jnp.zeros_like(extra_r)]
    for m in range(2):
        cos_r, sin_r, extra_r = plane(1 + 2 * m)
        cos_i, sin_i, extra_i = plane(2 + 2 * m)
        real_rows += [cos_r + sin_i, extra_r, cos_r - sin_i, extra_r]
        imag_rows += [cos_i - sin_r, extra_i, -cos_i - sin_r, -extra_i]
    data = split(jnp.concatenate(real_rows + imag_rows, axis=0))

    def y_block(ref, k, part):
        return ref[rank ^ k, part]

    def y_matrix(ref):
        return jnp.concatenate(
            [
                jnp.concatenate([y_block(ref, k, 0), y_block(ref, k, 1)], axis=1)
                for k in range(PARTS)
            ],
            axis=0,
        )

    turned = dot3(data, (y_matrix(y_hi), y_matrix(y_lo)), (1, 0))
    half = 5 * EXT
    spec_re = turned[:half, :PIX] + turned[half:, PIX:]
    spec_im = turned[half:, :PIX] - turned[:half, PIX:]
    even_re = even_im = odd_re = odd_im = None
    tile_top = lax.broadcasted_iota(jnp.int32, (8, PIX), 0) == 0
    for order in range(5):
        def rows(spec):
            main = spec[order * EXT : order * EXT + MAIN]
            extra = spec[order * EXT + MAIN : (order + 1) * EXT]
            tile = jnp.where(tile_top, extra, main[16:24])
            return jnp.concatenate([main, tile, main[24:]], axis=0)

        re, im = rows(spec_re), rows(spec_im)
        plus, minus = weights[order, 0], weights[order, 1]
        terms = (plus * re, plus * im, minus * re, minus * im)
        if order == 0:
            even_re, even_im, odd_re, odd_im = terms
        else:
            even_re, even_im = even_re + terms[0], even_im + terms[1]
            odd_re, odd_im = odd_re + terms[2], odd_im + terms[3]
    odd_cos, odd_sin = odd[0:1], odd[1:2]
    odd_re, odd_im = odd_re * odd_cos - odd_im * odd_sin, odd_re * odd_sin + odd_im * odd_cos
    filtered = split(jnp.concatenate([even_re, even_im, odd_re, odd_im], axis=0))

    def u_matrix(ref):
        return jnp.concatenate(
            [
                jnp.concatenate([y_block(ref, k, 0), y_block(ref, k, 1)], axis=0)
                for k in range(PARTS)
            ],
            axis=0,
        )

    back = dot3(filtered, (u_matrix(y_hi), u_matrix(y_lo)), (1, 1))
    for k in range(PARTS):
        cos_part = back[:, 2 * ROWS * k : 2 * ROWS * k + ROWS]
        sin_part = back[:, 2 * ROWS * k + ROWS : 2 * ROWS * (k + 1)]
        for parity in range(2):
            base = 2 * COLS * parity
            re, im = slice(base, base + COLS), slice(base + COLS, base + 2 * COLS)
            outs[k][0:COLS, parity * ROWS : (parity + 1) * ROWS] = cos_part[re] - sin_part[im]
            outs[k][COLS : 2 * COLS, parity * ROWS : (parity + 1) * ROWS] = (
                sin_part[re] + cos_part[im]
            )


def final_kernel(place, got0, got1, got2, got3, first, step, out, woven):
    rank = place[0]
    blocks = (got0, got1, got2, got3)
    table_rows = []
    for k in range(PARTS):
        source = rank ^ k
        re, im = first[source, 0], first[source, 1]
        step_re, step_im = step[source, 0], step[source, 1]
        res, ims = [re], [-im]
        for _ in range(7):
            re, im = re * step_re - im * step_im, re * step_im + im * step_re
            res.append(re)
            ims.append(-im)
        table_rows += [jnp.concatenate(res, axis=1), jnp.concatenate(ims, axis=1)]
    table = split(jnp.concatenate(table_rows, axis=0))
    data = split(jnp.concatenate([b[...] for b in blocks], axis=0))
    picture = dot3(data, table, (0, 0))
    for block in range(GRID // 128):
        lanes = slice(128 * block, 128 * (block + 1))
        woven[block, pl.ds(0, ROWS, 2), :] = picture[:ROWS, lanes]
        woven[block, pl.ds(1, ROWS, 2), :] = picture[ROWS:, lanes]
        out[:, lanes] = woven[block]


def order_weights(rank, gains, shift):
    cutoff = cut_share * PIX
    row = jnp.arange(COLS, dtype=jnp.int32)
    freq_x = jnp.where(row < MAIN, 4 * row + rank, 4 * (row - FOLD) + rank - PIX)
    freq_x = jnp.where((row == MAIN) & (rank == 0), -PIX // 2, freq_x)
    freq_y = (
        jnp.arange(PIX, dtype=jnp.int32)[None, :] - PIX * jnp.arange(2, dtype=jnp.int32)[:, None]
    )
    curves = []
    for m in (0, 1, -1, 2, -2):
        x = (freq_x - m * shift[1]).astype(jnp.float32)[None, :, None]
        y = (freq_y - m * shift[0]).astype(jnp.float32)[:, None, :]
        radius = jnp.minimum(jnp.sqrt(y * y + x * x) / cutoff, 1.0)
        curves.append(
            2.0 / math.pi * (jnp.arccos(radius) - radius * jnp.sqrt(1.0 - radius * radius))
        )
    own = [gains[2], gains[3], gains[1], gains[4], gains[0]]
    other = [gains[2], gains[1], gains[3], gains[0], gains[4]]
    own_den = wiener + sum(g * g * c * c for g, c in zip(own, curves))
    other_den = wiener + sum(g * g * c * c for g, c in zip(other, curves))
    own_den = 0.5 / own_den
    other_den = 0.5 / other_den
    result = []
    for g, h, c in zip(own, other, curves):
        weight = c * (g * own_den + h * other_den)
        result.append(jnp.stack([weight[0] + weight[1], weight[0] - weight[1]]))
    return jnp.stack(result)


def smem():
    return pl.BlockSpec(memory_space=pltpu.SMEM)


def vmem():
    return pl.BlockSpec(memory_space=pltpu.VMEM)


def from_partners(blocks):
    got = [blocks[0]]
    for k in range(1, PARTS):
        got.append(lax.ppermute(blocks[k], "row", [(i, i ^ k) for i in range(PARTS)]))
    return got


def per_device(frames, phase_offset, order_gain, band_shift):
    (x_hi, x_lo), (y_hi, y_lo), first, step, odd = tables()
    rank = lax.axis_index("row")
    place = rank.reshape(1).astype(jnp.int32)
    totals = lax.psum(jnp.sum(frames.astype(jnp.float32), axis=(2, 3)), "row")
    params = pltpu.CompilerParams(vmem_limit_bytes=40 * 1024 * 1024)
    sent = pl.pallas_call(
        forward_kernel,
        out_shape=[jax.ShapeDtypeStruct((5, 128, ROWS), jnp.float32)] * PARTS,
        in_specs=[smem()] * 4 + [vmem()] * 3,
        out_specs=[vmem()] * PARTS,
        compiler_params=params,
    )(place, band_shift, phase_offset, totals, frames, x_hi, x_lo)
    got = from_partners(sent)
    weights = order_weights(rank, order_gain[0], band_shift[0])
    sent = pl.pallas_call(
        middle_kernel,
        out_shape=[jax.ShapeDtypeStruct((2 * COLS, 2 * ROWS), jnp.float32)] * PARTS,
        in_specs=[smem()] + [vmem()] * 8,
        out_specs=[vmem()] * PARTS,
        compiler_params=params,
    )(place, *got, weights, y_hi, y_lo, odd)
    got = from_partners(sent)
    return pl.pallas_call(
        final_kernel,
        out_shape=jax.ShapeDtypeStruct((2 * ROWS, GRID), jnp.float32),
        in_specs=[smem()] + [vmem()] * 6,
        out_specs=vmem(),
        scratch_shapes=[pltpu.VMEM((GRID // 128, 2 * ROWS, 128), jnp.float32)],
        compiler_params=params,
    )(place, *got, first, step)


def solution(mesh):
    in_specs = (P("fov", None, "row", None), P("fov"), P("fov", None), P("fov", None))
    out_specs = P(("fov", "row"), None)
    return jax.shard_map(
        per_device, mesh=mesh, in_specs=in_specs, out_specs=out_specs, check_vma=False
    )
```

profile of v0, /device:TPU:1, one launch (start us, length us, event | category | flops | bytes accessed | tf_op | source)
XLA Modules:
  0.0 75.7 jit_solution(3834505677128478425)
XLA Ops:
  0.0 0.0 copy-start.9
  0.0 1.3 %convert_reduce_fusion = f32[5]{0:T(128)S(1)} fusion(bf16[1,5,128,512]{3,2,1,0:T(8,128)(2,1)} %frames.1), kind=kLoop, calls=%fused_computation | loop fusion | flops 655355 | bytes 655380 | tf_op jit(solution)/shard_map/reduce_sum | solution.py:297
  1.3 9.7 %psum.7.totals = f32[1,5]{1,0:T(1,128)S(1)} all-reduce(f32[1,5]{1,0:T(1,128)S(1)} %bitcast.29), channel_id=1, replica_groups=mesh['fov'=64,'row'=4] {'row'}, use_global_device_ids=true, to_apply=%region_1.0 | all-reduce | flops 5 | bytes 40 | tf_op jit(solution)/shard_map/psum | solution.py:297
  11.7 0.0 copy-start
  11.7 1.1 %copy-done = bf16[1,5,128,512]{3,2,1,0:T(8,128)(2,1)S(1)} copy-done((bf16[1,5,128,512]{3,2,1,0:T(8,128)(2,1)S(1)}, bf16[1,5,128,512]{3,2,1,0:T(8,128)(2,1)}, u32[]{:S(2)}) %copy-start) | copy-done | bytes 655384
  12.7 0.0 copy-start.3
  12.7 1.0 %copy-done.3 = bf16[4,128,512]{2,1,0:T(8,128)(2,1)S(1)} copy-done((bf16[4,128,512]{2,1,0:T(8,128)(2,1)S(1)}, bf16[4,128,512]{2,1,0:T(8,128)(2,1)}, u32[]{:S(2)}) %copy-start.3) | copy-done | bytes 524312
  13.8 0.0 copy-start.4
  13.8 1.0 %copy-done.4 = bf16[4,128,512]{2,1,0:T(8,128)(2,1)S(1)} copy-done((bf16[4,128,512]{2,1,0:T(8,128)(2,1)S(1)}, bf16[4,128,512]{2,1,0:T(8,128)(2,1)}, u32[]{:S(2)}) %copy-start.4) | copy-done | bytes 524312
  14.8 0.0 copy-start.7
  14.8 0.7 copy-done.7
  15.5 2.8 %shard_map.109 = (f32[5,128,128]{2,1,0:T(8,128)S(1)}, f32[5,128,128]{2,1,0:T(8,128)S(1)}, f32[5,128,128]{2,1,0:T(8,128)S(1)}, f32[5,128,128]{2,1,0:T(8,128)S(1)}) custom-call(s32[1]{0:T(128)} %bitcast.place, s32[1,2]{1,0:T(1,128)S(1)} %copy-done.7, f32[1]{0:T(128)S(6)} %copy.16.offset, f32[1,5]{1,0:T(1,128)S(1)} %psum.7.totals, ...), custom_call_target="tpu_custom_call" | custom-call | tf_op jit(solution)/shard_map/pallas_call | solution.py:299
  18.3 2.0 %collective-permute-start = (f32[5,128,128]{2,1,0:T(8,128)S(1)}, f32[5,128,128]{2,1,0:T(8,128)S(1)}, u32[]{:S(2)}, u32[]{:S(2)}) collective-permute-start(f32[5,128,128]{2,1,0:T(8,128)S(1)} %get-tuple-element.14), channel_id=1, source_target_pairs={{0,1},{1,0},{2,3},{3,2},{4,5},{5,4},{6,7},{7,6},{8,9},{9,8},{10,11... | collective-permute-start | bytes 983048 | tf_op jit(solution)/shard_map/ppermute | solution.py:289
  20.3 0.0 collective-permute-start.1
  20.3 3.2 %collective-permute-start.2 = (f32[5,128,128]{2,1,0:T(8,128)S(1)}, f32[5,128,128]{2,1,0:T(8,128)S(1)}, u32[]{:S(2)}, u32[]{:S(2)}) collective-permute-start(f32[5,128,128]{2,1,0:T(8,128)S(1)} %get-tuple-element.16), channel_id=1, source_target_pairs={{0,3},{1,2},{2,1},{3,0},{4,7},{5,6},{6,5},{7,4},{8,11},{9,10},{10,... | collective-permute-start | bytes 983048 | tf_op jit(solution)/shard_map/ppermute | solution.py:289
  23.5 0.6 fusion.6
  27.7 0.7 convert_multiply_fusion.8
  28.4 0.0 copy-done.9
  28.4 0.7 fusion.5
  35.5 0.6 convert_multiply_fusion.3
  36.2 9.1 %add_multiply_fusion = (f32[2,112,512]{2,1,0:T(8,128)S(1)}, f32[2,112,512]{2,1,0:T(8,128)S(1)}, f32[2,112,512]{2,1,0:T(8,128)S(1)}, f32[2,112,512]{2,1,0:T(8,128)S(1)}) fusion(f32[]{:T(128)} %bitcast.8, f32[]{:T(128)} %bitcast.7, f32[112]{0:T(128)S(1)} %get-tuple-element.49, f32[2,512]{1,0:T(2,128)S(1)} %get-tuple-element.38, f32[]{:T(128)S(6)} %mul.423, ...), kind=kLoop, calls=%fused_computation.12 | loop fusion | flops 11583488 | bytes 1857764 | tf_op jit(solution)/shard_map/mul | solution.py:273
  45.3 7.2 %multiply_multiply_fusion = f32[2,112,512]{2,1,0:T(8,128)S(1)} fusion(f32[]{:T(128)} %bitcast.2, f32[112]{0:T(128)S(1)} %get-tuple-element.50, f32[2,512]{1,0:T(2,128)S(1)} %get-tuple-element.41, f32[]{:T(128)S(6)} %mul.423, f32[112]{0:T(128)S(1)} %get-tuple-element.49, f32[2,512]{1,0:T(2,128)S(1)} %get-tuple-element.38, f32[]{:T(128)S(6)} %mul.411, ...), kind=kLoop, calls=%fused_computation.11 | loop fusion | flops 10092544 | bytes 481496 | tf_op jit(solution)/shard_map/mul | solution.py:273
  52.6 0.1 slice_add_fusion.2
  52.7 0.1 slice_add_fusion
  52.8 0.0 copy-start.1
  52.8 0.0 copy-start.2
  52.8 0.0 copy-start.8
  53.0 0.0 collective-permute-done.got1
  53.0 0.0 collective-permute-done.1.got2
  53.0 0.0 collective-permute-done.2.got3
  53.0 1.0 %copy-done.1 = bf16[4,2,128,512]{3,2,1,0:T(8,128)(2,1)S(1)} copy-done((bf16[4,2,128,512]{3,2,1,0:T(8,128)(2,1)S(1)}, bf16[4,2,128,512]{3,2,1,0:T(8,128)(2,1)}, u32[]{:S(2)}) %copy-start.1) | copy-done | bytes 1048600
  54.0 0.3 copy-done.2
  54.3 0.0 copy-done.8
  54.3 0.0 copy-start.5
  54.3 0.0 copy-start.6
  54.3 4.4 %shard_map.110 = (f32[224,256]{1,0:T(8,128)S(1)}, f32[224,256]{1,0:T(8,128)S(1)}, f32[224,256]{1,0:T(8,128)S(1)}, f32[224,256]{1,0:T(8,128)S(1)}) custom-call(s32[1]{0:T(128)} %bitcast.place, f32[5,128,128]{2,1,0:T(8,128)S(1)} %get-tuple-element.13.got0, f32[5,128,128]{2,1,0:T(8,128)S(1)} %collective-permute-done.got1, ...), custom_call_target="tpu_custom_call" | custom-call | tf_op jit(solution)/shard_map/pallas_call | solution.py:308
  58.8 0.2 collective-permute-start.3
  59.0 0.0 collective-permute-start.4
  59.0 3.5 %collective-permute-start.5 = (f32[224,256]{1,0:T(8,128)S(1)}, f32[224,256]{1,0:T(8,128)S(1)}, u32[]{:S(2)}, u32[]{:S(2)}) collective-permute-start(f32[224,256]{1,0:T(8,128)S(1)} %get-tuple-element.20), channel_id=1, source_target_pairs={{0,3},{1,2},{2,1},{3,0},{4,7},{5,6},{6,5},{7,4},{8,11},{9,10},{10,... | collective-permute-start | bytes 688136 | tf_op jit(solution)/shard_map/ppermute | solution.py:289
  62.5 0.0 collective-permute-done.3.got1
  62.5 4.8 %collective-permute-done.4.got2 = f32[224,256]{1,0:T(8,128)S(1)} collective-permute-done((f32[224,256]{1,0:T(8,128)S(1)}, f32[224,256]{1,0:T(8,128)S(1)}, u32[]{:S(2)}, u32[]{:S(2)}) %collective-permute-start.4) | collective-permute-done | bytes 229408 | tf_op jit(solution)/shard_map/ppermute | solution.py:289
  67.3 5.5 %collective-permute-done.5.got3 = f32[224,256]{1,0:T(8,128)S(1)} collective-permute-done((f32[224,256]{1,0:T(8,128)S(1)}, f32[224,256]{1,0:T(8,128)S(1)}, u32[]{:S(2)}, u32[]{:S(2)}) %collective-permute-start.5) | collective-permute-done | bytes 229408 | tf_op jit(solution)/shard_map/ppermute | solution.py:289
  72.8 0.0 copy-done.5
  72.8 0.0 copy-done.6
  72.8 3.0 %shard_map.111 = f32[256,1024]{1,0:T(8,128)} custom-call(s32[1]{0:T(128)} %bitcast.place, f32[224,256]{1,0:T(8,128)S(1)} %get-tuple-element.17.got0, f32[224,256]{1,0:T(8,128)S(1)} %collective-permute-done.3.got1, f32[224,256]{1,0:T(8,128)S(1)} %collective-permute-done.4.got2, f32[224,256]{1,0:T(8,128)S(1)} %collective-permute-done.5.got3, ...), custom_call_target="tpu_custom_call" | custom-call | tf_op jit(solution)/shard_map/pallas_call | solution.py:316
  (8 shorter events, 0.2 us)
Async XLA Ops:
  0.0 28.4 %copy-start.9 = (f32[1,5]{1,0:T(1,128)S(1)}, f32[1,5]{1,0:T(1,128)}, u32[]{:S(2)}) copy-start(f32[1,5]{1,0:T(1,128)} %param.13) | copy-start | bytes 64
  11.7 1.1 %copy-start = (bf16[1,5,128,512]{3,2,1,0:T(8,128)(2,1)S(1)}, bf16[1,5,128,512]{3,2,1,0:T(8,128)(2,1)}, u32[]{:S(2)}) copy-start(bf16[1,5,128,512]{3,2,1,0:T(8,128)(2,1)} %frames.1) | copy-start | bytes 1966084
  12.7 1.0 %copy-start.3 = (bf16[4,128,512]{2,1,0:T(8,128)(2,1)S(1)}, bf16[4,128,512]{2,1,0:T(8,128)(2,1)}, u32[]{:S(2)}) copy-start(bf16[4,128,512]{2,1,0:T(8,128)(2,1)} %constant.57.clone.x_hi) | copy-start | bytes 1572868
  13.8 1.0 %copy-start.4 = (bf16[4,128,512]{2,1,0:T(8,128)(2,1)S(1)}, bf16[4,128,512]{2,1,0:T(8,128)(2,1)}, u32[]{:S(2)}) copy-start(bf16[4,128,512]{2,1,0:T(8,128)(2,1)} %constant.58.clone.x_lo) | copy-start | bytes 1572868
  14.8 0.7 copy-start.7
  18.3 34.7 %collective-permute-start = (f32[5,128,128]{2,1,0:T(8,128)S(1)}, f32[5,128,128]{2,1,0:T(8,128)S(1)}, u32[]{:S(2)}, u32[]{:S(2)}) collective-permute-start(f32[5,128,128]{2,1,0:T(8,128)S(1)} %get-tuple-element.14), channel_id=1, source_target_pairs={{0,1},{1,0},{2,3},{3,2},{4,5},{5,4},{6,7},{7,6},{8,9},{9,8},{10,11... | collective-permute-start | bytes 983048 | tf_op jit(solution)/shard_map/ppermute | solution.py:289
  20.3 32.7 %collective-permute-start.1 = (f32[5,128,128]{2,1,0:T(8,128)S(1)}, f32[5,128,128]{2,1,0:T(8,128)S(1)}, u32[]{:S(2)}, u32[]{:S(2)}) collective-permute-start(f32[5,128,128]{2,1,0:T(8,128)S(1)} %get-tuple-element.15), channel_id=1, source_target_pairs={{0,2},{1,3},{2,0},{3,1},{4,6},{5,7},{6,4},{7,5},{8,10},{9,11},{10,... | collective-permute-start | bytes 983048 | tf_op jit(solution)/shard_map/ppermute | solution.py:289
  20.3 32.7 %collective-permute-start.2 = (f32[5,128,128]{2,1,0:T(8,128)S(1)}, f32[5,128,128]{2,1,0:T(8,128)S(1)}, u32[]{:S(2)}, u32[]{:S(2)}) collective-permute-start(f32[5,128,128]{2,1,0:T(8,128)S(1)} %get-tuple-element.16), channel_id=1, source_target_pairs={{0,3},{1,2},{2,1},{3,0},{4,7},{5,6},{6,5},{7,4},{8,11},{9,10},{10,... | collective-permute-start | bytes 983048 | tf_op jit(solution)/shard_map/ppermute | solution.py:289
  52.8 1.2 %copy-start.1 = (bf16[4,2,128,512]{3,2,1,0:T(8,128)(2,1)S(1)}, bf16[4,2,128,512]{3,2,1,0:T(8,128)(2,1)}, u32[]{:S(2)}) copy-start(bf16[4,2,128,512]{3,2,1,0:T(8,128)(2,1)} %constant.59.clone.y_hi) | copy-start | bytes 3145732
  52.8 1.5 %copy-start.2 = (bf16[4,2,128,512]{3,2,1,0:T(8,128)(2,1)S(1)}, bf16[4,2,128,512]{3,2,1,0:T(8,128)(2,1)}, u32[]{:S(2)}) copy-start(bf16[4,2,128,512]{3,2,1,0:T(8,128)(2,1)} %constant.60.clone.y_lo) | copy-start | bytes 3145732
  52.8 1.5 %copy-start.8 = (f32[2,512]{1,0:T(2,128)S(1)}, f32[2,512]{1,0:T(2,128)}, u32[]{:S(2)}) copy-start(f32[2,512]{1,0:T(2,128)} %constant.61.clone.odd) | copy-start | bytes 12292
  54.3 18.4 %copy-start.5 = (f32[4,2,112,128]{3,2,1,0:T(8,128)S(1)}, f32[4,2,112,128]{3,2,1,0:T(8,128)}, u32[]{:S(2)}) copy-start(f32[4,2,112,128]{3,2,1,0:T(8,128)} %constant.62.clone.first) | copy-start | bytes 1376260
  54.3 18.4 %copy-start.6 = (f32[4,2,112,128]{3,2,1,0:T(8,128)S(1)}, f32[4,2,112,128]{3,2,1,0:T(8,128)}, u32[]{:S(2)}) copy-start(f32[4,2,112,128]{3,2,1,0:T(8,128)} %constant.63.clone.step) | copy-start | bytes 1376260
  58.8 3.7 %collective-permute-start.3 = (f32[224,256]{1,0:T(8,128)S(1)}, f32[224,256]{1,0:T(8,128)S(1)}, u32[]{:S(2)}, u32[]{:S(2)}) collective-permute-start(f32[224,256]{1,0:T(8,128)S(1)} %get-tuple-element.18), channel_id=1, source_target_pairs={{0,1},{1,0},{2,3},{3,2},{4,5},{5,4},{6,7},{7,6},{8,9},{9,8},{10,11... | collective-permute-start | bytes 688136 | tf_op jit(solution)/shard_map/ppermute | solution.py:289
  59.0 8.3 %collective-permute-start.4 = (f32[224,256]{1,0:T(8,128)S(1)}, f32[224,256]{1,0:T(8,128)S(1)}, u32[]{:S(2)}, u32[]{:S(2)}) collective-permute-start(f32[224,256]{1,0:T(8,128)S(1)} %get-tuple-element.19), channel_id=1, source_target_pairs={{0,2},{1,3},{2,0},{3,1},{4,6},{5,7},{6,4},{7,5},{8,10},{9,11},{10,... | collective-permute-start | bytes 688136 | tf_op jit(solution)/shard_map/ppermute | solution.py:289
  59.0 13.7 %collective-permute-start.5 = (f32[224,256]{1,0:T(8,128)S(1)}, f32[224,256]{1,0:T(8,128)S(1)}, u32[]{:S(2)}, u32[]{:S(2)}) collective-permute-start(f32[224,256]{1,0:T(8,128)S(1)} %get-tuple-element.20), channel_id=1, source_target_pairs={{0,3},{1,2},{2,1},{3,0},{4,7},{5,6},{6,5},{7,4},{8,11},{9,10},{10,... | collective-permute-start | bytes 688136 | tf_op jit(solution)/shard_map/ppermute | solution.py:289
where the time goes:
time: 76.2 us; the launch traced here: 75.7 us
  other arithmetic  19.3 us (25%)
  between operations  10.9 us (14%)
  Pallas kernels  10.2 us (13%)
  waiting for transfers between devices  10.2 us (13%)
  blocking collectives  9.69 us (13%)
  starting transfers between devices  8.92 us (12%)
  local copies, waits for them, and re-layouts  6.42 us (8%)
    mul x2, other arithmetic, order_weights(): weight = c * (g * own_den + h * other_den)  16.3 us
    ppermute x6, waiting for transfers between devices, from_partners(): lax.ppermute(blocks[k], 'row', [(i, i ^ k) for i in range(PARTS)])  10.2 us
    psum x1, blocking collectives, per_device(): totals = lax.psum(jnp.sum(frames.astype(jnp.float32), axis=(2, 3)), 'row')  9.69 us
    ppermute x6, starting transfers between devices, from_partners(): lax.ppermute(blocks[k], 'row', [(i, i ^ k) for i in range(PARTS)])  8.92 us
    unnamed x20, local copies, waits for them, and re-layouts  5.16 us
    pallas_call x1, Pallas kernels, per_device(): pl.pallas_call(middle_kernel, out_shape=[jax.ShapeDtypeStruct((2 * COLS,...  4.44 us
    pallas_call x1, Pallas kernels, per_device(): pl.pallas_call(final_kernel, out_shape=jax.ShapeDtypeStruct((2 * ROWS, GR...  2.95 us
    pallas_call x1, Pallas kernels, per_device(): pl.pallas_call(forward_kernel, out_shape=[jax.ShapeDtypeStruct((5, 128, R...  2.81 us
  transfers between devices with their start and end apart: 6, of which 2 were waited for; matrix products, arithmetic and copies ran while one was open for 25% of the time, Pallas kernels for 0%

commit v1 on v0

v1 whole, which is shorter than its diff:
```python
import functools
import math

import jax
import jax.numpy as jnp
import numpy as np
from jax import lax
from jax.experimental import pallas as pl
from jax.experimental.pallas import tpu as pltpu
from jax.sharding import PartitionSpec as P

wiener = 0.1
gain_out = 8.0
cut_share = 0.45
PIX = 512
GRID = 1024
PHASES = 5
PARTS = 4
ROWS = PIX // PARTS
CHUNKS = (0, 1)
LOW = (32, 0)
MAIN = 32
FOLD_LOW = (32, 16)
FOLD = (32, 16)
COLS = (64, 48)
EXT = (32, 40)
ORDERS = (0, 1, -1, 2, -2)
ARC = (
    1.5707963050,
    -0.2145988016,
    0.0889789874,
    -0.0501743046,
    0.0308918810,
    -0.0170881256,
    0.0066700901,
    -0.0012624911,
)


def split_np(array):
    hi = array.astype(jnp.bfloat16)
    lo = (array - hi.astype(np.float32)).astype(jnp.bfloat16)
    return hi, lo


def split(array):
    hi = array.astype(jnp.bfloat16)
    lo = (array - hi.astype(jnp.float32)).astype(jnp.bfloat16)
    return hi, lo


def column_freq_np(d, chunk):
    main = 4 * (np.arange(MAIN) + LOW[chunk]) + d
    fold = 4 * (np.arange(FOLD[chunk]) + FOLD_LOW[chunk]) + d - PIX
    if d == 0 and chunk == 1:
        fold[0] = -PIX // 2
    return np.concatenate([main, fold])


@functools.cache
def tables():
    index = np.arange(PIX)
    angle = 2.0 * np.pi * (np.outer(index, index) % PIX) / PIX
    cos_all = np.cos(angle).astype(np.float32)
    sin_all = np.sin(angle).astype(np.float32)
    sin_half = sin_all[: PIX // 2].copy()
    sin_half[0] = cos_all[PIX // 2]
    x_table = np.stack(
        [
            np.stack(
                [
                    np.concatenate(
                        [
                            cos_all[d : PIX // 2 : PARTS][LOW[c] : LOW[c] + MAIN],
                            sin_half[d::PARTS][LOW[c] : LOW[c] + MAIN],
                        ]
                    )
                    for d in range(PARTS)
                ]
            )
            for c in CHUNKS
        ]
    )
    y_table = np.stack(
        [
            np.stack([cos_all[s * ROWS : (s + 1) * ROWS], sin_all[s * ROWS : (s + 1) * ROWS]])
            for s in range(PARTS)
        ]
    )
    first = []
    for c in CHUNKS:
        block = np.zeros((PARTS, 2, COLS[c], 128), np.float32)
        for s in range(PARTS):
            freq = column_freq_np(s, c)
            scale = gain_out / (GRID * GRID) * np.where(freq == 0, 1.0, 2.0)
            turn = 2.0 * np.pi * ((freq[:, None] * np.arange(128)[None, :]) % GRID) / GRID
            block[s, 0] = scale[:, None] * np.cos(turn)
            block[s, 1] = scale[:, None] * np.sin(turn)
        first.append(block)
    turn = 2.0 * np.pi * index / GRID
    odd = np.stack([np.cos(turn), np.sin(turn)]).astype(np.float32)
    return split_np(x_table), split_np(y_table), first, odd


def dot3(left, right, dims):
    lhs = jnp.concatenate([left[0], left[0], left[1]], axis=dims[0])
    rhs = jnp.concatenate([right[0], right[1], right[0]], axis=dims[1])
    return lax.dot_general(
        lhs, rhs, (((dims[0],), (dims[1],)), ((), ())), preferred_element_type=jnp.float32
    )


def turn_pair(steps):
    angle = (2.0 * math.pi / PIX) * ((steps + 256) % 512 - 256).astype(jnp.float32)
    return jnp.cos(angle), jnp.sin(angle)


def sums_kernel(source, sums, frames, sems):
    copies = [
        pltpu.make_async_copy(source.at[0, p], frames.at[p], sems.at[p]) for p in range(PHASES)
    ]
    for copy in copies:
        copy.start()
    for p in range(PHASES):
        copies[p].wait()
        rows = jnp.sum(frames[p].astype(jnp.float32), axis=0, keepdims=True)
        lanes = rows[:, :128] + rows[:, 128:256] + rows[:, 256:384] + rows[:, 384:]
        sums[p : p + 1, :] = lanes
    sums[PHASES:, :] = jnp.zeros((8 - PHASES, 128), jnp.float32)


def phase_kernel(place, shift, offset, hi_any, lo_any, turns, phases, x_hi, x_lo, sems):
    copies = [
        pltpu.make_async_copy(hi_any, x_hi, sems.at[0]),
        pltpu.make_async_copy(lo_any, x_lo, sems.at[1]),
    ]
    for copy in copies:
        copy.start()
    rank = place[0]
    shift_y = shift[0, 0]
    shift_x = shift[0, 1]
    x_cos, x_sin = turn_pair(lax.broadcasted_iota(jnp.int32, (8, PIX), 1) * shift_x)
    row_at = lax.broadcasted_iota(jnp.int32, (ROWS, 128), 0) + rank * ROWS
    y_cos, y_sin = turn_pair(row_at * shift_y)
    x_cos, x_sin = x_cos[:1], x_sin[:1]
    y_cos = jnp.concatenate([y_cos] * 4, axis=1)
    y_sin = jnp.concatenate([y_sin] * 4, axis=1)
    turn_re = x_cos * y_cos - x_sin * y_sin
    turn_im = x_cos * y_sin + x_sin * y_cos
    turns[0] = turn_re
    turns[1] = turn_im
    turns[2] = turn_re * turn_re - turn_im * turn_im
    turns[3] = 2.0 * turn_re * turn_im
    phase_at = lax.broadcasted_iota(jnp.int32, (8, 128), 0).astype(jnp.float32)
    phase_at = (2.0 * math.pi / PHASES) * phase_at + offset[0]
    phases[0] = jnp.cos(phase_at)
    phases[1] = jnp.sin(phase_at)
    phases[2] = jnp.cos(2.0 * phase_at)
    phases[3] = jnp.sin(2.0 * phase_at)
    for copy in copies:
        copy.wait()


def spectra_rows(rank, chunk, band, x_hi, x_lo, outs):
    table = (
        jnp.concatenate([x_hi[chunk, rank ^ k] for k in range(PARTS)], axis=0),
        jnp.concatenate([x_lo[chunk, rank ^ k] for k in range(PARTS)], axis=0),
    )
    spectra = dot3(table, band, (1, 1))
    for k in range(PARTS):
        for plane in range(5):
            outs[k][plane] = spectra[
                k * 2 * MAIN : (k + 1) * 2 * MAIN, plane * ROWS : (plane + 1) * ROWS
            ]


def forward_kernel(place, sums0, sums1, sums2, sums3, turns, phases, frames, x_hi, x_lo, *rest):
    outs, (band_hi, band_lo) = rest[:PARTS], rest[PARTS:]
    rank = place[0]
    total = (sums0[...] + sums1[...]) + (sums2[...] + sums3[...])
    total = jnp.sum(total, axis=1, keepdims=True)
    weight_all = (PIX * PIX / PHASES) / total[:PHASES]
    acc = None
    for p in range(PHASES):
        weight = weight_all[p : p + 1]
        plane = frames[p].astype(jnp.float32)
        terms = [plane * weight] + [
            plane * (weight * phases[i, p : p + 1, 0:1]) for i in range(4)
        ]
        acc = terms if p == 0 else [a + b for a, b in zip(acc, terms)]
    zero, one_re, one_im, two_re, two_im = acc
    planes = [
        zero,
        one_re * turns[0] + one_im * turns[1],
        one_re * turns[1] - one_im * turns[0],
        two_re * turns[2] + two_im * turns[3],
        two_re * turns[3] - two_im * turns[2],
    ]
    for index, plane in enumerate(planes):
        hi, lo = split(plane)
        band_hi[index * ROWS : (index + 1) * ROWS, :] = hi
        band_lo[index * ROWS : (index + 1) * ROWS, :] = lo
    spectra_rows(rank, 0, (band_hi[...], band_lo[...]), x_hi, x_lo, outs)


def forward_rest_kernel(place, band_hi, band_lo, x_hi, x_lo, *rest):
    outs, token = rest[:PARTS], rest[PARTS]
    spectra_rows(place[0], 1, (band_hi[...], band_lo[...]), x_hi, x_lo, outs)
    token[...] = jnp.zeros((8, 128), jnp.float32)


def transfer_curve(squared):
    radius = jnp.minimum(jnp.sqrt(squared * (1.0 / (cut_share * PIX) ** 2)), 1.0)
    arc = jnp.full_like(radius, ARC[7])
    for coefficient in ARC[6::-1]:
        arc = arc * radius + coefficient
    return (2.0 / math.pi) * jnp.sqrt(1.0 - radius) * (arc - radius * jnp.sqrt(1.0 + radius))


def weights_kernel(place, gains, shift, token, first0, first1, hi_any, lo_any, *rest):
    weights, final_hi, final_lo = rest[0:2], rest[2:4], rest[4:6]
    y_hi_out, y_lo_out, sems = rest[6:]
    copies = [
        pltpu.make_async_copy(hi_any, y_hi_out, sems.at[0]),
        pltpu.make_async_copy(lo_any, y_lo_out, sems.at[1]),
    ]
    for copy in copies:
        copy.start()
    rank = place[0]
    shift_y, shift_x = shift[0, 0], shift[0, 1]
    own = [gains[0, m + 2] for m in ORDERS]
    other = [gains[0, 2 - m] for m in ORDERS]
    sub = lax.broadcasted_iota(jnp.int32, (8, 1), 0)
    lane = lax.broadcasted_iota(jnp.int32, (1, PIX), 1)

    def tile_step(chunk, tile):
        low = 8 * tile
        folded = low >= MAIN
        freq = 4 * jnp.where(folded, low - MAIN + FOLD_LOW[chunk], low + LOW[chunk]) + rank
        freq = jnp.where(folded, freq - PIX, freq)
        freq_x = freq + 4 * sub
        if chunk == 1:
            lone = jnp.logical_and(low == MAIN, rank == 0)
            freq_x = jnp.where(jnp.where(sub == 0, lone.astype(jnp.int32), 0) == 1, -PIX // 2, freq_x)
        halves = []
        for half in range(2):
            own_den = jnp.full((8, PIX), wiener, jnp.float32)
            other_den = jnp.full((8, PIX), wiener, jnp.float32)
            curves = []
            for m, g, h in zip(ORDERS, own, other):
                x = (freq_x - m * shift_x).astype(jnp.float32)
                y = (lane - (PIX * half + m * shift_y)).astype(jnp.float32)
                curve = transfer_curve(x * x + y * y)
                power = curve * curve
                own_den = own_den + (g * g) * power
                other_den = other_den + (h * h) * power
                curves.append(curve)
            own_den = 0.5 / own_den
            other_den = 0.5 / other_den
            halves.append([c * (g * own_den + h * other_den) for c, g, h in zip(curves, own, other)])
        rows = pl.ds(pl.multiple_of(low, 8), 8)
        for order in range(5):
            weights[chunk][order, 0, rows, :] = halves[0][order] + halves[1][order]
            weights[chunk][order, 1, rows, :] = halves[0][order] - halves[1][order]

    for chunk in CHUNKS:
        lax.fori_loop(
            0, COLS[chunk] // 8, lambda tile, _, chunk=chunk: (tile_step(chunk, tile), 0)[1], 0
        )
        first = (first0, first1)[chunk]
        rows = COLS[chunk]
        sign = 1.0 - 2.0 * (lax.broadcasted_iota(jnp.int32, (rows, 128), 0) % 2).astype(jnp.float32)
        for k in range(PARTS):
            source = rank ^ k
            step = jnp.full((8, 128), source, jnp.int32).astype(jnp.float32) * (math.pi / 4)
            step_re = sign * jnp.cos(step)[:1]
            step_im = sign * jnp.sin(step)[:1]
            re, im = first[source, 0], first[source, 1]
            for block in range(GRID // 128):
                lanes = slice(128 * block, 128 * (block + 1))
                for part, value in ((0, re), (1, -im)):
                    hi, lo = split(value)
                    at = slice((2 * k + part) * rows, (2 * k + part + 1) * rows)
                    final_hi[chunk][at, lanes] = hi
                    final_lo[chunk][at, lanes] = lo
                re, im = re * step_re - im * step_im, re * step_im + im * step_re
    for copy in copies:
        copy.wait()


def middle_kernel(chunk, place, got0, got1, got2, got3, weights, y_hi, y_lo, odd, *outs):
    rank = place[0]
    blocks = (got0, got1, got2, got3)
    rows, ext = COLS[chunk], EXT[chunk]
    if chunk == 1:
        first_row = lax.broadcasted_iota(jnp.int32, (MAIN, PIX), 0) == 0
        lone = jnp.logical_and(first_row, jnp.full((MAIN, PIX), rank, jnp.int32) == 0)
        top = lax.broadcasted_iota(jnp.int32, (8, PIX), 0) == 0

    def plane(index):
        whole = jnp.concatenate([b[index] for b in blocks], axis=1)
        cosines, sines = whole[:MAIN], whole[MAIN:]
        if chunk == 0:
            return cosines, sines, None
        return cosines, jnp.where(lone, 0.0, sines), jnp.where(top, sines[:8], 0.0)

    real_rows = []
    imag_rows = []

    def add_row(re, im, extra_re, extra_im):
        real_rows.append(re)
        imag_rows.append(im)
        if chunk == 1:
            real_rows.append(extra_re)
            imag_rows.append(extra_im() if callable(extra_im) else extra_im)

    cos_r, sin_r, extra_r = plane(0)
    add_row(cos_r, -sin_r, extra_r, lambda: jnp.zeros_like(extra_r))
    for m in range(2):
        cos_r, sin_r, extra_r = plane(1 + 2 * m)
        cos_i, sin_i, extra_i = plane(2 + 2 * m)
        add_row(cos_r + sin_i, cos_i - sin_r, extra_r, extra_i)
        add_row(cos_r - sin_i, -cos_i - sin_r, extra_r, lambda: -extra_i)
    data = split(jnp.concatenate(real_rows + imag_rows, axis=0))

    def y_matrix(ref):
        return jnp.concatenate(
            [jnp.concatenate([ref[rank ^ k, 0], ref[rank ^ k, 1]], axis=1) for k in range(PARTS)],
            axis=0,
        )

    turned = dot3(data, (y_matrix(y_hi), y_matrix(y_lo)), (1, 0))
    half = 5 * ext
    spec_re = turned[:half, :PIX] + turned[half:, PIX:]
    spec_im = turned[half:, :PIX] - turned[:half, PIX:]
    sums = None
    for order in range(5):

        def both(spec):
            main = spec[order * ext : order * ext + MAIN]
            if chunk == 0:
                return jnp.concatenate([main, main], axis=0)
            extra = spec[order * ext + MAIN : (order + 1) * ext]
            return jnp.concatenate([main, jnp.where(top, extra, main[16:24]), main[24:]], axis=0)

        re, im = both(spec_re), both(spec_im)
        plus, minus = weights[order, 0], weights[order, 1]
        terms = (plus * re, plus * im, minus * re, minus * im)
        sums = terms if order == 0 else tuple(a + b for a, b in zip(sums, terms))
    even_re, even_im, odd_re, odd_im = sums
    odd_cos, odd_sin = odd[0:1], odd[1:2]
    odd_re, odd_im = odd_re * odd_cos - odd_im * odd_sin, odd_re * odd_sin + odd_im * odd_cos
    filtered = split(jnp.concatenate([even_re, even_im, odd_re, odd_im], axis=0))

    def u_matrix(ref):
        return jnp.concatenate(
            [jnp.concatenate([ref[rank ^ k, 0], ref[rank ^ k, 1]], axis=0) for k in range(PARTS)],
            axis=0,
        )

    back = dot3(filtered, (u_matrix(y_hi), u_matrix(y_lo)), (1, 1))
    for k in range(PARTS):
        cos_part = back[:, 2 * ROWS * k : 2 * ROWS * k + ROWS]
        sin_part = back[:, 2 * ROWS * k + ROWS : 2 * ROWS * (k + 1)]
        for parity in range(2):
            base = 2 * rows * parity
            re, im = slice(base, base + rows), slice(base + rows, base + 2 * rows)
            lanes = slice(parity * ROWS, (parity + 1) * ROWS)
            outs[k][0:rows, lanes] = cos_part[re] - sin_part[im]
            outs[k][rows : 2 * rows, lanes] = sin_part[re] + cos_part[im]


def gathered(blocks):
    return split(jnp.concatenate([b[...] for b in blocks], axis=0))


def part_kernel(got0, got1, got2, got3, final_hi, final_lo, part):
    data = gathered((got0, got1, got2, got3))
    part[...] = dot3(data, (final_hi[...], final_lo[...]), (0, 0))


def final_kernel(got0, got1, got2, got3, final_hi, final_lo, part, out, woven, sems):
    data = gathered((got0, got1, got2, got3))
    copies = []
    for strip in range(GRID // 256):
        lanes = slice(256 * strip, 256 * (strip + 1))
        picture = part[:, lanes] + dot3(data, (final_hi[:, lanes], final_lo[:, lanes]), (0, 0))
        for block in range(2):
            at = 2 * strip + block
            piece = slice(128 * block, 128 * (block + 1))
            woven[at, pl.ds(0, ROWS, 2), :] = picture[:ROWS, piece]
            woven[at, pl.ds(1, ROWS, 2), :] = picture[ROWS:, piece]
            copy = pltpu.make_async_copy(
                woven.at[at], out.at[:, pl.ds(128 * at, 128)], sems.at[at]
            )
            copy.start()
            copies.append(copy)
    for copy in copies:
        copy.wait()


def smem():
    return pl.BlockSpec(memory_space=pltpu.SMEM)


def vmem():
    return pl.BlockSpec(memory_space=pltpu.VMEM)


def hbm():
    return pl.BlockSpec(memory_space=pltpu.HBM)


def f32(*shape):
    return jax.ShapeDtypeStruct(shape, jnp.float32)


def bf16(*shape):
    return jax.ShapeDtypeStruct(shape, jnp.bfloat16)


def call(kernel, out_shape, in_specs, out_specs=None, scratch=(), limit=24):
    if out_specs is None:
        out_specs = jax.tree.map(lambda _: vmem(), out_shape)
    return pl.pallas_call(
        kernel,
        out_shape=out_shape,
        in_specs=in_specs,
        out_specs=out_specs,
        scratch_shapes=list(scratch),
        compiler_params=pltpu.CompilerParams(vmem_limit_bytes=limit * 1024 * 1024),
    )


def from_partners(blocks):
    got = [blocks[0]]
    for k in range(1, PARTS):
        got.append(lax.ppermute(blocks[k], "row", [(i, i ^ k) for i in range(PARTS)]))
    return got


def per_device(frames, phase_offset, order_gain, band_shift):
    (x_hi, x_lo), (y_hi, y_lo), first, odd = tables()
    rank = lax.axis_index("row")
    place = rank.reshape(1).astype(jnp.int32)
    two = pltpu.SemaphoreType.DMA((2,))

    sums, frames = call(
        sums_kernel,
        [f32(8, 128), bf16(PHASES, ROWS, PIX)],
        [hbm()],
        scratch=[pltpu.SemaphoreType.DMA((PHASES,))],
    )(frames)
    sums = from_partners([sums] * PARTS)
    turns, phases, x_hi, x_lo = call(
        phase_kernel,
        [f32(4, ROWS, PIX), f32(4, 8, 128)] + [bf16(*x_hi.shape)] * 2,
        [smem()] * 3 + [hbm()] * 2,
        scratch=[two],
    )(place, band_shift, phase_offset, x_hi, x_lo)
    block = f32(5, 2 * MAIN, ROWS)
    *sent, band_hi, band_lo = call(
        forward_kernel,
        [block] * PARTS + [bf16(5 * ROWS, PIX)] * 2,
        [smem()] + [vmem()] * 9,
    )(place, *sums, turns, phases, frames, x_hi, x_lo)
    spectra = [from_partners(sent)]
    *sent, token = call(
        forward_rest_kernel, [block] * PARTS + [f32(8, 128)], [smem()] + [vmem()] * 4
    )(place, band_hi, band_lo, x_hi, x_lo)
    spectra.append(from_partners(sent))
    made = call(
        weights_kernel,
        [f32(5, 2, COLS[c], PIX) for c in CHUNKS]
        + [bf16(8 * COLS[c], GRID) for c in CHUNKS] * 2
        + [bf16(*y_hi.shape)] * 2,
        [smem()] * 3 + [vmem()] * 3 + [hbm()] * 2,
        scratch=[two],
    )(place, order_gain, band_shift, token, *first, y_hi, y_lo)
    weights, final_hi, final_lo, (y_hi, y_lo) = made[:2], made[2:4], made[4:6], made[6:]
    got = []
    for c in CHUNKS:
        sent = call(
            functools.partial(middle_kernel, c),
            [f32(2 * COLS[c], 2 * ROWS)] * PARTS,
            [smem()] + [vmem()] * 8,
        )(place, *spectra[c], weights[c], y_hi, y_lo, odd)
        got.append(from_partners(sent))
    part = call(part_kernel, f32(2 * ROWS, GRID), [vmem()] * 6)(*got[0], final_hi[0], final_lo[0])
    return call(
        final_kernel,
        f32(2 * ROWS, GRID),
        [vmem()] * 7,
        hbm(),
        [
            pltpu.VMEM((GRID // 128, 2 * ROWS, 128), jnp.float32),
            pltpu.SemaphoreType.DMA((GRID // 128,)),
        ],
    )(*got[1], final_hi[1], final_lo[1], part)


def solution(mesh):
    in_specs = (P("fov", None, "row", None), P("fov"), P("fov", None), P("fov", None))
    out_specs = P(("fov", "row"), None)
    return jax.shard_map(
        per_device, mesh=mesh, in_specs=in_specs, out_specs=out_specs, check_vma=False
    )
```

time: 76.2 us -> 48.8 us (0.64)
  other arithmetic: 19.3 us -> 0 us
  starting transfers between devices: 8.92 us -> 21.4 us
  between operations: 10.9 us -> 1.03 us
  blocking collectives: 9.69 us -> 0 us
  Pallas kernels: 10.2 us -> 18.7 us
  waiting for transfers between devices: 10.2 us -> 3.59 us
  local copies, waits for them, and re-layouts: 6.42 us -> 3.86 us
    mul x6 -> x0, other arithmetic: 17.6 us -> none  [the longest x2 16.3 us: order_weights(): weight = c * (g * own_den + h * other_den)]
    ppermute x6 -> x15, starting transfers between devices: 8.92 us -> 21.4 us  [from_partners(): lax.ppermute(blocks[k], 'row', [(i, i ^ k) for i in range(PARTS)])]
    psum x1 -> x0, blocking collectives: 9.69 us -> none  [per_device(): totals = lax.psum(jnp.sum(frames.astype(jnp.float32), axis=(2, 3)), 'row')]
    pallas_call x3 -> x9, Pallas kernels: 10.2 us -> 18.7 us  [the longest x1 6.67 us: per_device(): call(weights_kernel, [f32(5, 2, COLS[c], PIX) for c in CHUNKS] + [bf16(8...]
    ppermute x6 -> x15, waiting for transfers between devices: 10.2 us -> 3.59 us  [from_partners(): lax.ppermute(blocks[k], 'row', [(i, i ^ k) for i in range(PARTS)])]
    reduce_sum x1 -> x0, other arithmetic: 1.31 us -> none  [per_device(): totals = lax.psum(jnp.sum(frames.astype(jnp.float32), axis=(2, 3)), 'row')]
    unnamed x20, local copies, waits for them, and re-layouts: 5.16 us -> 3.86 us
    slice x2 -> x0, local copies, waits for them, and re-layouts: 1.26 us -> none  [the longest x1 0.68 us: order_weights(): own = [gains[2], gains[3], gains[1], gains[4], gains[0]]]
  transfers between devices with their start and end apart: 6 -> 15, of which waited for: 2 -> 2; matrix products, arithmetic and copies ran while one was open for 25% -> 0% of each run, Pallas kernels for 0% -> 30%
where the time goes in v1:
time: 48.8 us; the launch traced here: 48.6 us
  starting transfers between devices  21.4 us (44%)
  Pallas kernels  18.7 us (38%)
  local copies, waits for them, and re-layouts  3.86 us (8%)
  waiting for transfers between devices  3.59 us (7%)
  between operations  1.03 us (2%)
    ppermute x15, starting transfers between devices, from_partners(): lax.ppermute(blocks[k], 'row', [(i, i ^ k) for i in range(PARTS)])  21.4 us
    pallas_call x1, Pallas kernels, per_device(): call(weights_kernel, [f32(5, 2, COLS[c], PIX) for c in CHUNKS] + [bf16(8...  6.67 us
    pallas_call x2, Pallas kernels, per_device(): call(functools.partial(middle_kernel, c), [f32(2 * COLS[c], 2 * ROWS)] *...  4.92 us
    unnamed x20, local copies, waits for them, and re-layouts  3.86 us
    ppermute x15, waiting for transfers between devices, from_partners(): lax.ppermute(blocks[k], 'row', [(i, i ^ k) for i in range(PARTS)])  3.59 us
    pallas_call x1, Pallas kernels, per_device(): call(final_kernel, f32(2 * ROWS, GRID), [vmem()] * 7, hbm(), [pltpu.VMEM(...  1.8 us
    pallas_call x1, Pallas kernels, per_device(): call(forward_kernel, [block] * PARTS + [bf16(5 * ROWS, PIX)] * 2, [smem()...  1.38 us
    pallas_call x1, Pallas kernels, per_device(): call(phase_kernel, [f32(4, ROWS, PIX), f32(4, 8, 128)] + [bf16(*x_hi.shap...  1.13 us
  transfers between devices with their start and end apart: 15, of which 2 were waited for; matrix products, arithmetic and copies ran while one was open for 0% of the time, Pallas kernels for 30%

profile of v1, /device:TPU:1, one launch (start us, length us, event | category | flops | bytes accessed | tf_op | source)
XLA Modules:
  0.0 48.6 jit_solution(14138055818490539477)
XLA Ops:
  0.0 1.1 %copy-done.2 = bf16[1,5,128,512]{3,2,1,0:T(8,128)(2,1)S(1)} copy-done((bf16[1,5,128,512]{3,2,1,0:T(8,128)(2,1)S(1)}, bf16[1,5,128,512]{3,2,1,0:T(8,128)(2,1)}, u32[]{:S(2)}) %copy-start.2) | copy-done | bytes 655384
  1.1 1.0 %shard_map.109 = (f32[8,128]{1,0:T(8,128)S(1)}, bf16[5,128,512]{2,1,0:T(8,128)(2,1)S(1)}) custom-call(bf16[1,5,128,512]{3,2,1,0:T(8,128)(2,1)S(1)} %copy-done.2), custom_call_target="tpu_custom_call" | custom-call | tf_op jit(solution)/shard_map/pallas_call | solution.py:448
  2.1 3.3 %collective-permute-start = (f32[8,128]{1,0:T(8,128)S(1)}, f32[8,128]{1,0:T(8,128)S(1)}, u32[]{:S(2)}, u32[]{:S(2)}) collective-permute-start(f32[8,128]{1,0:T(8,128)S(1)} %get-tuple-element.38.sums0), channel_id=1, source_target_pairs={{0,1},{1,0},{2,3},{3,2},{4,5},{5,4},{6,7},{7,6},{8,9},{9,8},{10,11... | collective-permute-start | bytes 12296 | tf_op jit(solution)/shard_map/ppermute | solution.py:438
  5.4 1.2 %collective-permute-start.1 = (f32[8,128]{1,0:T(8,128)S(1)}, f32[8,128]{1,0:T(8,128)S(1)}, u32[]{:S(2)}, u32[]{:S(2)}) collective-permute-start(f32[8,128]{1,0:T(8,128)S(1)} %get-tuple-element.38.sums0), channel_id=1, source_target_pairs={{0,2},{1,3},{2,0},{3,1},{4,6},{5,7},{6,4},{7,5},{8,10},{9,11},{10,... | collective-permute-start | bytes 12296 | tf_op jit(solution)/shard_map/ppermute | solution.py:438
  6.6 2.0 %collective-permute-start.2 = (f32[8,128]{1,0:T(8,128)S(1)}, f32[8,128]{1,0:T(8,128)S(1)}, u32[]{:S(2)}, u32[]{:S(2)}) collective-permute-start(f32[8,128]{1,0:T(8,128)S(1)} %get-tuple-element.38.sums0), channel_id=1, source_target_pairs={{0,3},{1,2},{2,1},{3,0},{4,7},{5,6},{6,5},{7,4},{8,11},{9,10},{10,... | collective-permute-start | bytes 12296 | tf_op jit(solution)/shard_map/ppermute | solution.py:438
  9.3 0.0 copy-start.3
  9.3 1.0 %copy-done.3 = bf16[2,4,64,512]{3,2,1,0:T(8,128)(2,1)S(1)} copy-done((bf16[2,4,64,512]{3,2,1,0:T(8,128)(2,1)S(1)}, bf16[2,4,64,512]{3,2,1,0:T(8,128)(2,1)}, u32[]{:S(2)}) %copy-start.3) | copy-done | bytes 524312
  10.3 1.0 %copy-done.4 = bf16[2,4,64,512]{3,2,1,0:T(8,128)(2,1)S(1)} copy-done((bf16[2,4,64,512]{3,2,1,0:T(8,128)(2,1)S(1)}, bf16[2,4,64,512]{3,2,1,0:T(8,128)(2,1)}, u32[]{:S(2)}) %copy-start.4) | copy-done | bytes 524312
  11.4 0.7 %copy-done.8 = s32[1,2]{1,0:T(1,128)S(1)} copy-done((s32[1,2]{1,0:T(1,128)S(1)}, s32[1,2]{1,0:T(1,128)}, u32[]{:S(2)}) %copy-start.8) | copy-done | bytes 32
  12.0 1.1 %shard_map.110 = (f32[4,128,512]{2,1,0:T(8,128)S(1)}, f32[4,8,128]{2,1,0:T(8,128)S(1)}, bf16[2,4,64,512]{3,2,1,0:T(8,128)(2,1)S(1)}, bf16[2,4,64,512]{3,2,1,0:T(8,128)(2,1)S(1)}) custom-call(s32[1]{0:T(128)} %bitcast.place, s32[1,2]{1,0:T(1,128)S(1)} %copy-done.8, f32[1]{0:T(128)S(6)} %copy.12.offset, bf16[2,4,64,512]{3,2,1,0:T(8,128)(2,1)S(1)} %copy-done.3, ...), custom_call_target="tpu_custom_call" | custom-call | tf_op jit(solution)/shard_map/pallas_call | solution.py:455
  13.2 0.0 collective-permute-done.sums1
  13.2 0.0 collective-permute-done.1.sums2
  13.2 0.0 collective-permute-done.2.sums3
  13.2 0.0 copy-start.6
  13.2 1.4 %shard_map.111 = (f32[5,64,128]{2,1,0:T(8,128)S(1)}, f32[5,64,128]{2,1,0:T(8,128)S(1)}, f32[5,64,128]{2,1,0:T(8,128)S(1)}, f32[5,64,128]{2,1,0:T(8,128)S(1)}, bf...) custom-call(s32[1]{0:T(128)} %bitcast.place, f32[8,128]{1,0:T(8,128)S(1)} %get-tuple-element.38.sums0, ...), custom_call_target="tpu_custom_call" | custom-call | tf_op jit(solution)/shard_map/pallas_call | solution.py:462
  14.6 0.0 copy-start
  14.6 0.0 copy-start.1
  14.6 0.0 copy-start.5
  14.6 0.0 copy-start.9
  14.6 0.2 collective-permute-start.9
  14.8 1.2 %collective-permute-start.10 = (f32[5,64,128]{2,1,0:T(8,128)S(1)}, f32[5,64,128]{2,1,0:T(8,128)S(1)}, u32[]{:S(2)}, u32[]{:S(2)}) collective-permute-start(f32[5,64,128]{2,1,0:T(8,128)S(1)} %get-tuple-element.62), channel_id=1, source_target_pairs={{0,2},{1,3},{2,0},{3,1},{4,6},{5,7},{6,4},{7,5},{8,10},{9,11},{10,... | collective-permute-start | bytes 491528 | tf_op jit(solution)/shard_map/ppermute | solution.py:438
  16.0 2.3 %collective-permute-start.11 = (f32[5,64,128]{2,1,0:T(8,128)S(1)}, f32[5,64,128]{2,1,0:T(8,128)S(1)}, u32[]{:S(2)}, u32[]{:S(2)}) collective-permute-start(f32[5,64,128]{2,1,0:T(8,128)S(1)} %get-tuple-element.63), channel_id=1, source_target_pairs={{0,3},{1,2},{2,1},{3,0},{4,7},{5,6},{6,5},{7,4},{8,11},{9,10},{10,... | collective-permute-start | bytes 491528 | tf_op jit(solution)/shard_map/ppermute | solution.py:438
  18.4 0.8 %shard_map.112 = (f32[5,64,128]{2,1,0:T(8,128)S(1)}, f32[5,64,128]{2,1,0:T(8,128)S(1)}, f32[5,64,128]{2,1,0:T(8,128)S(1)}, f32[5,64,128]{2,1,0:T(8,128)S(1)}, f32[8,128]{1,0:T(8,128)S(1)}) custom-call(s32[1]{0:T(128)} %bitcast.place, bf16[640,512]{1,0:T(8,128)(2,1)S(1)} %get-tuple-element.44.band_hi, bf16[640,512]{1,0:T(8,128)(2,1)S(1)} %get-tuple-element.45.band_lo, ...), custom_call_target="tpu_custom_call" | custom-call | tf_op jit(solution)/shard_map/pallas_call | solution.py:468
  19.2 0.0 copy-start.7
  19.2 0.1 collective-permute-start.3
  19.3 1.3 %collective-permute-start.4 = (f32[5,64,128]{2,1,0:T(8,128)S(1)}, f32[5,64,128]{2,1,0:T(8,128)S(1)}, u32[]{:S(2)}, u32[]{:S(2)}) collective-permute-start(f32[5,64,128]{2,1,0:T(8,128)S(1)} %get-tuple-element.48), channel_id=1, source_target_pairs={{0,2},{1,3},{2,0},{3,1},{4,6},{5,7},{6,4},{7,5},{8,10},{9,11},{10,... | collective-permute-start | bytes 491528 | tf_op jit(solution)/shard_map/ppermute | solution.py:438
  20.6 0.0 collective-permute-done.9.got1
  20.6 2.3 %collective-permute-start.5 = (f32[5,64,128]{2,1,0:T(8,128)S(1)}, f32[5,64,128]{2,1,0:T(8,128)S(1)}, u32[]{:S(2)}, u32[]{:S(2)}) collective-permute-start(f32[5,64,128]{2,1,0:T(8,128)S(1)} %get-tuple-element.49), channel_id=1, source_target_pairs={{0,3},{1,2},{2,1},{3,0},{4,7},{5,6},{6,5},{7,4},{8,11},{9,10},{10,... | collective-permute-start | bytes 491528 | tf_op jit(solution)/shard_map/ppermute | solution.py:438
  22.9 6.7 %shard_map.113 = (f32[5,2,64,512]{3,2,1,0:T(8,128)S(1)}, f32[5,2,48,512]{3,2,1,0:T(8,128)S(1)}, bf16[512,1024]{1,0:T(8,128)(2,1)S(1)}, bf16[384,1024]{1,0:T(8,12...) custom-call(s32[1]{0:T(128)} %bitcast.place, ...), custom_call_target="tpu_custom_call" | custom-call | tf_op jit(solution)/shard_map/pallas_call | solution.py:472
  29.6 0.0 collective-permute-done.10.got2
  29.6 0.0 collective-permute-done.11.got3
  29.6 2.3 %shard_map.115 = (f32[128,256]{1,0:T(8,128)S(1)}, f32[128,256]{1,0:T(8,128)S(1)}, f32[128,256]{1,0:T(8,128)S(1)}, f32[128,256]{1,0:T(8,128)S(1)}) custom-call(s32[1]{0:T(128)} %bitcast.place, f32[5,64,128]{2,1,0:T(8,128)S(1)} %get-tuple-element.60.got0, f32[5,64,128]{2,1,0:T(8,128)S(1)} %collective-permute-done.9.got1, ...), custom_call_target="tpu_custom_call" | custom-call | tf_op jit(solution)/shard_map/pallas_call | solution.py:483
  32.0 0.1 collective-permute-start.12
  32.1 1.5 %collective-permute-start.13 = (f32[128,256]{1,0:T(8,128)S(1)}, f32[128,256]{1,0:T(8,128)S(1)}, u32[]{:S(2)}, u32[]{:S(2)}) collective-permute-start(f32[128,256]{1,0:T(8,128)S(1)} %get-tuple-element.67), channel_id=1, source_target_pairs={{0,2},{1,3},{2,0},{3,1},{4,6},{5,7},{6,4},{7,5},{8,10},{9,11},{10,... | collective-permute-start | bytes 393224 | tf_op jit(solution)/shard_map/ppermute | solution.py:438
  33.5 0.0 collective-permute-done.3.got1
  33.5 2.2 %collective-permute-start.14 = (f32[128,256]{1,0:T(8,128)S(1)}, f32[128,256]{1,0:T(8,128)S(1)}, u32[]{:S(2)}, u32[]{:S(2)}) collective-permute-start(f32[128,256]{1,0:T(8,128)S(1)} %get-tuple-element.68), channel_id=1, source_target_pairs={{0,3},{1,2},{2,1},{3,0},{4,7},{5,6},{6,5},{7,4},{8,11},{9,10},{10,... | collective-permute-start | bytes 393224 | tf_op jit(solution)/shard_map/ppermute | solution.py:438
  35.7 0.0 collective-permute-done.4.got2
  35.7 2.6 %shard_map.114 = (f32[96,256]{1,0:T(8,128)S(1)}, f32[96,256]{1,0:T(8,128)S(1)}, f32[96,256]{1,0:T(8,128)S(1)}, f32[96,256]{1,0:T(8,128)S(1)}) custom-call(s32[1]{0:T(128)} %bitcast.place, f32[5,64,128]{2,1,0:T(8,128)S(1)} %get-tuple-element.46.got0, f32[5,64,128]{2,1,0:T(8,128)S(1)} %collective-permute-done.3.got1, ...), custom_call_target="tpu_custom_call" | custom-call | tf_op jit(solution)/shard_map/pallas_call | solution.py:483
  38.3 0.1 collective-permute-start.6
  38.4 1.3 %collective-permute-start.7 = (f32[96,256]{1,0:T(8,128)S(1)}, f32[96,256]{1,0:T(8,128)S(1)}, u32[]{:S(2)}, u32[]{:S(2)}) collective-permute-start(f32[96,256]{1,0:T(8,128)S(1)} %get-tuple-element.56), channel_id=1, source_target_pairs={{0,2},{1,3},{2,0},{3,1},{4,6},{5,7},{6,4},{7,5},{8,10},{9,11},{10,... | collective-permute-start | bytes 294920 | tf_op jit(solution)/shard_map/ppermute | solution.py:438
  39.7 0.0 collective-permute-done.12.got1
  39.7 2.3 %collective-permute-start.8 = (f32[96,256]{1,0:T(8,128)S(1)}, f32[96,256]{1,0:T(8,128)S(1)}, u32[]{:S(2)}, u32[]{:S(2)}) collective-permute-start(f32[96,256]{1,0:T(8,128)S(1)} %get-tuple-element.57), channel_id=1, source_target_pairs={{0,3},{1,2},{2,1},{3,0},{4,7},{5,6},{6,5},{7,4},{8,11},{9,10},{10,... | collective-permute-start | bytes 294920 | tf_op jit(solution)/shard_map/ppermute | solution.py:438
  42.1 0.0 collective-permute-done.13.got2
  42.1 1.0 %shard_map.116.part = f32[256,1024]{1,0:T(8,128)S(1)} custom-call(f32[128,256]{1,0:T(8,128)S(1)} %get-tuple-element.65.got0, f32[128,256]{1,0:T(8,128)S(1)} %collective-permute-done.12.got1, f32[128,256]{1,0:T(8,128)S(1)} %collective-permute-done.13.got2, f32[128,256]{1,0:T(8,128)S(1)} %collective-permute-done.14.got3, ...), custom_call_target="tpu_custom_call" | custom-call | tf_op jit(solution)/shard_map/pallas_call | solution.py:489
  43.1 0.0 collective-permute-done.6.got1
  43.1 0.9 %collective-permute-done.7.got2 = f32[96,256]{1,0:T(8,128)S(1)} collective-permute-done((f32[96,256]{1,0:T(8,128)S(1)}, f32[96,256]{1,0:T(8,128)S(1)}, u32[]{:S(2)}, u32[]{:S(2)}) %collective-permute-start.7) | collective-permute-done | bytes 98336 | tf_op jit(solution)/shard_map/ppermute | solution.py:438
  44.0 2.7 %collective-permute-done.8.got3 = f32[96,256]{1,0:T(8,128)S(1)} collective-permute-done((f32[96,256]{1,0:T(8,128)S(1)}, f32[96,256]{1,0:T(8,128)S(1)}, u32[]{:S(2)}, u32[]{:S(2)}) %collective-permute-start.8) | collective-permute-done | bytes 98336 | tf_op jit(solution)/shard_map/ppermute | solution.py:438
  46.6 1.8 %shard_map.117 = f32[256,1024]{1,0:T(8,128)} custom-call(f32[96,256]{1,0:T(8,128)S(1)} %get-tuple-element.54.got0, f32[96,256]{1,0:T(8,128)S(1)} %collective-permute-done.6.got1, f32[96,256]{1,0:T(8,128)S(1)} %collective-permute-done.7.got2, f32[96,256]{1,0:T(8,128)S(1)} %collective-permute-done.8.got3, bf16[384,1024]{1,0:T(8,128)(2,1)S(1)} %get-tuple-element.58.final_hi, ...), custom_call_target="tpu_custom_call" | custom-call | tf_op jit(solution)/shard_map/pallas_call | solution.py:490
  (11 shorter events, 0.0 us)
Async XLA Ops:
  0.0 1.1 %copy-start.2 = (bf16[1,5,128,512]{3,2,1,0:T(8,128)(2,1)S(1)}, bf16[1,5,128,512]{3,2,1,0:T(8,128)(2,1)}, u32[]{:S(2)}) copy-start(bf16[1,5,128,512]{3,2,1,0:T(8,128)(2,1)} %source.1) | copy-start | bytes 1966084
  2.1 11.1 %collective-permute-start = (f32[8,128]{1,0:T(8,128)S(1)}, f32[8,128]{1,0:T(8,128)S(1)}, u32[]{:S(2)}, u32[]{:S(2)}) collective-permute-start(f32[8,128]{1,0:T(8,128)S(1)} %get-tuple-element.38.sums0), channel_id=1, source_target_pairs={{0,1},{1,0},{2,3},{3,2},{4,5},{5,4},{6,7},{7,6},{8,9},{9,8},{10,11... | collective-permute-start | bytes 12296 | tf_op jit(solution)/shard_map/ppermute | solution.py:438
  5.4 7.8 %collective-permute-start.1 = (f32[8,128]{1,0:T(8,128)S(1)}, f32[8,128]{1,0:T(8,128)S(1)}, u32[]{:S(2)}, u32[]{:S(2)}) collective-permute-start(f32[8,128]{1,0:T(8,128)S(1)} %get-tuple-element.38.sums0), channel_id=1, source_target_pairs={{0,2},{1,3},{2,0},{3,1},{4,6},{5,7},{6,4},{7,5},{8,10},{9,11},{10,... | collective-permute-start | bytes 12296 | tf_op jit(solution)/shard_map/ppermute | solution.py:438
  6.6 6.6 %collective-permute-start.2 = (f32[8,128]{1,0:T(8,128)S(1)}, f32[8,128]{1,0:T(8,128)S(1)}, u32[]{:S(2)}, u32[]{:S(2)}) collective-permute-start(f32[8,128]{1,0:T(8,128)S(1)} %get-tuple-element.38.sums0), channel_id=1, source_target_pairs={{0,3},{1,2},{2,1},{3,0},{4,7},{5,6},{6,5},{7,4},{8,11},{9,10},{10,... | collective-permute-start | bytes 12296 | tf_op jit(solution)/shard_map/ppermute | solution.py:438
  9.3 1.0 %copy-start.3 = (bf16[2,4,64,512]{3,2,1,0:T(8,128)(2,1)S(1)}, bf16[2,4,64,512]{3,2,1,0:T(8,128)(2,1)}, u32[]{:S(2)}) copy-start(bf16[2,4,64,512]{3,2,1,0:T(8,128)(2,1)} %constant.18.clone.hi_any) | copy-start | bytes 1572868
  10.3 1.0 %copy-start.4 = (bf16[2,4,64,512]{3,2,1,0:T(8,128)(2,1)S(1)}, bf16[2,4,64,512]{3,2,1,0:T(8,128)(2,1)}, u32[]{:S(2)}) copy-start(bf16[2,4,64,512]{3,2,1,0:T(8,128)(2,1)} %constant.19.clone.lo_any) | copy-start | bytes 1572868
  11.4 0.7 %copy-start.8 = (s32[1,2]{1,0:T(1,128)S(1)}, s32[1,2]{1,0:T(1,128)}, u32[]{:S(2)}) copy-start(s32[1,2]{1,0:T(1,128)} %shift.3) | copy-start | bytes 28
  13.2 9.7 %copy-start.6 = (f32[4,2,48,128]{3,2,1,0:T(8,128)S(1)}, f32[4,2,48,128]{3,2,1,0:T(8,128)}, u32[]{:S(2)}) copy-start(f32[4,2,48,128]{3,2,1,0:T(8,128)} %constant.21.clone.first1) | copy-start | bytes 589828
  14.6 8.3 %copy-start = (bf16[4,2,128,512]{3,2,1,0:T(8,128)(2,1)S(1)}, bf16[4,2,128,512]{3,2,1,0:T(8,128)(2,1)}, u32[]{:S(2)}) copy-start(bf16[4,2,128,512]{3,2,1,0:T(8,128)(2,1)} %constant.22.clone.hi_any) | copy-start | bytes 3145732
  14.6 8.3 %copy-start.1 = (bf16[4,2,128,512]{3,2,1,0:T(8,128)(2,1)S(1)}, bf16[4,2,128,512]{3,2,1,0:T(8,128)(2,1)}, u32[]{:S(2)}) copy-start(bf16[4,2,128,512]{3,2,1,0:T(8,128)(2,1)} %constant.23.clone.lo_any) | copy-start | bytes 3145732
  14.6 8.3 %copy-start.5 = (f32[4,2,64,128]{3,2,1,0:T(8,128)S(1)}, f32[4,2,64,128]{3,2,1,0:T(8,128)}, u32[]{:S(2)}) copy-start(f32[4,2,64,128]{3,2,1,0:T(8,128)} %constant.20.clone.first0) | copy-start | bytes 786436
  14.6 8.3 %copy-start.9 = (f32[1,5]{1,0:T(1,128)S(1)}, f32[1,5]{1,0:T(1,128)}, u32[]{:S(2)}) copy-start(f32[1,5]{1,0:T(1,128)} %gains.1) | copy-start | bytes 64
  14.6 6.0 %collective-permute-start.9 = (f32[5,64,128]{2,1,0:T(8,128)S(1)}, f32[5,64,128]{2,1,0:T(8,128)S(1)}, u32[]{:S(2)}, u32[]{:S(2)}) collective-permute-start(f32[5,64,128]{2,1,0:T(8,128)S(1)} %get-tuple-element.61), channel_id=1, source_target_pairs={{0,1},{1,0},{2,3},{3,2},{4,5},{5,4},{6,7},{7,6},{8,9},{9,8},{10,11... | collective-permute-start | bytes 491528 | tf_op jit(solution)/shard_map/ppermute | solution.py:438
  14.8 14.8 %collective-permute-start.10 = (f32[5,64,128]{2,1,0:T(8,128)S(1)}, f32[5,64,128]{2,1,0:T(8,128)S(1)}, u32[]{:S(2)}, u32[]{:S(2)}) collective-permute-start(f32[5,64,128]{2,1,0:T(8,128)S(1)} %get-tuple-element.62), channel_id=1, source_target_pairs={{0,2},{1,3},{2,0},{3,1},{4,6},{5,7},{6,4},{7,5},{8,10},{9,11},{10,... | collective-permute-start | bytes 491528 | tf_op jit(solution)/shard_map/ppermute | solution.py:438
  16.0 13.6 %collective-permute-start.11 = (f32[5,64,128]{2,1,0:T(8,128)S(1)}, f32[5,64,128]{2,1,0:T(8,128)S(1)}, u32[]{:S(2)}, u32[]{:S(2)}) collective-permute-start(f32[5,64,128]{2,1,0:T(8,128)S(1)} %get-tuple-element.63), channel_id=1, source_target_pairs={{0,3},{1,2},{2,1},{3,0},{4,7},{5,6},{6,5},{7,4},{8,11},{9,10},{10,... | collective-permute-start | bytes 491528 | tf_op jit(solution)/shard_map/ppermute | solution.py:438
  19.2 10.5 %copy-start.7 = (f32[2,512]{1,0:T(2,128)S(1)}, f32[2,512]{1,0:T(2,128)}, u32[]{:S(2)}) copy-start(f32[2,512]{1,0:T(2,128)} %constant.24.clone.odd) | copy-start | bytes 12292
  19.2 14.3 %collective-permute-start.3 = (f32[5,64,128]{2,1,0:T(8,128)S(1)}, f32[5,64,128]{2,1,0:T(8,128)S(1)}, u32[]{:S(2)}, u32[]{:S(2)}) collective-permute-start(f32[5,64,128]{2,1,0:T(8,128)S(1)} %get-tuple-element.47), channel_id=1, source_target_pairs={{0,1},{1,0},{2,3},{3,2},{4,5},{5,4},{6,7},{7,6},{8,9},{9,8},{10,11... | collective-permute-start | bytes 491528 | tf_op jit(solution)/shard_map/ppermute | solution.py:438
  19.3 16.4 %collective-permute-start.4 = (f32[5,64,128]{2,1,0:T(8,128)S(1)}, f32[5,64,128]{2,1,0:T(8,128)S(1)}, u32[]{:S(2)}, u32[]{:S(2)}) collective-permute-start(f32[5,64,128]{2,1,0:T(8,128)S(1)} %get-tuple-element.48), channel_id=1, source_target_pairs={{0,2},{1,3},{2,0},{3,1},{4,6},{5,7},{6,4},{7,5},{8,10},{9,11},{10,... | collective-permute-start | bytes 491528 | tf_op jit(solution)/shard_map/ppermute | solution.py:438
  20.6 15.1 %collective-permute-start.5 = (f32[5,64,128]{2,1,0:T(8,128)S(1)}, f32[5,64,128]{2,1,0:T(8,128)S(1)}, u32[]{:S(2)}, u32[]{:S(2)}) collective-permute-start(f32[5,64,128]{2,1,0:T(8,128)S(1)} %get-tuple-element.49), channel_id=1, source_target_pairs={{0,3},{1,2},{2,1},{3,0},{4,7},{5,6},{6,5},{7,4},{8,11},{9,10},{10,... | collective-permute-start | bytes 491528 | tf_op jit(solution)/shard_map/ppermute | solution.py:438
  32.0 7.8 %collective-permute-start.12 = (f32[128,256]{1,0:T(8,128)S(1)}, f32[128,256]{1,0:T(8,128)S(1)}, u32[]{:S(2)}, u32[]{:S(2)}) collective-permute-start(f32[128,256]{1,0:T(8,128)S(1)} %get-tuple-element.66), channel_id=1, source_target_pairs={{0,1},{1,0},{2,3},{3,2},{4,5},{5,4},{6,7},{7,6},{8,9},{9,8},{10,11... | collective-permute-start | bytes 393224 | tf_op jit(solution)/shard_map/ppermute | solution.py:438
  32.1 10.0 %collective-permute-start.13 = (f32[128,256]{1,0:T(8,128)S(1)}, f32[128,256]{1,0:T(8,128)S(1)}, u32[]{:S(2)}, u32[]{:S(2)}) collective-permute-start(f32[128,256]{1,0:T(8,128)S(1)} %get-tuple-element.67), channel_id=1, source_target_pairs={{0,2},{1,3},{2,0},{3,1},{4,6},{5,7},{6,4},{7,5},{8,10},{9,11},{10,... | collective-permute-start | bytes 393224 | tf_op jit(solution)/shard_map/ppermute | solution.py:438
  33.5 8.5 %collective-permute-start.14 = (f32[128,256]{1,0:T(8,128)S(1)}, f32[128,256]{1,0:T(8,128)S(1)}, u32[]{:S(2)}, u32[]{:S(2)}) collective-permute-start(f32[128,256]{1,0:T(8,128)S(1)} %get-tuple-element.68), channel_id=1, source_target_pairs={{0,3},{1,2},{2,1},{3,0},{4,7},{5,6},{6,5},{7,4},{8,11},{9,10},{10,... | collective-permute-start | bytes 393224 | tf_op jit(solution)/shard_map/ppermute | solution.py:438
  38.3 4.8 %collective-permute-start.6 = (f32[96,256]{1,0:T(8,128)S(1)}, f32[96,256]{1,0:T(8,128)S(1)}, u32[]{:S(2)}, u32[]{:S(2)}) collective-permute-start(f32[96,256]{1,0:T(8,128)S(1)} %get-tuple-element.55), channel_id=1, source_target_pairs={{0,1},{1,0},{2,3},{3,2},{4,5},{5,4},{6,7},{7,6},{8,9},{9,8},{10,11... | collective-permute-start | bytes 294920 | tf_op jit(solution)/shard_map/ppermute | solution.py:438
  38.4 5.5 %collective-permute-start.7 = (f32[96,256]{1,0:T(8,128)S(1)}, f32[96,256]{1,0:T(8,128)S(1)}, u32[]{:S(2)}, u32[]{:S(2)}) collective-permute-start(f32[96,256]{1,0:T(8,128)S(1)} %get-tuple-element.56), channel_id=1, source_target_pairs={{0,2},{1,3},{2,0},{3,1},{4,6},{5,7},{6,4},{7,5},{8,10},{9,11},{10,... | collective-permute-start | bytes 294920 | tf_op jit(solution)/shard_map/ppermute | solution.py:438
  39.7 6.9 %collective-permute-start.8 = (f32[96,256]{1,0:T(8,128)S(1)}, f32[96,256]{1,0:T(8,128)S(1)}, u32[]{:S(2)}, u32[]{:S(2)}) collective-permute-start(f32[96,256]{1,0:T(8,128)S(1)} %get-tuple-element.57), channel_id=1, source_target_pairs={{0,3},{1,2},{2,1},{3,0},{4,7},{5,6},{6,5},{7,4},{8,11},{9,10},{10,... | collective-permute-start | bytes 294920 | tf_op jit(solution)/shard_map/ppermute | solution.py:438

commit v2 on v1

v2 whole, which is shorter than its diff:
```python
import functools
import math

import jax
import jax.numpy as jnp
import numpy as np
from jax import lax
from jax.experimental import pallas as pl
from jax.experimental.pallas import tpu as pltpu
from jax.sharding import PartitionSpec as P


wiener = 0.1
gain_out = 8.0
cut_share = 0.45
PIX = 512
GRID = 1024
PHASES = 5
PARTS = 4
ROWS = PIX // PARTS
CHUNKS = (0, 1)
LOW = (24, 0)
MAIN = (40, 24)
FOLD_LOW = (24, 16)
FOLD = (40, 8)
COLS = (80, 32)
EXT = (40, 32)
ORDERS = (0, 1, -1, 2, -2)
ARC = (
    1.5707963050,
    -0.2145988016,
    0.0889789874,
    -0.0501743046,
    0.0308918810,
    -0.0170881256,
    0.0066700901,
    -0.0012624911,
)


def split_np(array):
    hi = array.astype(jnp.bfloat16)
    lo = (array - hi.astype(np.float32)).astype(jnp.bfloat16)
    return hi, lo


def split(array):
    hi = array.astype(jnp.bfloat16)
    lo = (array - hi.astype(jnp.float32)).astype(jnp.bfloat16)
    return hi, lo


def column_freq_np(d, chunk):
    def column(low, count):
        l = np.arange(low, low + count)
        return 64 * (l // 16) + 16 * d + l % 16

    fold = column(FOLD_LOW[chunk], FOLD[chunk]) - PIX
    if d == 0 and chunk == 1:
        fold[0] = -PIX // 2
    return np.concatenate([column(LOW[chunk], MAIN[chunk]), fold])


@functools.cache
def tables():
    index = np.arange(PIX)
    angle = 2.0 * np.pi * (np.outer(index[:ROWS], index) % PIX) / PIX
    base = np.stack([np.cos(angle), np.sin(angle)]).astype(np.float32)
    first = np.zeros((PARTS, 2, sum(COLS), 128), np.float32)
    for s in range(PARTS):
        freq = np.concatenate([column_freq_np(s, c) for c in CHUNKS])
        scale = gain_out / (GRID * GRID) * np.where(freq == 0, 1.0, 2.0)
        turn = 2.0 * np.pi * ((freq[:, None] * np.arange(128)[None, :]) % GRID) / GRID
        first[s, 0] = scale[:, None] * np.cos(turn)
        first[s, 1] = scale[:, None] * np.sin(turn)
    turn = 2.0 * np.pi * index / GRID
    odd = np.stack([np.cos(turn), np.sin(turn)]).astype(np.float32)
    return np.stack(split_np(base)), first, odd


def dot3(left, right, dims):
    lhs = jnp.concatenate([left[0], left[0], left[1]], axis=dims[0])
    rhs = jnp.concatenate([right[0], right[1], right[0]], axis=dims[1])
    return lax.dot_general(
        lhs, rhs, (((dims[0],), (dims[1],)), ((), ())), preferred_element_type=jnp.float32
    )


def turn_pair(steps):
    angle = (2.0 * math.pi / PIX) * ((steps + 256) % 512 - 256).astype(jnp.float32)
    return jnp.cos(angle), jnp.sin(angle)


def phase_kernel(place, shift, offset, source, base, frames, turns, phases, *rest):
    y_out, x_out, sem = rest[0:2], (rest[2:4], rest[4:6]), rest[6]
    copy = pltpu.make_async_copy(source.at[0], frames, sem)
    copy.start()
    rank = place[0]
    shift_y = shift[0]
    shift_x = shift[1]
    x_cos, x_sin = turn_pair(lax.broadcasted_iota(jnp.int32, (8, PIX), 1) * shift_x)
    row_at = lax.broadcasted_iota(jnp.int32, (ROWS, 128), 0) + rank * ROWS
    y_cos, y_sin = turn_pair(row_at * shift_y)
    x_cos, x_sin = x_cos[:1], x_sin[:1]
    y_cos = jnp.concatenate([y_cos] * 4, axis=1)
    y_sin = jnp.concatenate([y_sin] * 4, axis=1)
    turn_re = x_cos * y_cos - x_sin * y_sin
    turn_im = x_cos * y_sin + x_sin * y_cos
    turns[0] = turn_re
    turns[1] = turn_im
    turns[2] = turn_re * turn_re - turn_im * turn_im
    turns[3] = 2.0 * turn_re * turn_im
    phase_at = lax.broadcasted_iota(jnp.int32, (8, 128), 0).astype(jnp.float32)
    phase_at = (2.0 * math.pi / PHASES) * phase_at + offset[0]
    phases[0] = jnp.cos(phase_at)
    phases[1] = jnp.sin(phase_at)
    phases[2] = jnp.cos(2.0 * phase_at)
    phases[3] = jnp.sin(2.0 * phase_at)
    lane = lax.broadcasted_iota(jnp.int32, (1, PIX), 1)
    parity = lane % 2
    sign = (1 - lane % 4 + parity).astype(jnp.float32)
    quarter_re = jnp.where(parity == 0, sign, 0.0)
    quarter_im = jnp.where(parity == 1, sign, 0.0)
    half_turn = 1.0 - 2.0 * parity.astype(jnp.float32)
    for part in range(2):
        cosine, sine = base[part, 0].astype(jnp.float32), base[part, 1].astype(jnp.float32)
        cos_re, cos_im = cosine * quarter_re, cosine * quarter_im
        sin_re, sin_im = sine * quarter_re, sine * quarter_im
        blocks = [
            (cosine, sine),
            (cos_re - sin_im, sin_re + cos_im),
            (cosine * half_turn, sine * half_turn),
            (cos_re + sin_im, sin_re - cos_im),
        ]
        for s in range(PARTS):
            for kind in range(2):
                y_out[part][s, kind] = blocks[s][kind].astype(jnp.bfloat16)
        lone = half_turn if part == 0 else jnp.zeros_like(half_turn)
        top = lax.broadcasted_iota(jnp.int32, (8, PIX), 0) == 0
        for chunk in CHUNKS:
            for d in range(PARTS):
                pieces = []
                for kind in range(2):
                    for l in range(LOW[chunk], LOW[chunk] + MAIN[chunk], 8):
                        column = 64 * (l // 16) + 16 * d + l % 16
                        s, t = column // ROWS, column % ROWS
                        piece = blocks[s][kind][t : t + 8]
                        if column == 0 and kind == 1:
                            piece = jnp.where(top, lone, piece)
                        pieces.append(piece)
                x_out[chunk][part][d] = jnp.concatenate(pieces, axis=0).astype(jnp.bfloat16)
    copy.wait()


def spectra_rows(rank, rows, band, x_hi, x_lo, outs):
    table = (
        jnp.concatenate([x_hi[rank ^ k] for k in range(PARTS)], axis=0),
        jnp.concatenate([x_lo[rank ^ k] for k in range(PARTS)], axis=0),
    )
    spectra = dot3(table, band, (1, 1))
    for k in range(PARTS):
        for plane in range(5):
            outs[k][plane] = spectra[
                k * rows : (k + 1) * rows, plane * ROWS : (plane + 1) * ROWS
            ]


def forward_kernel(place, sums0, sums1, sums2, sums3, turns, phases, frames, x_hi, x_lo, *rest):
    outs, (band_hi, band_lo) = rest[:PARTS], rest[PARTS:]
    total = (sums0[...] + sums1[...]) + (sums2[...] + sums3[...])
    weight_all = (PIX * PIX / PHASES) / total
    acc = None
    for p in range(PHASES):
        weight = weight_all[:, p : p + 1]
        plane = frames[p].astype(jnp.float32)
        terms = [plane * weight] + [
            plane * (weight * phases[i, p : p + 1, 0:1]) for i in range(4)
        ]
        acc = terms if p == 0 else [a + b for a, b in zip(acc, terms)]
    zero, one_re, one_im, two_re, two_im = acc
    planes = [
        zero,
        one_re * turns[0] + one_im * turns[1],
        one_re * turns[1] - one_im * turns[0],
        two_re * turns[2] + two_im * turns[3],
        two_re * turns[3] - two_im * turns[2],
    ]
    for index, plane in enumerate(planes):
        hi, lo = split(plane)
        band_hi[index * ROWS : (index + 1) * ROWS, :] = hi
        band_lo[index * ROWS : (index + 1) * ROWS, :] = lo
    spectra_rows(place[0], 2 * MAIN[0], (band_hi[...], band_lo[...]), x_hi, x_lo, outs)


def forward_rest_kernel(place, band_hi, band_lo, x_hi, x_lo, *outs):
    spectra_rows(place[0], 2 * MAIN[1], (band_hi[...], band_lo[...]), x_hi, x_lo, outs)


def transfer_curve(squared):
    radius = jnp.minimum(jnp.sqrt(squared * (1.0 / (cut_share * PIX) ** 2)), 1.0)
    arc = jnp.full_like(radius, ARC[7])
    for coefficient in ARC[6::-1]:
        arc = arc * radius + coefficient
    return (2.0 / math.pi) * jnp.sqrt(1.0 - radius) * (arc - radius * jnp.sqrt(1.0 + radius))


def weights_kernel(place, gains, shift, after, weights0, weights1, y_square, y_low):
    weights = (weights0, weights1)
    rank = place[0]
    shift_y, shift_x = shift[0], shift[1]
    own = [gains[m + 2] for m in ORDERS]
    other = [gains[2 - m] for m in ORDERS]
    sub = lax.broadcasted_iota(jnp.int32, (8, 1), 0)
    lane = lax.broadcasted_iota(jnp.int32, (8, PIX), 1)
    for order, m in enumerate(ORDERS):
        y = ((lane - m * shift_y + PIX // 2) & (PIX - 1)) - PIX // 2
        y_low[order] = jnp.where(y + m * shift_y >= 0, 1.0, 0.0)
        y = y.astype(jnp.float32)
        y_square[order] = y * y

    def tile_step(chunk, tile):
        low = 8 * tile
        folded = low >= MAIN[chunk]
        l = jnp.where(folded, low - MAIN[chunk] + FOLD_LOW[chunk], low + LOW[chunk])
        freq = 64 * (l // 16) + 16 * rank + l % 16
        freq_x = jnp.where(folded, freq - PIX, freq) + sub
        if chunk == 1:
            lone = jnp.logical_and(low == MAIN[1], rank == 0).astype(jnp.int32)
            freq_x = jnp.where(jnp.where(sub == 0, lone, 0) == 1, -PIX // 2, freq_x)
        dens = [jnp.full((8, PIX), wiener, jnp.float32)] * 4
        curves = []
        for order, m in enumerate(ORDERS):
            x = (freq_x - m * shift_x).astype(jnp.float32)
            curve = transfer_curve(x * x + y_square[order])
            power = curve * curve
            power_low = power * y_low[order]
            power_high = power - power_low
            g, h = own[order] * own[order], other[order] * other[order]
            dens = [
                dens[0] + g * power_low,
                dens[1] + g * power_high,
                dens[2] + h * power_low,
                dens[3] + h * power_high,
            ]
            curves.append(curve)
        own_low, own_high, other_low, other_high = [0.5 / den for den in dens]
        rows = pl.ds(pl.multiple_of(low, 8), 8)
        for order in range(5):
            is_low = y_low[order] > 0.5
            own_den = jnp.where(is_low, own_low, own_high)
            other_den = jnp.where(is_low, other_low, other_high)
            weight = curves[order] * (own[order] * own_den + other[order] * other_den)
            weights[chunk][order, 0, rows, :] = weight
            weights[chunk][order, 1, rows, :] = jnp.where(is_low, weight, -weight)

    for chunk in CHUNKS:
        lax.fori_loop(
            0, COLS[chunk] // 8, lambda tile, _, chunk=chunk: (tile_step(chunk, tile), 0)[1], 0
        )


def table_kernel(place, first, after, hi0, hi1, lo0, lo1):
    outs = ((hi0, lo0), (hi1, lo1))
    rank = place[0]
    turn = lax.broadcasted_iota(jnp.int32, (8, 128), 0).astype(jnp.float32) * (math.pi / 4)
    turn_re, turn_im = jnp.cos(turn), jnp.sin(turn)
    low = 0
    for chunk in CHUNKS:
        rows = COLS[chunk]
        step_re = jnp.concatenate([turn_re] * (rows // 8), axis=0)
        step_im = jnp.concatenate([turn_im] * (rows // 8), axis=0)
        for k in range(PARTS):
            source = rank ^ k
            re, im = first[source, 0, low : low + rows], first[source, 1, low : low + rows]
            for block in range(GRID // 128):
                lanes = slice(128 * block, 128 * (block + 1))
                for part, value in ((0, re), (1, -im)):
                    at = slice((2 * k + part) * rows, (2 * k + part + 1) * rows)
                    outs[chunk][0][at, lanes], outs[chunk][1][at, lanes] = split(value)
                re, im = re * step_re - im * step_im, re * step_im + im * step_re
        low += rows


def middle_kernel(chunk, place, got0, got1, got2, got3, weights, y_hi, y_lo, odd, *outs):
    rank = place[0]
    blocks = (got0, got1, got2, got3)
    rows, ext, count = COLS[chunk], EXT[chunk], MAIN[chunk]
    if chunk == 1:
        first_row = lax.broadcasted_iota(jnp.int32, (count, PIX), 0) == 0
        lone = jnp.logical_and(first_row, jnp.full((count, PIX), rank, jnp.int32) == 0)
        top = lax.broadcasted_iota(jnp.int32, (8, PIX), 0) == 0
        swap = lone[:8]

    def plane(index):
        whole = jnp.concatenate([b[index] for b in blocks], axis=1)
        cosines, sines = whole[:count], whole[count:]
        if chunk == 0:
            return cosines, sines, None
        return cosines, jnp.where(lone, 0.0, sines), jnp.where(top, sines[:8], 0.0)

    real_rows = []
    imag_rows = []

    def add_row(re, im, extra_re, extra_im):
        real_rows.append(re)
        imag_rows.append(im)
        if chunk == 1:
            real_rows.append(extra_re)
            imag_rows.append(extra_im() if callable(extra_im) else extra_im)

    cos_r, sin_r, extra_r = plane(0)
    add_row(cos_r, -sin_r, extra_r, lambda: jnp.zeros_like(extra_r))
    for m in range(2):
        cos_r, sin_r, extra_r = plane(1 + 2 * m)
        cos_i, sin_i, extra_i = plane(2 + 2 * m)
        add_row(cos_r + sin_i, cos_i - sin_r, extra_r, extra_i)
        add_row(cos_r - sin_i, -cos_i - sin_r, extra_r, lambda: -extra_i)
    data = split(jnp.concatenate(real_rows + imag_rows, axis=0))

    def y_matrix(ref):
        return jnp.concatenate(
            [jnp.concatenate([ref[rank ^ k, 0], ref[rank ^ k, 1]], axis=1) for k in range(PARTS)],
            axis=0,
        )

    turned = dot3(data, (y_matrix(y_hi), y_matrix(y_lo)), (1, 0))
    half = 5 * ext
    spec_re = turned[:half, :PIX] + turned[half:, PIX:]
    spec_im = turned[half:, :PIX] - turned[:half, PIX:]
    sums = None
    for order in range(5):

        def both(spec):
            main = spec[order * ext : order * ext + count]
            if chunk == 0:
                return jnp.concatenate([main, main], axis=0)
            extra = spec[order * ext + count : (order + 1) * ext]
            return jnp.concatenate(
                [main, jnp.where(swap, extra, main[16:24])] + ([main[24:]] if count > 24 else []), axis=0
            )

        re, im = both(spec_re), both(spec_im)
        plus, minus = weights[order, 0], weights[order, 1]
        terms = (plus * re, plus * im, minus * re, minus * im)
        sums = terms if order == 0 else tuple(a + b for a, b in zip(sums, terms))
    even_re, even_im, odd_re, odd_im = sums
    odd_cos, odd_sin = odd[0:1], odd[1:2]
    odd_re, odd_im = odd_re * odd_cos - odd_im * odd_sin, odd_re * odd_sin + odd_im * odd_cos
    filtered = split(jnp.concatenate([even_re, even_im, odd_re, odd_im], axis=0))

    def u_matrix(ref):
        return jnp.concatenate(
            [jnp.concatenate([ref[rank ^ k, 0], ref[rank ^ k, 1]], axis=0) for k in range(PARTS)],
            axis=0,
        )

    back = dot3(filtered, (u_matrix(y_hi), u_matrix(y_lo)), (1, 1))
    for k in range(PARTS):
        cos_part = back[:, 2 * ROWS * k : 2 * ROWS * k + ROWS]
        sin_part = back[:, 2 * ROWS * k + ROWS : 2 * ROWS * (k + 1)]
        for parity in range(2):
            base = 2 * rows * parity
            re, im = slice(base, base + rows), slice(base + rows, base + 2 * rows)
            lanes = slice(parity * ROWS, (parity + 1) * ROWS)
            outs[k][0:rows, lanes] = cos_part[re] - sin_part[im]
            outs[k][rows : 2 * rows, lanes] = sin_part[re] + cos_part[im]


def gathered(blocks):
    return split(jnp.concatenate([b[...] for b in blocks], axis=0))


def part_kernel(got0, got1, got2, got3, final_hi, final_lo, part):
    data = gathered((got0, got1, got2, got3))
    part[...] = dot3(data, (final_hi[...], final_lo[...]), (0, 0))


def final_kernel(got0, got1, got2, got3, final_hi, final_lo, part, out, woven, sems):
    data = gathered((got0, got1, got2, got3))
    copies = []
    for strip in range(GRID // 256):
        lanes = slice(256 * strip, 256 * (strip + 1))
        picture = part[:, lanes] + dot3(data, (final_hi[:, lanes], final_lo[:, lanes]), (0, 0))
        for block in range(2):
            at = 2 * strip + block
            piece = slice(128 * block, 128 * (block + 1))
            woven[at, pl.ds(0, ROWS, 2), :] = picture[:ROWS, piece]
            woven[at, pl.ds(1, ROWS, 2), :] = picture[ROWS:, piece]
            copy = pltpu.make_async_copy(
                woven.at[at], out.at[:, pl.ds(128 * at, 128)], sems.at[at]
            )
            copy.start()
            copies.append(copy)
    for copy in copies:
        copy.wait()


def smem():
    return pl.BlockSpec(memory_space=pltpu.SMEM)


def vmem():
    return pl.BlockSpec(memory_space=pltpu.VMEM)


def hbm():
    return pl.BlockSpec(memory_space=pltpu.HBM)


def f32(*shape):
    return jax.ShapeDtypeStruct(shape, jnp.float32)


def bf16(*shape):
    return jax.ShapeDtypeStruct(shape, jnp.bfloat16)


def call(kernel, out_shape, in_specs, out_specs=None, scratch=(), limit=24):
    if out_specs is None:
        out_specs = jax.tree.map(lambda _: vmem(), out_shape)
    return pl.pallas_call(
        kernel,
        out_shape=out_shape,
        in_specs=in_specs,
        out_specs=out_specs,
        scratch_shapes=list(scratch),
        compiler_params=pltpu.CompilerParams(vmem_limit_bytes=limit * 1024 * 1024),
    )


def from_partners(blocks):
    got = [blocks[0]]
    for k in range(1, PARTS):
        got.append(lax.ppermute(blocks[k], "row", [(i, i ^ k) for i in range(PARTS)]))
    return got


def reconstruct(frames, phase_offset, order_gain, band_shift):
    base, first, odd = tables()
    order_gain, band_shift = order_gain[0], band_shift[0]
    rank = lax.axis_index("row")
    place = rank.reshape(1).astype(jnp.int32)

    sums = jnp.sum(frames.astype(jnp.float32), axis=(2, 3))
    sums = from_partners([sums] * PARTS)
    frames, turns, phases, y_hi, y_lo, *x_parts = call(
        phase_kernel,
        [bf16(PHASES, ROWS, PIX), f32(4, ROWS, PIX), f32(4, 8, 128)]
        + [bf16(PARTS, 2, ROWS, PIX)] * 2
        + [bf16(PARTS, 2 * MAIN[c], PIX) for c in CHUNKS for _ in range(2)],
        [smem()] * 3 + [hbm(), vmem()],
        scratch=[pltpu.SemaphoreType.DMA],
    )(place, band_shift, phase_offset, frames, base)
    blocks = [f32(5, 2 * MAIN[c], ROWS) for c in CHUNKS]
    *sent, band_hi, band_lo = call(
        forward_kernel,
        [blocks[0]] * PARTS + [bf16(5 * ROWS, PIX)] * 2,
        [smem()] + [vmem()] * 9,
    )(place, *sums, turns, phases, frames, *x_parts[:2])
    spectra = [from_partners(sent)]
    sent = call(forward_rest_kernel, [blocks[1]] * PARTS, [smem()] + [vmem()] * 4)(
        place, band_hi, band_lo, *x_parts[2:]
    )
    spectra.append(from_partners(sent))
    weights = call(
        weights_kernel,
        [f32(5, 2, COLS[c], PIX) for c in CHUNKS],
        [smem()] * 3 + [vmem()],
        scratch=[pltpu.VMEM((5, 8, PIX), jnp.float32)] * 2,
    )(place, order_gain, band_shift, sent[0])
    hi0, hi1, lo0, lo1 = call(
        table_kernel,
        [bf16(8 * COLS[c], GRID) for c in CHUNKS] * 2,
        [smem()] + [vmem()] * 2,
    )(place, first, sent[0])
    got = []
    for c in CHUNKS:
        sent = call(
            functools.partial(middle_kernel, c),
            [f32(2 * COLS[c], 2 * ROWS)] * PARTS,
            [smem()] + [vmem()] * 8,
        )(place, *spectra[c], weights[c], y_hi, y_lo, odd)
        got.append(from_partners(sent))
    part = call(part_kernel, f32(2 * ROWS, GRID), [vmem()] * 6)(*got[0], hi0, lo0)
    return call(
        final_kernel,
        f32(2 * ROWS, GRID),
        [vmem()] * 7,
        hbm(),
        [
            pltpu.VMEM((GRID // 128, 2 * ROWS, 128), jnp.float32),
            pltpu.SemaphoreType.DMA((GRID // 128,)),
        ],
    )(*got[1], hi1, lo1, part)


def solution(mesh):
    in_specs = (P("fov", None, "row", None), P("fov"), P("fov", None), P("fov", None))
    out_specs = P(("fov", "row"), None)
    return jax.shard_map(
        reconstruct, mesh=mesh, in_specs=in_specs, out_specs=out_specs, check_vma=False
    )
```

time: 48.8 us -> 51.9 us (1.064)
  waiting for transfers between devices: 3.59 us -> 9.48 us
  Pallas kernels: 18.7 us -> 16.6 us
  other arithmetic: 0 us -> 1.3 us
  local copies, waits for them, and re-layouts: 3.86 us -> 2.8 us
  starting transfers between devices: 21.4 us -> 20.6 us
    ppermute x15, waiting for transfers between devices: 3.59 us -> 9.48 us  [from_partners(): lax.ppermute(blocks[k], 'row', [(i, i ^ k) for i in range(PARTS)])]
    pallas_call x9, Pallas kernels: 18.7 us -> 16.6 us  [the longest x2 5.22 us: reconstruct(): call(functools.partial(middle_kernel, c), [f32(2 * COLS[c], 2 * ROWS)] *...]
    reduce_sum x0 -> x1, other arithmetic: none -> 1.3 us  [reconstruct(): sums = jnp.sum(frames.astype(jnp.float32), axis=(2, 3))]
    unnamed x20 -> x12, local copies, waits for them, and re-layouts: 3.86 us -> 2.8 us
    ppermute x15, starting transfers between devices: 21.4 us -> 20.6 us  [from_partners(): lax.ppermute(blocks[k], 'row', [(i, i ^ k) for i in range(PARTS)])]
  transfers between devices with their start and end apart: 15 -> 15, of which waited for: 2 -> 4; matrix products, arithmetic and copies ran while one was open for 0% -> 0% of each run, Pallas kernels for 30% -> 26%
where the time goes in v2:
time: 51.9 us; the launch traced here: 51.7 us
  starting transfers between devices  20.6 us (40%)
  Pallas kernels  16.6 us (32%)
  waiting for transfers between devices  9.48 us (18%)
  local copies, waits for them, and re-layouts  2.8 us (5%)
  other arithmetic  1.3 us (3%)
  between operations  0.98 us (2%)
    ppermute x15, starting transfers between devices, from_partners(): lax.ppermute(blocks[k], 'row', [(i, i ^ k) for i in range(PARTS)])  20.6 us
    ppermute x15, waiting for transfers between devices, from_partners(): lax.ppermute(blocks[k], 'row', [(i, i ^ k) for i in range(PARTS)])  9.48 us
    pallas_call x2, Pallas kernels, reconstruct(): call(functools.partial(middle_kernel, c), [f32(2 * COLS[c], 2 * ROWS)] *...  5.22 us
    pallas_call x1, Pallas kernels, reconstruct(): call(weights_kernel, [f32(5, 2, COLS[c], PIX) for c in CHUNKS], [smem()]...  3.47 us
    unnamed x12, local copies, waits for them, and re-layouts  2.8 us
    pallas_call x1, Pallas kernels, reconstruct(): call(phase_kernel, [bf16(PHASES, ROWS, PIX), f32(4, ROWS, PIX), f32(4, 8,...  1.7 us
    pallas_call x1, Pallas kernels, reconstruct(): call(forward_kernel, [blocks[0]] * PARTS + [bf16(5 * ROWS, PIX)] * 2, [sm...  1.55 us
    pallas_call x1, Pallas kernels, reconstruct(): call(final_kernel, f32(2 * ROWS, GRID), [vmem()] * 7, hbm(), [pltpu.VMEM(...  1.52 us
  transfers between devices with their start and end apart: 15, of which 4 were waited for; matrix products, arithmetic and copies ran while one was open for 0% of the time, Pallas kernels for 26%

profile of v2, /device:TPU:1, one launch (start us, length us, event | category | flops | bytes accessed | tf_op | source)
XLA Modules:
  0.0 51.7 jit_solution(11624056062470795869)
XLA Ops:
  0.0 1.3 %convert_reduce_fusion = f32[5]{0:T(128)S(1)} fusion(bf16[1,5,128,512]{3,2,1,0:T(8,128)(2,1)} %source.1), kind=kLoop, calls=%fused_computation | loop fusion | flops 655355 | bytes 655380 | tf_op jit(solution)/shard_map/reduce_sum | solution.py:444
  1.3 4.3 %collective-permute-start.2 = (f32[1,5]{1,0:T(1,128)S(1)}, f32[1,5]{1,0:T(1,128)S(1)}, u32[]{:S(2)}, u32[]{:S(2)}) collective-permute-start(f32[1,5]{1,0:T(1,128)S(1)} %bitcast.6), channel_id=1, source_target_pairs={{0,3},{1,2},{2,1},{3,0},{4,7},{5,6},{6,5},{7,4},{8,11},{9,10},{10,... | collective-permute-start | bytes 68 | tf_op jit(solution)/shard_map/ppermute | solution.py:434
  5.6 1.8 %collective-permute-start.1 = (f32[1,5]{1,0:T(1,128)S(1)}, f32[1,5]{1,0:T(1,128)S(1)}, u32[]{:S(2)}, u32[]{:S(2)}) collective-permute-start(f32[1,5]{1,0:T(1,128)S(1)} %bitcast.7), channel_id=1, source_target_pairs={{0,2},{1,3},{2,0},{3,1},{4,6},{5,7},{6,4},{7,5},{8,10},{9,11},{10,... | collective-permute-start | bytes 68 | tf_op jit(solution)/shard_map/ppermute | solution.py:434
  7.4 0.0 collective-permute-start
  8.1 0.0 copy-start
  8.1 1.1 %copy-done = bf16[1,5,128,512]{3,2,1,0:T(8,128)(2,1)S(1)} copy-done((bf16[1,5,128,512]{3,2,1,0:T(8,128)(2,1)S(1)}, bf16[1,5,128,512]{3,2,1,0:T(8,128)(2,1)}, u32[]{:S(2)}) %copy-start) | copy-done | bytes 655384
  9.2 1.0 %copy-done.1 = bf16[2,2,128,512]{3,2,1,0:T(8,128)(2,1)S(1)} copy-done((bf16[2,2,128,512]{3,2,1,0:T(8,128)(2,1)S(1)}, bf16[2,2,128,512]{3,2,1,0:T(8,128)(2,1)}, u32[]{:S(2)}) %copy-start.1) | copy-done | bytes 524312
  10.2 0.7 %copy-done.4 = s32[1,2]{1,0:T(1,128)S(1)} copy-done((s32[1,2]{1,0:T(1,128)S(1)}, s32[1,2]{1,0:T(1,128)}, u32[]{:S(2)}) %copy-start.4) | copy-done | bytes 32
  10.9 1.7 %shard_map.73 = (bf16[5,128,512]{2,1,0:T(8,128)(2,1)S(1)}, f32[4,128,512]{2,1,0:T(8,128)S(1)}, f32[4,8,128]{2,1,0:T(8,128)S(1)}, bf16[4,2,128,512]{3,2,1,0:T(8,1...) custom-call(s32[1]{0:T(128)} %bitcast.place, ...), custom_call_target="tpu_custom_call" | custom-call | tf_op jit(solution)/shard_map/pallas_call | solution.py:446
  12.6 0.0 collective-permute-done.2.sums3
  12.6 0.0 collective-permute-done.1.sums2
  12.6 0.0 collective-permute-done.sums1
  12.6 1.6 %shard_map.74 = (f32[5,80,128]{2,1,0:T(8,128)S(1)}, f32[5,80,128]{2,1,0:T(8,128)S(1)}, f32[5,80,128]{2,1,0:T(8,128)S(1)}, f32[5,80,128]{2,1,0:T(8,128)S(1)}, bf1...) custom-call(s32[1]{0:T(128)} %bitcast.place, f32[1,5]{1,0:T(1,128)S(1)} %bitcast.9, ...), custom_call_target="tpu_custom_call" | custom-call | tf_op jit(solution)/shard_map/pallas_call | solution.py:455
  14.1 0.0 copy-start.5
  14.2 0.0 copy-start.3
  14.2 0.6 %collective-permute-start.9 = (f32[5,80,128]{2,1,0:T(8,128)S(1)}, f32[5,80,128]{2,1,0:T(8,128)S(1)}, u32[]{:S(2)}, u32[]{:S(2)}) collective-permute-start(f32[5,80,128]{2,1,0:T(8,128)S(1)} %get-tuple-element.61), channel_id=1, source_target_pairs={{0,1},{1,0},{2,3},{3,2},{4,5},{5,4},{6,7},{7,6},{8,9},{9,8},{10,11... | collective-permute-start | bytes 614408 | tf_op jit(solution)/shard_map/ppermute | solution.py:434
  14.8 1.2 %collective-permute-start.10 = (f32[5,80,128]{2,1,0:T(8,128)S(1)}, f32[5,80,128]{2,1,0:T(8,128)S(1)}, u32[]{:S(2)}, u32[]{:S(2)}) collective-permute-start(f32[5,80,128]{2,1,0:T(8,128)S(1)} %get-tuple-element.62), channel_id=1, source_target_pairs={{0,2},{1,3},{2,0},{3,1},{4,6},{5,7},{6,4},{7,5},{8,10},{9,11},{10,... | collective-permute-start | bytes 614408 | tf_op jit(solution)/shard_map/ppermute | solution.py:434
  16.0 2.0 %collective-permute-start.11 = (f32[5,80,128]{2,1,0:T(8,128)S(1)}, f32[5,80,128]{2,1,0:T(8,128)S(1)}, u32[]{:S(2)}, u32[]{:S(2)}) collective-permute-start(f32[5,80,128]{2,1,0:T(8,128)S(1)} %get-tuple-element.63), channel_id=1, source_target_pairs={{0,3},{1,2},{2,1},{3,0},{4,7},{5,6},{6,5},{7,4},{8,11},{9,10},{10,... | collective-permute-start | bytes 614408 | tf_op jit(solution)/shard_map/ppermute | solution.py:434
  18.0 0.8 %shard_map.75 = (f32[5,48,128]{2,1,0:T(8,128)S(1)}, f32[5,48,128]{2,1,0:T(8,128)S(1)}, f32[5,48,128]{2,1,0:T(8,128)S(1)}, f32[5,48,128]{2,1,0:T(8,128)S(1)}) custom-call(s32[1]{0:T(128)} %bitcast.place, bf16[640,512]{1,0:T(8,128)(2,1)S(1)} %get-tuple-element.43.band_hi, bf16[640,512]{1,0:T(8,128)(2,1)S(1)} %get-tuple-element.44.band_lo, ...), custom_call_target="tpu_custom_call" | custom-call | tf_op jit(solution)/shard_map/pallas_call | solution.py:461
  18.8 0.2 collective-permute-start.3
  19.0 0.0 copy-done.5
  19.0 3.5 %shard_map.76 = (f32[5,2,80,512]{3,2,1,0:T(8,128)S(1)}, f32[5,2,32,512]{3,2,1,0:T(8,128)S(1)}) custom-call(s32[1]{0:T(128)} %bitcast.place, f32[5]{0:T(128)S(1)} %bitcast.10, s32[2]{0:T(128)S(1)} %bitcast.5, f32[5,48,128]{2,1,0:T(8,128)S(1)} %get-tuple-element.47.after.got0), custom_call_target="tpu_custom_call" | custom-call | tf_op jit(solution)/shard_map/pallas_call | solution.py:465
  22.5 0.0 collective-permute-done.9.got1
  22.5 0.3 collective-permute-done.10.got2
  22.8 4.7 %collective-permute-done.11.got3 = f32[5,80,128]{2,1,0:T(8,128)S(1)} collective-permute-done((f32[5,80,128]{2,1,0:T(8,128)S(1)}, f32[5,80,128]{2,1,0:T(8,128)S(1)}, u32[]{:S(2)}, u32[]{:S(2)}) %collective-permute-start.11) | collective-permute-done | bytes 204832 | tf_op jit(solution)/shard_map/ppermute | solution.py:434
  27.5 2.9 %shard_map.79 = (f32[160,256]{1,0:T(8,128)S(1)}, f32[160,256]{1,0:T(8,128)S(1)}, f32[160,256]{1,0:T(8,128)S(1)}, f32[160,256]{1,0:T(8,128)S(1)}) custom-call(s32[1]{0:T(128)} %bitcast.place, f32[5,80,128]{2,1,0:T(8,128)S(1)} %get-tuple-element.60.got0, f32[5,80,128]{2,1,0:T(8,128)S(1)} %collective-permute-done.9.got1, ...), custom_call_target="tpu_custom_call" | custom-call | tf_op jit(solution)/shard_map/pallas_call | solution.py:478
  30.4 0.2 collective-permute-start.12
  30.6 1.2 %collective-permute-start.4 = (f32[5,48,128]{2,1,0:T(8,128)S(1)}, f32[5,48,128]{2,1,0:T(8,128)S(1)}, u32[]{:S(2)}, u32[]{:S(2)}) collective-permute-start(f32[5,48,128]{2,1,0:T(8,128)S(1)} %get-tuple-element.49), channel_id=1, source_target_pairs={{0,2},{1,3},{2,0},{3,1},{4,6},{5,7},{6,4},{7,5},{8,10},{9,11},{10,... | collective-permute-start | bytes 368648 | tf_op jit(solution)/shard_map/ppermute | solution.py:434
  31.8 2.3 %collective-permute-start.5 = (f32[5,48,128]{2,1,0:T(8,128)S(1)}, f32[5,48,128]{2,1,0:T(8,128)S(1)}, u32[]{:S(2)}, u32[]{:S(2)}) collective-permute-start(f32[5,48,128]{2,1,0:T(8,128)S(1)} %get-tuple-element.50), channel_id=1, source_target_pairs={{0,3},{1,2},{2,1},{3,0},{4,7},{5,6},{6,5},{7,4},{8,11},{9,10},{10,... | collective-permute-start | bytes 368648 | tf_op jit(solution)/shard_map/ppermute | solution.py:434
  34.1 1.2 %collective-permute-start.13 = (f32[160,256]{1,0:T(8,128)S(1)}, f32[160,256]{1,0:T(8,128)S(1)}, u32[]{:S(2)}, u32[]{:S(2)}) collective-permute-start(f32[160,256]{1,0:T(8,128)S(1)} %get-tuple-element.67), channel_id=1, source_target_pairs={{0,2},{1,3},{2,0},{3,1},{4,6},{5,7},{6,4},{7,5},{8,10},{9,11},{10,... | collective-permute-start | bytes 491528 | tf_op jit(solution)/shard_map/ppermute | solution.py:434
  35.3 0.0 collective-permute-done.3.got1
  35.3 1.8 %collective-permute-start.14 = (f32[160,256]{1,0:T(8,128)S(1)}, f32[160,256]{1,0:T(8,128)S(1)}, u32[]{:S(2)}, u32[]{:S(2)}) collective-permute-start(f32[160,256]{1,0:T(8,128)S(1)} %get-tuple-element.68), channel_id=1, source_target_pairs={{0,3},{1,2},{2,1},{3,0},{4,7},{5,6},{6,5},{7,4},{8,11},{9,10},{10,... | collective-permute-start | bytes 491528 | tf_op jit(solution)/shard_map/ppermute | solution.py:434
  37.1 0.0 collective-permute-done.4.got2
  37.1 3.5 %collective-permute-done.5.got3 = f32[5,48,128]{2,1,0:T(8,128)S(1)} collective-permute-done((f32[5,48,128]{2,1,0:T(8,128)S(1)}, f32[5,48,128]{2,1,0:T(8,128)S(1)}, u32[]{:S(2)}, u32[]{:S(2)}) %collective-permute-start.5) | collective-permute-done | bytes 122912 | tf_op jit(solution)/shard_map/ppermute | solution.py:434
  40.6 2.3 %shard_map.77 = (f32[64,256]{1,0:T(8,128)S(1)}, f32[64,256]{1,0:T(8,128)S(1)}, f32[64,256]{1,0:T(8,128)S(1)}, f32[64,256]{1,0:T(8,128)S(1)}) custom-call(s32[1]{0:T(128)} %bitcast.place, f32[5,48,128]{2,1,0:T(8,128)S(1)} %get-tuple-element.47.after.got0, f32[5,48,128]{2,1,0:T(8,128)S(1)} %collective-permute-done.3.got1, ...), custom_call_target="tpu_custom_call" | custom-call | tf_op jit(solution)/shard_map/pallas_call | solution.py:478
  42.9 0.1 collective-permute-start.6
  43.0 0.7 %collective-permute-start.7 = (f32[64,256]{1,0:T(8,128)S(1)}, f32[64,256]{1,0:T(8,128)S(1)}, u32[]{:S(2)}, u32[]{:S(2)}) collective-permute-start(f32[64,256]{1,0:T(8,128)S(1)} %get-tuple-element.56), channel_id=1, source_target_pairs={{0,2},{1,3},{2,0},{3,1},{4,6},{5,7},{6,4},{7,5},{8,10},{9,11},{10,... | collective-permute-start | bytes 196616 | tf_op jit(solution)/shard_map/ppermute | solution.py:434
  43.8 0.0 collective-permute-done.12.got1
  43.8 2.9 %collective-permute-start.8 = (f32[64,256]{1,0:T(8,128)S(1)}, f32[64,256]{1,0:T(8,128)S(1)}, u32[]{:S(2)}, u32[]{:S(2)}) collective-permute-start(f32[64,256]{1,0:T(8,128)S(1)} %get-tuple-element.57), channel_id=1, source_target_pairs={{0,3},{1,2},{2,1},{3,0},{4,7},{5,6},{6,5},{7,4},{8,11},{9,10},{10,... | collective-permute-start | bytes 196616 | tf_op jit(solution)/shard_map/ppermute | solution.py:434
  46.7 0.0 copy-done.2
  46.7 1.0 %shard_map.78 = (bf16[640,1024]{1,0:T(8,128)(2,1)S(1)}, bf16[256,1024]{1,0:T(8,128)(2,1)S(1)}, bf16[640,1024]{1,0:T(8,128)(2,1)S(1)}, bf16[256,1024]{1,0:T(8,128)(2,1)S(1)}) custom-call(s32[1]{0:T(128)} %bitcast.place, f32[4,2,112,128]{3,2,1,0:T(8,128)S(1)} %copy-done.2, f32[5,48,128]{2,1,0:T(8,128)S(1)} %get-tuple-element.47.after.got0), custom_call_target="tpu_custom_call" | custom-call | tf_op jit(solution)/shard_map/pallas_call | solution.py:471
  47.7 0.0 collective-permute-done.13.got2
  47.7 0.0 collective-permute-done.14.got3
  47.7 1.3 %shard_map.80.part = f32[256,1024]{1,0:T(8,128)S(1)} custom-call(f32[160,256]{1,0:T(8,128)S(1)} %get-tuple-element.65.got0, f32[160,256]{1,0:T(8,128)S(1)} %collective-permute-done.12.got1, f32[160,256]{1,0:T(8,128)S(1)} %collective-permute-done.13.got2, f32[160,256]{1,0:T(8,128)S(1)} %collective-permute-done.14.got3, ...), custom_call_target="tpu_custom_call" | custom-call | tf_op jit(solution)/shard_map/pallas_call | solution.py:484
  49.0 0.0 collective-permute-done.6.got1
  49.0 0.0 collective-permute-done.7.got2
  49.0 1.0 %collective-permute-done.8.got3 = f32[64,256]{1,0:T(8,128)S(1)} collective-permute-done((f32[64,256]{1,0:T(8,128)S(1)}, f32[64,256]{1,0:T(8,128)S(1)}, u32[]{:S(2)}, u32[]{:S(2)}) %collective-permute-start.8) | collective-permute-done | bytes 65568 | tf_op jit(solution)/shard_map/ppermute | solution.py:434
  50.0 1.5 %shard_map.81 = f32[256,1024]{1,0:T(8,128)} custom-call(f32[64,256]{1,0:T(8,128)S(1)} %get-tuple-element.54.got0, f32[64,256]{1,0:T(8,128)S(1)} %collective-permute-done.6.got1, f32[64,256]{1,0:T(8,128)S(1)} %collective-permute-done.7.got2, f32[64,256]{1,0:T(8,128)S(1)} %collective-permute-done.8.got3, bf16[256,1024]{1,0:T(8,128)(2,1)S(1)} %get-tuple-element.58.final_hi, ...), custom_call_target="tpu_custom_call" | custom-call | tf_op jit(solution)/shard_map/pallas_call | solution.py:485
  (4 shorter events, 0.0 us)
Async XLA Ops:
  1.3 11.3 %collective-permute-start.2 = (f32[1,5]{1,0:T(1,128)S(1)}, f32[1,5]{1,0:T(1,128)S(1)}, u32[]{:S(2)}, u32[]{:S(2)}) collective-permute-start(f32[1,5]{1,0:T(1,128)S(1)} %bitcast.6), channel_id=1, source_target_pairs={{0,3},{1,2},{2,1},{3,0},{4,7},{5,6},{6,5},{7,4},{8,11},{9,10},{10,... | collective-permute-start | bytes 68 | tf_op jit(solution)/shard_map/ppermute | solution.py:434
  5.6 6.9 %collective-permute-start.1 = (f32[1,5]{1,0:T(1,128)S(1)}, f32[1,5]{1,0:T(1,128)S(1)}, u32[]{:S(2)}, u32[]{:S(2)}) collective-permute-start(f32[1,5]{1,0:T(1,128)S(1)} %bitcast.7), channel_id=1, source_target_pairs={{0,2},{1,3},{2,0},{3,1},{4,6},{5,7},{6,4},{7,5},{8,10},{9,11},{10,... | collective-permute-start | bytes 68 | tf_op jit(solution)/shard_map/ppermute | solution.py:434
  7.4 5.2 %collective-permute-start = (f32[1,5]{1,0:T(1,128)S(1)}, f32[1,5]{1,0:T(1,128)S(1)}, u32[]{:S(2)}, u32[]{:S(2)}) collective-permute-start(f32[1,5]{1,0:T(1,128)S(1)} %bitcast.8), channel_id=1, source_target_pairs={{0,1},{1,0},{2,3},{3,2},{4,5},{5,4},{6,7},{7,6},{8,9},{9,8},{10,11... | collective-permute-start | bytes 68 | tf_op jit(solution)/shard_map/ppermute | solution.py:434
  8.1 1.1 %copy-start = (bf16[1,5,128,512]{3,2,1,0:T(8,128)(2,1)S(1)}, bf16[1,5,128,512]{3,2,1,0:T(8,128)(2,1)}, u32[]{:S(2)}) copy-start(bf16[1,5,128,512]{3,2,1,0:T(8,128)(2,1)} %source.1) | copy-start | bytes 1966084
  9.2 1.0 %copy-start.1 = (bf16[2,2,128,512]{3,2,1,0:T(8,128)(2,1)S(1)}, bf16[2,2,128,512]{3,2,1,0:T(8,128)(2,1)}, u32[]{:S(2)}) copy-start(bf16[2,2,128,512]{3,2,1,0:T(8,128)(2,1)} %constant.12.clone.base) | copy-start | bytes 1572868
  10.2 0.7 %copy-start.4 = (s32[1,2]{1,0:T(1,128)S(1)}, s32[1,2]{1,0:T(1,128)}, u32[]{:S(2)}) copy-start(s32[1,2]{1,0:T(1,128)} %param.10) | copy-start | bytes 28
  14.1 4.9 %copy-start.5 = (f32[1,5]{1,0:T(1,128)S(1)}, f32[1,5]{1,0:T(1,128)}, u32[]{:S(2)}) copy-start(f32[1,5]{1,0:T(1,128)} %param.9) | copy-start | bytes 64
  14.2 13.3 %copy-start.3 = (f32[2,512]{1,0:T(2,128)S(1)}, f32[2,512]{1,0:T(2,128)}, u32[]{:S(2)}) copy-start(f32[2,512]{1,0:T(2,128)} %constant.14.clone.odd) | copy-start | bytes 12292
  14.2 8.3 %collective-permute-start.9 = (f32[5,80,128]{2,1,0:T(8,128)S(1)}, f32[5,80,128]{2,1,0:T(8,128)S(1)}, u32[]{:S(2)}, u32[]{:S(2)}) collective-permute-start(f32[5,80,128]{2,1,0:T(8,128)S(1)} %get-tuple-element.61), channel_id=1, source_target_pairs={{0,1},{1,0},{2,3},{3,2},{4,5},{5,4},{6,7},{7,6},{8,9},{9,8},{10,11... | collective-permute-start | bytes 614408 | tf_op jit(solution)/shard_map/ppermute | solution.py:434
  14.8 8.0 %collective-permute-start.10 = (f32[5,80,128]{2,1,0:T(8,128)S(1)}, f32[5,80,128]{2,1,0:T(8,128)S(1)}, u32[]{:S(2)}, u32[]{:S(2)}) collective-permute-start(f32[5,80,128]{2,1,0:T(8,128)S(1)} %get-tuple-element.62), channel_id=1, source_target_pairs={{0,2},{1,3},{2,0},{3,1},{4,6},{5,7},{6,4},{7,5},{8,10},{9,11},{10,... | collective-permute-start | bytes 614408 | tf_op jit(solution)/shard_map/ppermute | solution.py:434
  16.0 11.5 %collective-permute-start.11 = (f32[5,80,128]{2,1,0:T(8,128)S(1)}, f32[5,80,128]{2,1,0:T(8,128)S(1)}, u32[]{:S(2)}, u32[]{:S(2)}) collective-permute-start(f32[5,80,128]{2,1,0:T(8,128)S(1)} %get-tuple-element.63), channel_id=1, source_target_pairs={{0,3},{1,2},{2,1},{3,0},{4,7},{5,6},{6,5},{7,4},{8,11},{9,10},{10,... | collective-permute-start | bytes 614408 | tf_op jit(solution)/shard_map/ppermute | solution.py:434
  18.8 16.5 %collective-permute-start.3 = (f32[5,48,128]{2,1,0:T(8,128)S(1)}, f32[5,48,128]{2,1,0:T(8,128)S(1)}, u32[]{:S(2)}, u32[]{:S(2)}) collective-permute-start(f32[5,48,128]{2,1,0:T(8,128)S(1)} %get-tuple-element.48), channel_id=1, source_target_pairs={{0,1},{1,0},{2,3},{3,2},{4,5},{5,4},{6,7},{7,6},{8,9},{9,8},{10,11... | collective-permute-start | bytes 368648 | tf_op jit(solution)/shard_map/ppermute | solution.py:434
  30.4 13.4 %collective-permute-start.12 = (f32[160,256]{1,0:T(8,128)S(1)}, f32[160,256]{1,0:T(8,128)S(1)}, u32[]{:S(2)}, u32[]{:S(2)}) collective-permute-start(f32[160,256]{1,0:T(8,128)S(1)} %get-tuple-element.66), channel_id=1, source_target_pairs={{0,1},{1,0},{2,3},{3,2},{4,5},{5,4},{6,7},{7,6},{8,9},{9,8},{10,11... | collective-permute-start | bytes 491528 | tf_op jit(solution)/shard_map/ppermute | solution.py:434
  30.6 6.5 %collective-permute-start.4 = (f32[5,48,128]{2,1,0:T(8,128)S(1)}, f32[5,48,128]{2,1,0:T(8,128)S(1)}, u32[]{:S(2)}, u32[]{:S(2)}) collective-permute-start(f32[5,48,128]{2,1,0:T(8,128)S(1)} %get-tuple-element.49), channel_id=1, source_target_pairs={{0,2},{1,3},{2,0},{3,1},{4,6},{5,7},{6,4},{7,5},{8,10},{9,11},{10,... | collective-permute-start | bytes 368648 | tf_op jit(solution)/shard_map/ppermute | solution.py:434
  31.8 8.8 %collective-permute-start.5 = (f32[5,48,128]{2,1,0:T(8,128)S(1)}, f32[5,48,128]{2,1,0:T(8,128)S(1)}, u32[]{:S(2)}, u32[]{:S(2)}) collective-permute-start(f32[5,48,128]{2,1,0:T(8,128)S(1)} %get-tuple-element.50), channel_id=1, source_target_pairs={{0,3},{1,2},{2,1},{3,0},{4,7},{5,6},{6,5},{7,4},{8,11},{9,10},{10,... | collective-permute-start | bytes 368648 | tf_op jit(solution)/shard_map/ppermute | solution.py:434
  34.1 13.6 %collective-permute-start.13 = (f32[160,256]{1,0:T(8,128)S(1)}, f32[160,256]{1,0:T(8,128)S(1)}, u32[]{:S(2)}, u32[]{:S(2)}) collective-permute-start(f32[160,256]{1,0:T(8,128)S(1)} %get-tuple-element.67), channel_id=1, source_target_pairs={{0,2},{1,3},{2,0},{3,1},{4,6},{5,7},{6,4},{7,5},{8,10},{9,11},{10,... | collective-permute-start | bytes 491528 | tf_op jit(solution)/shard_map/ppermute | solution.py:434
  35.3 12.4 %collective-permute-start.14 = (f32[160,256]{1,0:T(8,128)S(1)}, f32[160,256]{1,0:T(8,128)S(1)}, u32[]{:S(2)}, u32[]{:S(2)}) collective-permute-start(f32[160,256]{1,0:T(8,128)S(1)} %get-tuple-element.68), channel_id=1, source_target_pairs={{0,3},{1,2},{2,1},{3,0},{4,7},{5,6},{6,5},{7,4},{8,11},{9,10},{10,... | collective-permute-start | bytes 491528 | tf_op jit(solution)/shard_map/ppermute | solution.py:434
  40.6 6.1 %copy-start.2 = (f32[4,2,112,128]{3,2,1,0:T(8,128)S(1)}, f32[4,2,112,128]{3,2,1,0:T(8,128)}, u32[]{:S(2)}) copy-start(f32[4,2,112,128]{3,2,1,0:T(8,128)} %constant.13.clone.first) | copy-start | bytes 1376260
  42.9 6.1 %collective-permute-start.6 = (f32[64,256]{1,0:T(8,128)S(1)}, f32[64,256]{1,0:T(8,128)S(1)}, u32[]{:S(2)}, u32[]{:S(2)}) collective-permute-start(f32[64,256]{1,0:T(8,128)S(1)} %get-tuple-element.55), channel_id=1, source_target_pairs={{0,1},{1,0},{2,3},{3,2},{4,5},{5,4},{6,7},{7,6},{8,9},{9,8},{10,11... | collective-permute-start | bytes 196616 | tf_op jit(solution)/shard_map/ppermute | solution.py:434
  43.0 6.0 %collective-permute-start.7 = (f32[64,256]{1,0:T(8,128)S(1)}, f32[64,256]{1,0:T(8,128)S(1)}, u32[]{:S(2)}, u32[]{:S(2)}) collective-permute-start(f32[64,256]{1,0:T(8,128)S(1)} %get-tuple-element.56), channel_id=1, source_target_pairs={{0,2},{1,3},{2,0},{3,1},{4,6},{5,7},{6,4},{7,5},{8,10},{9,11},{10,... | collective-permute-start | bytes 196616 | tf_op jit(solution)/shard_map/ppermute | solution.py:434
  43.8 6.2 %collective-permute-start.8 = (f32[64,256]{1,0:T(8,128)S(1)}, f32[64,256]{1,0:T(8,128)S(1)}, u32[]{:S(2)}, u32[]{:S(2)}) collective-permute-start(f32[64,256]{1,0:T(8,128)S(1)} %get-tuple-element.57), channel_id=1, source_target_pairs={{0,3},{1,2},{2,1},{3,0},{4,7},{5,6},{6,5},{7,4},{8,11},{9,10},{10,... | collective-permute-start | bytes 196616 | tf_op jit(solution)/shard_map/ppermute | solution.py:434

commit v3 on v2

--- a/solution.py
+++ b/solution.py
@@ -91,9 +91,11 @@
     return jnp.cos(angle), jnp.sin(angle)
 
 
-def phase_kernel(place, shift, offset, source, base, frames, turns, phases, *rest):
-    y_out, x_out, sem = rest[0:2], (rest[2:4], rest[4:6]), rest[6]
-    copy = pltpu.make_async_copy(source.at[0], frames, sem)
+def phase_kernel(place, shift, offset, source, base_far, frames, turns, phases, *rest):
+    y_out, x_out, base, sems = rest[0:2], (rest[2:4], rest[4:6]), rest[6], rest[7]
+    base_copy = pltpu.make_async_copy(base_far, base, sems.at[0])
+    base_copy.start()
+    copy = pltpu.make_async_copy(source.at[0], frames, sems.at[1])
     copy.start()
     rank = place[0]
     shift_y = shift[0]
@@ -122,6 +124,7 @@
     quarter_re = jnp.where(parity == 0, sign, 0.0)
     quarter_im = jnp.where(parity == 1, sign, 0.0)
     half_turn = 1.0 - 2.0 * parity.astype(jnp.float32)
+    base_copy.wait()
     for part in range(2):
         cosine, sine = base[part, 0].astype(jnp.float32), base[part, 1].astype(jnp.float32)
         cos_re, cos_im = cosine * quarter_re, cosine * quarter_im
@@ -448,9 +451,15 @@
         [bf16(PHASES, ROWS, PIX), f32(4, ROWS, PIX), f32(4, 8, 128)]
         + [bf16(PARTS, 2, ROWS, PIX)] * 2
         + [bf16(PARTS, 2 * MAIN[c], PIX) for c in CHUNKS for _ in range(2)],
-        [smem()] * 3 + [hbm(), vmem()],
-        scratch=[pltpu.SemaphoreType.DMA],
-    )(place, band_shift, phase_offset, frames, base)
+        [smem()] * 3 + [hbm(), hbm()],
+        scratch=[pltpu.VMEM(base.shape, jnp.bfloat16), pltpu.SemaphoreType.DMA((2,))],
+    )(
+        place,
+        band_shift,
+        phase_offset,
+        pltpu.with_memory_space_constraint(frames, pltpu.HBM),
+        pltpu.with_memory_space_constraint(base, pltpu.HBM),
+    )
     blocks = [f32(5, 2 * MAIN[c], ROWS) for c in CHUNKS]
     *sent, band_hi, band_lo = call(
         forward_kernel,

time: 51.9 us -> 50.1 us (0.965)
  local copies, waits for them, and re-layouts: 2.8 us -> 0.67 us
    unnamed x12 -> x8, local copies, waits for them, and re-layouts: 2.8 us -> 0.67 us
  transfers between devices with their start and end apart: 15 -> 15, of which waited for: 4 -> 4; matrix products, arithmetic and copies ran while one was open for 0% -> 0% of each run, Pallas kernels for 26% -> 28%
where the time goes in v3:
time: 50.1 us; the launch traced here: 49.9 us
  starting transfers between devices  20.6 us (41%)
  Pallas kernels  16.9 us (34%)
  waiting for transfers between devices  9.48 us (19%)
  other arithmetic  1.3 us (3%)
  between operations  0.98 us (2%)
  local copies, waits for them, and re-layouts  0.67 us (1%)
    ppermute x15, starting transfers between devices, from_partners(): lax.ppermute(blocks[k], 'row', [(i, i ^ k) for i in range(PARTS)])  20.6 us
    ppermute x15, waiting for transfers between devices, from_partners(): lax.ppermute(blocks[k], 'row', [(i, i ^ k) for i in range(PARTS)])  9.48 us
    pallas_call x2, Pallas kernels, reconstruct(): call(functools.partial(middle_kernel, c), [f32(2 * COLS[c], 2 * ROWS)] *...  5.23 us
    pallas_call x1, Pallas kernels, reconstruct(): call(weights_kernel, [f32(5, 2, COLS[c], PIX) for c in CHUNKS], [smem()]...  3.47 us
    pallas_call x1, Pallas kernels, reconstruct(): call(phase_kernel, [bf16(PHASES, ROWS, PIX), f32(4, ROWS, PIX), f32(4, 8,...  2.07 us
    pallas_call x1, Pallas kernels, reconstruct(): call(forward_kernel, [blocks[0]] * PARTS + [bf16(5 * ROWS, PIX)] * 2, [sm...  1.53 us
    pallas_call x1, Pallas kernels, reconstruct(): call(final_kernel, f32(2 * ROWS, GRID), [vmem()] * 7, hbm(), [pltpu.VMEM(...  1.52 us
    reduce_sum x1, other arithmetic, reconstruct(): sums = jnp.sum(frames.astype(jnp.float32), axis=(2, 3))  1.3 us
  transfers between devices with their start and end apart: 15, of which 4 were waited for; matrix products, arithmetic and copies ran while one was open for 0% of the time, Pallas kernels for 28%

profile of v3, /device:TPU:1, one launch (start us, length us, event | category | flops | bytes accessed | tf_op | source)
XLA Modules:
  0.0 49.9 jit_solution(14898916754967474088)
XLA Ops:
  0.0 1.3 %convert_reduce_fusion = f32[5]{0:T(128)S(1)} fusion(bf16[1,5,128,512]{3,2,1,0:T(8,128)(2,1)} %source.1), kind=kLoop, calls=%fused_computation | loop fusion | flops 655355 | bytes 655380 | tf_op jit(solution)/shard_map/reduce_sum | solution.py:447
  1.3 4.3 %collective-permute-start.2 = (f32[1,5]{1,0:T(1,128)S(1)}, f32[1,5]{1,0:T(1,128)S(1)}, u32[]{:S(2)}, u32[]{:S(2)}) collective-permute-start(f32[1,5]{1,0:T(1,128)S(1)} %bitcast.6), channel_id=1, source_target_pairs={{0,3},{1,2},{2,1},{3,0},{4,7},{5,6},{6,5},{7,4},{8,11},{9,10},{10,... | collective-permute-start | bytes 68 | tf_op jit(solution)/shard_map/ppermute | solution.py:437
  5.6 1.8 %collective-permute-start.1 = (f32[1,5]{1,0:T(1,128)S(1)}, f32[1,5]{1,0:T(1,128)S(1)}, u32[]{:S(2)}, u32[]{:S(2)}) collective-permute-start(f32[1,5]{1,0:T(1,128)S(1)} %bitcast.7), channel_id=1, source_target_pairs={{0,2},{1,3},{2,0},{3,1},{4,6},{5,7},{6,4},{7,5},{8,10},{9,11},{10,... | collective-permute-start | bytes 68 | tf_op jit(solution)/shard_map/ppermute | solution.py:437
  7.4 0.0 collective-permute-start
  8.1 0.0 copy-start.2
  8.1 0.6 %copy-done.2 = s32[1,2]{1,0:T(1,128)S(1)} copy-done((s32[1,2]{1,0:T(1,128)S(1)}, s32[1,2]{1,0:T(1,128)}, u32[]{:S(2)}) %copy-start.2) | copy-done | bytes 32
  8.7 2.1 %shard_map.73 = (bf16[5,128,512]{2,1,0:T(8,128)(2,1)S(1)}, f32[4,128,512]{2,1,0:T(8,128)S(1)}, f32[4,8,128]{2,1,0:T(8,128)S(1)}, bf16[4,2,128,512]{3,2,1,0:T(8,1...) custom-call(s32[1]{0:T(128)} %bitcast.place, ...), custom_call_target="tpu_custom_call" | custom-call | tf_op jit(solution)/shard_map/pallas_call | solution.py:449
  10.8 0.0 collective-permute-done.2.sums3
  10.8 0.0 collective-permute-done.1.sums2
  10.8 0.0 collective-permute-done.sums1
  10.8 1.5 %shard_map.74 = (f32[5,80,128]{2,1,0:T(8,128)S(1)}, f32[5,80,128]{2,1,0:T(8,128)S(1)}, f32[5,80,128]{2,1,0:T(8,128)S(1)}, f32[5,80,128]{2,1,0:T(8,128)S(1)}, bf1...) custom-call(s32[1]{0:T(128)} %bitcast.place, f32[1,5]{1,0:T(1,128)S(1)} %bitcast.9, ...), custom_call_target="tpu_custom_call" | custom-call | tf_op jit(solution)/shard_map/pallas_call | solution.py:464
  12.4 0.0 copy-start.3
  12.4 0.0 copy-start.1
  12.4 0.6 %collective-permute-start.9 = (f32[5,80,128]{2,1,0:T(8,128)S(1)}, f32[5,80,128]{2,1,0:T(8,128)S(1)}, u32[]{:S(2)}, u32[]{:S(2)}) collective-permute-start(f32[5,80,128]{2,1,0:T(8,128)S(1)} %get-tuple-element.61), channel_id=1, source_target_pairs={{0,1},{1,0},{2,3},{3,2},{4,5},{5,4},{6,7},{7,6},{8,9},{9,8},{10,11... | collective-permute-start | bytes 614408 | tf_op jit(solution)/shard_map/ppermute | solution.py:437
  13.0 1.2 %collective-permute-start.10 = (f32[5,80,128]{2,1,0:T(8,128)S(1)}, f32[5,80,128]{2,1,0:T(8,128)S(1)}, u32[]{:S(2)}, u32[]{:S(2)}) collective-permute-start(f32[5,80,128]{2,1,0:T(8,128)S(1)} %get-tuple-element.62), channel_id=1, source_target_pairs={{0,2},{1,3},{2,0},{3,1},{4,6},{5,7},{6,4},{7,5},{8,10},{9,11},{10,... | collective-permute-start | bytes 614408 | tf_op jit(solution)/shard_map/ppermute | solution.py:437
  14.2 2.0 %collective-permute-start.11 = (f32[5,80,128]{2,1,0:T(8,128)S(1)}, f32[5,80,128]{2,1,0:T(8,128)S(1)}, u32[]{:S(2)}, u32[]{:S(2)}) collective-permute-start(f32[5,80,128]{2,1,0:T(8,128)S(1)} %get-tuple-element.63), channel_id=1, source_target_pairs={{0,3},{1,2},{2,1},{3,0},{4,7},{5,6},{6,5},{7,4},{8,11},{9,10},{10,... | collective-permute-start | bytes 614408 | tf_op jit(solution)/shard_map/ppermute | solution.py:437
  16.2 0.8 %shard_map.75 = (f32[5,48,128]{2,1,0:T(8,128)S(1)}, f32[5,48,128]{2,1,0:T(8,128)S(1)}, f32[5,48,128]{2,1,0:T(8,128)S(1)}, f32[5,48,128]{2,1,0:T(8,128)S(1)}) custom-call(s32[1]{0:T(128)} %bitcast.place, bf16[640,512]{1,0:T(8,128)(2,1)S(1)} %get-tuple-element.43.band_hi, bf16[640,512]{1,0:T(8,128)(2,1)S(1)} %get-tuple-element.44.band_lo, ...), custom_call_target="tpu_custom_call" | custom-call | tf_op jit(solution)/shard_map/pallas_call | solution.py:470
  17.0 0.2 collective-permute-start.3
  17.2 0.0 copy-done.3
  17.2 3.5 %shard_map.76 = (f32[5,2,80,512]{3,2,1,0:T(8,128)S(1)}, f32[5,2,32,512]{3,2,1,0:T(8,128)S(1)}) custom-call(s32[1]{0:T(128)} %bitcast.place, f32[5]{0:T(128)S(1)} %bitcast.10, s32[2]{0:T(128)S(1)} %bitcast.5, f32[5,48,128]{2,1,0:T(8,128)S(1)} %get-tuple-element.47.after.got0), custom_call_target="tpu_custom_call" | custom-call | tf_op jit(solution)/shard_map/pallas_call | solution.py:474
  20.7 0.0 collective-permute-done.9.got1
  20.7 0.3 collective-permute-done.10.got2
  21.0 4.7 %collective-permute-done.11.got3 = f32[5,80,128]{2,1,0:T(8,128)S(1)} collective-permute-done((f32[5,80,128]{2,1,0:T(8,128)S(1)}, f32[5,80,128]{2,1,0:T(8,128)S(1)}, u32[]{:S(2)}, u32[]{:S(2)}) %collective-permute-start.11) | collective-permute-done | bytes 204832 | tf_op jit(solution)/shard_map/ppermute | solution.py:437
  25.7 0.0 copy-done.1
  25.7 2.9 %shard_map.79 = (f32[160,256]{1,0:T(8,128)S(1)}, f32[160,256]{1,0:T(8,128)S(1)}, f32[160,256]{1,0:T(8,128)S(1)}, f32[160,256]{1,0:T(8,128)S(1)}) custom-call(s32[1]{0:T(128)} %bitcast.place, f32[5,80,128]{2,1,0:T(8,128)S(1)} %get-tuple-element.60.got0, f32[5,80,128]{2,1,0:T(8,128)S(1)} %collective-permute-done.9.got1, ...), custom_call_target="tpu_custom_call" | custom-call | tf_op jit(solution)/shard_map/pallas_call | solution.py:487
  28.6 0.2 collective-permute-start.12
  28.8 1.2 %collective-permute-start.4 = (f32[5,48,128]{2,1,0:T(8,128)S(1)}, f32[5,48,128]{2,1,0:T(8,128)S(1)}, u32[]{:S(2)}, u32[]{:S(2)}) collective-permute-start(f32[5,48,128]{2,1,0:T(8,128)S(1)} %get-tuple-element.49), channel_id=1, source_target_pairs={{0,2},{1,3},{2,0},{3,1},{4,6},{5,7},{6,4},{7,5},{8,10},{9,11},{10,... | collective-permute-start | bytes 368648 | tf_op jit(solution)/shard_map/ppermute | solution.py:437
  30.0 2.3 %collective-permute-start.5 = (f32[5,48,128]{2,1,0:T(8,128)S(1)}, f32[5,48,128]{2,1,0:T(8,128)S(1)}, u32[]{:S(2)}, u32[]{:S(2)}) collective-permute-start(f32[5,48,128]{2,1,0:T(8,128)S(1)} %get-tuple-element.50), channel_id=1, source_target_pairs={{0,3},{1,2},{2,1},{3,0},{4,7},{5,6},{6,5},{7,4},{8,11},{9,10},{10,... | collective-permute-start | bytes 368648 | tf_op jit(solution)/shard_map/ppermute | solution.py:437
  32.3 1.2 %collective-permute-start.13 = (f32[160,256]{1,0:T(8,128)S(1)}, f32[160,256]{1,0:T(8,128)S(1)}, u32[]{:S(2)}, u32[]{:S(2)}) collective-permute-start(f32[160,256]{1,0:T(8,128)S(1)} %get-tuple-element.67), channel_id=1, source_target_pairs={{0,2},{1,3},{2,0},{3,1},{4,6},{5,7},{6,4},{7,5},{8,10},{9,11},{10,... | collective-permute-start | bytes 491528 | tf_op jit(solution)/shard_map/ppermute | solution.py:437
  33.5 0.0 collective-permute-done.3.got1
  33.6 1.8 %collective-permute-start.14 = (f32[160,256]{1,0:T(8,128)S(1)}, f32[160,256]{1,0:T(8,128)S(1)}, u32[]{:S(2)}, u32[]{:S(2)}) collective-permute-start(f32[160,256]{1,0:T(8,128)S(1)} %get-tuple-element.68), channel_id=1, source_target_pairs={{0,3},{1,2},{2,1},{3,0},{4,7},{5,6},{6,5},{7,4},{8,11},{9,10},{10,... | collective-permute-start | bytes 491528 | tf_op jit(solution)/shard_map/ppermute | solution.py:437
  35.3 0.0 collective-permute-done.4.got2
  35.3 3.5 %collective-permute-done.5.got3 = f32[5,48,128]{2,1,0:T(8,128)S(1)} collective-permute-done((f32[5,48,128]{2,1,0:T(8,128)S(1)}, f32[5,48,128]{2,1,0:T(8,128)S(1)}, u32[]{:S(2)}, u32[]{:S(2)}) %collective-permute-start.5) | collective-permute-done | bytes 122912 | tf_op jit(solution)/shard_map/ppermute | solution.py:437
  38.8 0.0 copy-start
  38.8 2.3 %shard_map.77 = (f32[64,256]{1,0:T(8,128)S(1)}, f32[64,256]{1,0:T(8,128)S(1)}, f32[64,256]{1,0:T(8,128)S(1)}, f32[64,256]{1,0:T(8,128)S(1)}) custom-call(s32[1]{0:T(128)} %bitcast.place, f32[5,48,128]{2,1,0:T(8,128)S(1)} %get-tuple-element.47.after.got0, f32[5,48,128]{2,1,0:T(8,128)S(1)} %collective-permute-done.3.got1, ...), custom_call_target="tpu_custom_call" | custom-call | tf_op jit(solution)/shard_map/pallas_call | solution.py:487
  41.2 0.1 collective-permute-start.6
  41.3 0.7 %collective-permute-start.7 = (f32[64,256]{1,0:T(8,128)S(1)}, f32[64,256]{1,0:T(8,128)S(1)}, u32[]{:S(2)}, u32[]{:S(2)}) collective-permute-start(f32[64,256]{1,0:T(8,128)S(1)} %get-tuple-element.56), channel_id=1, source_target_pairs={{0,2},{1,3},{2,0},{3,1},{4,6},{5,7},{6,4},{7,5},{8,10},{9,11},{10,... | collective-permute-start | bytes 196616 | tf_op jit(solution)/shard_map/ppermute | solution.py:437
  42.0 0.0 collective-permute-done.12.got1
  42.0 2.9 %collective-permute-start.8 = (f32[64,256]{1,0:T(8,128)S(1)}, f32[64,256]{1,0:T(8,128)S(1)}, u32[]{:S(2)}, u32[]{:S(2)}) collective-permute-start(f32[64,256]{1,0:T(8,128)S(1)} %get-tuple-element.57), channel_id=1, source_target_pairs={{0,3},{1,2},{2,1},{3,0},{4,7},{5,6},{6,5},{7,4},{8,11},{9,10},{10,... | collective-permute-start | bytes 196616 | tf_op jit(solution)/shard_map/ppermute | solution.py:437
  44.9 0.0 copy-done
  44.9 1.0 %shard_map.78 = (bf16[640,1024]{1,0:T(8,128)(2,1)S(1)}, bf16[256,1024]{1,0:T(8,128)(2,1)S(1)}, bf16[640,1024]{1,0:T(8,128)(2,1)S(1)}, bf16[256,1024]{1,0:T(8,128)(2,1)S(1)}) custom-call(s32[1]{0:T(128)} %bitcast.place, f32[4,2,112,128]{3,2,1,0:T(8,128)S(1)} %copy-done, f32[5,48,128]{2,1,0:T(8,128)S(1)} %get-tuple-element.47.after.got0), custom_call_target="tpu_custom_call" | custom-call | tf_op jit(solution)/shard_map/pallas_call | solution.py:480
  45.9 0.0 collective-permute-done.13.got2
  45.9 0.0 collective-permute-done.14.got3
  45.9 1.3 %shard_map.80.part = f32[256,1024]{1,0:T(8,128)S(1)} custom-call(f32[160,256]{1,0:T(8,128)S(1)} %get-tuple-element.65.got0, f32[160,256]{1,0:T(8,128)S(1)} %collective-permute-done.12.got1, f32[160,256]{1,0:T(8,128)S(1)} %collective-permute-done.13.got2, f32[160,256]{1,0:T(8,128)S(1)} %collective-permute-done.14.got3, ...), custom_call_target="tpu_custom_call" | custom-call | tf_op jit(solution)/shard_map/pallas_call | solution.py:493
  47.2 0.0 collective-permute-done.6.got1
  47.3 0.0 collective-permute-done.7.got2
  47.3 1.0 %collective-permute-done.8.got3 = f32[64,256]{1,0:T(8,128)S(1)} collective-permute-done((f32[64,256]{1,0:T(8,128)S(1)}, f32[64,256]{1,0:T(8,128)S(1)}, u32[]{:S(2)}, u32[]{:S(2)}) %collective-permute-start.8) | collective-permute-done | bytes 65568 | tf_op jit(solution)/shard_map/ppermute | solution.py:437
  48.2 1.5 %shard_map.81 = f32[256,1024]{1,0:T(8,128)} custom-call(f32[64,256]{1,0:T(8,128)S(1)} %get-tuple-element.54.got0, f32[64,256]{1,0:T(8,128)S(1)} %collective-permute-done.6.got1, f32[64,256]{1,0:T(8,128)S(1)} %collective-permute-done.7.got2, f32[64,256]{1,0:T(8,128)S(1)} %collective-permute-done.8.got3, bf16[256,1024]{1,0:T(8,128)(2,1)S(1)} %get-tuple-element.58.final_hi, ...), custom_call_target="tpu_custom_call" | custom-call | tf_op jit(solution)/shard_map/pallas_call | solution.py:494
Async XLA Ops:
  1.3 9.5 %collective-permute-start.2 = (f32[1,5]{1,0:T(1,128)S(1)}, f32[1,5]{1,0:T(1,128)S(1)}, u32[]{:S(2)}, u32[]{:S(2)}) collective-permute-start(f32[1,5]{1,0:T(1,128)S(1)} %bitcast.6), channel_id=1, source_target_pairs={{0,3},{1,2},{2,1},{3,0},{4,7},{5,6},{6,5},{7,4},{8,11},{9,10},{10,... | collective-permute-start | bytes 68 | tf_op jit(solution)/shard_map/ppermute | solution.py:437
  5.6 5.2 %collective-permute-start.1 = (f32[1,5]{1,0:T(1,128)S(1)}, f32[1,5]{1,0:T(1,128)S(1)}, u32[]{:S(2)}, u32[]{:S(2)}) collective-permute-start(f32[1,5]{1,0:T(1,128)S(1)} %bitcast.7), channel_id=1, source_target_pairs={{0,2},{1,3},{2,0},{3,1},{4,6},{5,7},{6,4},{7,5},{8,10},{9,11},{10,... | collective-permute-start | bytes 68 | tf_op jit(solution)/shard_map/ppermute | solution.py:437
  7.4 3.4 %collective-permute-start = (f32[1,5]{1,0:T(1,128)S(1)}, f32[1,5]{1,0:T(1,128)S(1)}, u32[]{:S(2)}, u32[]{:S(2)}) collective-permute-start(f32[1,5]{1,0:T(1,128)S(1)} %bitcast.8), channel_id=1, source_target_pairs={{0,1},{1,0},{2,3},{3,2},{4,5},{5,4},{6,7},{7,6},{8,9},{9,8},{10,11... | collective-permute-start | bytes 68 | tf_op jit(solution)/shard_map/ppermute | solution.py:437
  8.1 0.7 %copy-start.2 = (s32[1,2]{1,0:T(1,128)S(1)}, s32[1,2]{1,0:T(1,128)}, u32[]{:S(2)}) copy-start(s32[1,2]{1,0:T(1,128)} %param.10) | copy-start | bytes 28
  12.4 4.9 %copy-start.3 = (f32[1,5]{1,0:T(1,128)S(1)}, f32[1,5]{1,0:T(1,128)}, u32[]{:S(2)}) copy-start(f32[1,5]{1,0:T(1,128)} %param.9) | copy-start | bytes 64
  12.4 13.3 %copy-start.1 = (f32[2,512]{1,0:T(2,128)S(1)}, f32[2,512]{1,0:T(2,128)}, u32[]{:S(2)}) copy-start(f32[2,512]{1,0:T(2,128)} %constant.14.clone.odd) | copy-start | bytes 12292
  12.4 8.3 %collective-permute-start.9 = (f32[5,80,128]{2,1,0:T(8,128)S(1)}, f32[5,80,128]{2,1,0:T(8,128)S(1)}, u32[]{:S(2)}, u32[]{:S(2)}) collective-permute-start(f32[5,80,128]{2,1,0:T(8,128)S(1)} %get-tuple-element.61), channel_id=1, source_target_pairs={{0,1},{1,0},{2,3},{3,2},{4,5},{5,4},{6,7},{7,6},{8,9},{9,8},{10,11... | collective-permute-start | bytes 614408 | tf_op jit(solution)/shard_map/ppermute | solution.py:437
  13.0 8.0 %collective-permute-start.10 = (f32[5,80,128]{2,1,0:T(8,128)S(1)}, f32[5,80,128]{2,1,0:T(8,128)S(1)}, u32[]{:S(2)}, u32[]{:S(2)}) collective-permute-start(f32[5,80,128]{2,1,0:T(8,128)S(1)} %get-tuple-element.62), channel_id=1, source_target_pairs={{0,2},{1,3},{2,0},{3,1},{4,6},{5,7},{6,4},{7,5},{8,10},{9,11},{10,... | collective-permute-start | bytes 614408 | tf_op jit(solution)/shard_map/ppermute | solution.py:437
  14.2 11.5 %collective-permute-start.11 = (f32[5,80,128]{2,1,0:T(8,128)S(1)}, f32[5,80,128]{2,1,0:T(8,128)S(1)}, u32[]{:S(2)}, u32[]{:S(2)}) collective-permute-start(f32[5,80,128]{2,1,0:T(8,128)S(1)} %get-tuple-element.63), channel_id=1, source_target_pairs={{0,3},{1,2},{2,1},{3,0},{4,7},{5,6},{6,5},{7,4},{8,11},{9,10},{10,... | collective-permute-start | bytes 614408 | tf_op jit(solution)/shard_map/ppermute | solution.py:437
  17.0 16.5 %collective-permute-start.3 = (f32[5,48,128]{2,1,0:T(8,128)S(1)}, f32[5,48,128]{2,1,0:T(8,128)S(1)}, u32[]{:S(2)}, u32[]{:S(2)}) collective-permute-start(f32[5,48,128]{2,1,0:T(8,128)S(1)} %get-tuple-element.48), channel_id=1, source_target_pairs={{0,1},{1,0},{2,3},{3,2},{4,5},{5,4},{6,7},{7,6},{8,9},{9,8},{10,11... | collective-permute-start | bytes 368648 | tf_op jit(solution)/shard_map/ppermute | solution.py:437
  28.6 13.4 %collective-permute-start.12 = (f32[160,256]{1,0:T(8,128)S(1)}, f32[160,256]{1,0:T(8,128)S(1)}, u32[]{:S(2)}, u32[]{:S(2)}) collective-permute-start(f32[160,256]{1,0:T(8,128)S(1)} %get-tuple-element.66), channel_id=1, source_target_pairs={{0,1},{1,0},{2,3},{3,2},{4,5},{5,4},{6,7},{7,6},{8,9},{9,8},{10,11... | collective-permute-start | bytes 491528 | tf_op jit(solution)/shard_map/ppermute | solution.py:437
  28.8 6.5 %collective-permute-start.4 = (f32[5,48,128]{2,1,0:T(8,128)S(1)}, f32[5,48,128]{2,1,0:T(8,128)S(1)}, u32[]{:S(2)}, u32[]{:S(2)}) collective-permute-start(f32[5,48,128]{2,1,0:T(8,128)S(1)} %get-tuple-element.49), channel_id=1, source_target_pairs={{0,2},{1,3},{2,0},{3,1},{4,6},{5,7},{6,4},{7,5},{8,10},{9,11},{10,... | collective-permute-start | bytes 368648 | tf_op jit(solution)/shard_map/ppermute | solution.py:437
  30.0 8.8 %collective-permute-start.5 = (f32[5,48,128]{2,1,0:T(8,128)S(1)}, f32[5,48,128]{2,1,0:T(8,128)S(1)}, u32[]{:S(2)}, u32[]{:S(2)}) collective-permute-start(f32[5,48,128]{2,1,0:T(8,128)S(1)} %get-tuple-element.50), channel_id=1, source_target_pairs={{0,3},{1,2},{2,1},{3,0},{4,7},{5,6},{6,5},{7,4},{8,11},{9,10},{10,... | collective-permute-start | bytes 368648 | tf_op jit(solution)/shard_map/ppermute | solution.py:437
  32.3 13.6 %collective-permute-start.13 = (f32[160,256]{1,0:T(8,128)S(1)}, f32[160,256]{1,0:T(8,128)S(1)}, u32[]{:S(2)}, u32[]{:S(2)}) collective-permute-start(f32[160,256]{1,0:T(8,128)S(1)} %get-tuple-element.67), channel_id=1, source_target_pairs={{0,2},{1,3},{2,0},{3,1},{4,6},{5,7},{6,4},{7,5},{8,10},{9,11},{10,... | collective-permute-start | bytes 491528 | tf_op jit(solution)/shard_map/ppermute | solution.py:437
  33.6 12.4 %collective-permute-start.14 = (f32[160,256]{1,0:T(8,128)S(1)}, f32[160,256]{1,0:T(8,128)S(1)}, u32[]{:S(2)}, u32[]{:S(2)}) collective-permute-start(f32[160,256]{1,0:T(8,128)S(1)} %get-tuple-element.68), channel_id=1, source_target_pairs={{0,3},{1,2},{2,1},{3,0},{4,7},{5,6},{6,5},{7,4},{8,11},{9,10},{10,... | collective-permute-start | bytes 491528 | tf_op jit(solution)/shard_map/ppermute | solution.py:437
  38.8 6.1 %copy-start = (f32[4,2,112,128]{3,2,1,0:T(8,128)S(1)}, f32[4,2,112,128]{3,2,1,0:T(8,128)}, u32[]{:S(2)}) copy-start(f32[4,2,112,128]{3,2,1,0:T(8,128)} %constant.13.clone.first) | copy-start | bytes 1376260
  41.2 6.1 %collective-permute-start.6 = (f32[64,256]{1,0:T(8,128)S(1)}, f32[64,256]{1,0:T(8,128)S(1)}, u32[]{:S(2)}, u32[]{:S(2)}) collective-permute-start(f32[64,256]{1,0:T(8,128)S(1)} %get-tuple-element.55), channel_id=1, source_target_pairs={{0,1},{1,0},{2,3},{3,2},{4,5},{5,4},{6,7},{7,6},{8,9},{9,8},{10,11... | collective-permute-start | bytes 196616 | tf_op jit(solution)/shard_map/ppermute | solution.py:437
  41.3 6.0 %collective-permute-start.7 = (f32[64,256]{1,0:T(8,128)S(1)}, f32[64,256]{1,0:T(8,128)S(1)}, u32[]{:S(2)}, u32[]{:S(2)}) collective-permute-start(f32[64,256]{1,0:T(8,128)S(1)} %get-tuple-element.56), channel_id=1, source_target_pairs={{0,2},{1,3},{2,0},{3,1},{4,6},{5,7},{6,4},{7,5},{8,10},{9,11},{10,... | collective-permute-start | bytes 196616 | tf_op jit(solution)/shard_map/ppermute | solution.py:437
  42.0 6.2 %collective-permute-start.8 = (f32[64,256]{1,0:T(8,128)S(1)}, f32[64,256]{1,0:T(8,128)S(1)}, u32[]{:S(2)}, u32[]{:S(2)}) collective-permute-start(f32[64,256]{1,0:T(8,128)S(1)} %get-tuple-element.57), channel_id=1, source_target_pairs={{0,3},{1,2},{2,1},{3,0},{4,7},{5,6},{6,5},{7,4},{8,11},{9,10},{10,... | collective-permute-start | bytes 196616 | tf_op jit(solution)/shard_map/ppermute | solution.py:437

commit v4 on v3

--- a/solution.py
+++ b/solution.py
@@ -91,27 +91,15 @@
     return jnp.cos(angle), jnp.sin(angle)
 
 
-def phase_kernel(place, shift, offset, source, base_far, frames, turns, phases, *rest):
-    y_out, x_out, base, sems = rest[0:2], (rest[2:4], rest[4:6]), rest[6], rest[7]
+def phase_kernel(place, offset, shift_far, source, base_far, frames, turns, phases, *rest):
+    y_out, x_out, (base, shift, sems) = rest[0:2], (rest[2:4], rest[4:6]), rest[6:]
     base_copy = pltpu.make_async_copy(base_far, base, sems.at[0])
     base_copy.start()
-    copy = pltpu.make_async_copy(source.at[0], frames, sems.at[1])
+    shift_copy = pltpu.make_async_copy(shift_far, shift, sems.at[1])
+    shift_copy.start()
+    copy = pltpu.make_async_copy(source.at[0], frames, sems.at[2])
     copy.start()
     rank = place[0]
-    shift_y = shift[0]
-    shift_x = shift[1]
-    x_cos, x_sin = turn_pair(lax.broadcasted_iota(jnp.int32, (8, PIX), 1) * shift_x)
-    row_at = lax.broadcasted_iota(jnp.int32, (ROWS, 128), 0) + rank * ROWS
-    y_cos, y_sin = turn_pair(row_at * shift_y)
-    x_cos, x_sin = x_cos[:1], x_sin[:1]
-    y_cos = jnp.concatenate([y_cos] * 4, axis=1)
-    y_sin = jnp.concatenate([y_sin] * 4, axis=1)
-    turn_re = x_cos * y_cos - x_sin * y_sin
-    turn_im = x_cos * y_sin + x_sin * y_cos
-    turns[0] = turn_re
-    turns[1] = turn_im
-    turns[2] = turn_re * turn_re - turn_im * turn_im
-    turns[3] = 2.0 * turn_re * turn_im
     phase_at = lax.broadcasted_iota(jnp.int32, (8, 128), 0).astype(jnp.float32)
     phase_at = (2.0 * math.pi / PHASES) * phase_at + offset[0]
     phases[0] = jnp.cos(phase_at)
@@ -152,24 +140,36 @@
                             piece = jnp.where(top, lone, piece)
                         pieces.append(piece)
                 x_out[chunk][part][d] = jnp.concatenate(pieces, axis=0).astype(jnp.bfloat16)
+    shift_copy.wait()
+    shift_y, shift_x = shift[0:1, 0:1], shift[0:1, 1:2]
+    x_cos, x_sin = turn_pair(lax.broadcasted_iota(jnp.int32, (8, PIX), 1) * shift_x)
+    row_at = lax.broadcasted_iota(jnp.int32, (ROWS, 128), 0) + rank * ROWS
+    y_cos, y_sin = turn_pair(row_at * shift_y)
+    x_cos, x_sin = x_cos[:1], x_sin[:1]
+    y_cos = jnp.concatenate([y_cos] * 4, axis=1)
+    y_sin = jnp.concatenate([y_sin] * 4, axis=1)
+    turn_re = x_cos * y_cos - x_sin * y_sin
+    turn_im = x_cos * y_sin + x_sin * y_cos
+    turns[0] = turn_re
+    turns[1] = turn_im
+    turns[2] = turn_re * turn_re - turn_im * turn_im
+    turns[3] = 2.0 * turn_re * turn_im
     copy.wait()
 
 
-def spectra_rows(rank, rows, band, x_hi, x_lo, outs):
+def spectra_rows(rank, rows, partners, band, x_hi, x_lo, outs):
     table = (
-        jnp.concatenate([x_hi[rank ^ k] for k in range(PARTS)], axis=0),
-        jnp.concatenate([x_lo[rank ^ k] for k in range(PARTS)], axis=0),
+        jnp.concatenate([x_hi[rank ^ k] for k in partners], axis=0),
+        jnp.concatenate([x_lo[rank ^ k] for k in partners], axis=0),
     )
     spectra = dot3(table, band, (1, 1))
-    for k in range(PARTS):
+    for k, out in enumerate(outs):
         for plane in range(5):
-            outs[k][plane] = spectra[
-                k * rows : (k + 1) * rows, plane * ROWS : (plane + 1) * ROWS
-            ]
+            out[plane] = spectra[k * rows : (k + 1) * rows, plane * ROWS : (plane + 1) * ROWS]
 
 
 def forward_kernel(place, sums0, sums1, sums2, sums3, turns, phases, frames, x_hi, x_lo, *rest):
-    outs, (band_hi, band_lo) = rest[:PARTS], rest[PARTS:]
+    outs, (band_hi, band_lo) = rest[:2], rest[2:]
     total = (sums0[...] + sums1[...]) + (sums2[...] + sums3[...])
     weight_all = (PIX * PIX / PHASES) / total
     acc = None
@@ -192,36 +192,43 @@
         hi, lo = split(plane)
         band_hi[index * ROWS : (index + 1) * ROWS, :] = hi
         band_lo[index * ROWS : (index + 1) * ROWS, :] = lo
-    spectra_rows(place[0], 2 * MAIN[0], (band_hi[...], band_lo[...]), x_hi, x_lo, outs)
-
-
-def forward_rest_kernel(place, band_hi, band_lo, x_hi, x_lo, *outs):
-    spectra_rows(place[0], 2 * MAIN[1], (band_hi[...], band_lo[...]), x_hi, x_lo, outs)
+    band = (band_hi[...], band_lo[...])
+    spectra_rows(place[0], 2 * MAIN[0], (2, 3), band, x_hi, x_lo, outs)
+
+
+def forward_rest_kernel(place, band_hi, band_lo, x_hi0, x_lo0, x_hi1, x_lo1, *outs):
+    band = (band_hi[...], band_lo[...])
+    spectra_rows(place[0], 2 * MAIN[1], (0, 1, 2, 3), band, x_hi1, x_lo1, outs[2:])
+    spectra_rows(place[0], 2 * MAIN[0], (0, 1), band, x_hi0, x_lo0, outs[:2])
+
+
+def root(value):
+    return value * lax.rsqrt(jnp.maximum(value, 1e-30))
 
 
 def transfer_curve(squared):
-    radius = jnp.minimum(jnp.sqrt(squared * (1.0 / (cut_share * PIX) ** 2)), 1.0)
-    arc = jnp.full_like(radius, ARC[7])
+    radius = jnp.minimum(root(squared), 1.0)
+    arc = jnp.full_like(radius, 2.0 / math.pi * ARC[7])
     for coefficient in ARC[6::-1]:
-        arc = arc * radius + coefficient
-    return (2.0 / math.pi) * jnp.sqrt(1.0 - radius) * (arc - radius * jnp.sqrt(1.0 + radius))
-
-
-def weights_kernel(place, gains, shift, after, weights0, weights1, y_square, y_low):
-    weights = (weights0, weights1)
+        arc = arc * radius + 2.0 / math.pi * coefficient
+    over = 1.0 + radius
+    return root(1.0 - radius) * (arc - (2.0 / math.pi) * radius * (over * lax.rsqrt(over)))
+
+
+def weights_kernel(chunk, place, gains, shift, after, weights, y_square, y_low):
     rank = place[0]
-    shift_y, shift_x = shift[0], shift[1]
-    own = [gains[m + 2] for m in ORDERS]
-    other = [gains[2 - m] for m in ORDERS]
+    shift_y, shift_x = shift[0, 0], shift[0, 1]
+    own = [gains[0, m + 2] for m in ORDERS]
+    other = [gains[0, 2 - m] for m in ORDERS]
     sub = lax.broadcasted_iota(jnp.int32, (8, 1), 0)
     lane = lax.broadcasted_iota(jnp.int32, (8, PIX), 1)
     for order, m in enumerate(ORDERS):
         y = ((lane - m * shift_y + PIX // 2) & (PIX - 1)) - PIX // 2
         y_low[order] = jnp.where(y + m * shift_y >= 0, 1.0, 0.0)
-        y = y.astype(jnp.float32)
+        y = y.astype(jnp.float32) * (1.0 / (cut_share * PIX))
         y_square[order] = y * y
 
-    def tile_step(chunk, tile):
+    def tile_step(tile, carry):
         low = 8 * tile
         folded = low >= MAIN[chunk]
         l = jnp.where(folded, low - MAIN[chunk] + FOLD_LOW[chunk], low + LOW[chunk])
@@ -233,7 +240,7 @@
         dens = [jnp.full((8, PIX), wiener, jnp.float32)] * 4
         curves = []
         for order, m in enumerate(ORDERS):
-            x = (freq_x - m * shift_x).astype(jnp.float32)
+            x = (freq_x - m * shift_x).astype(jnp.float32) * (1.0 / (cut_share * PIX))
             curve = transfer_curve(x * x + y_square[order])
             power = curve * curve
             power_low = power * y_low[order]
@@ -253,13 +260,12 @@
             own_den = jnp.where(is_low, own_low, own_high)
             other_den = jnp.where(is_low, other_low, other_high)
             weight = curves[order] * (own[order] * own_den + other[order] * other_den)
-            weights[chunk][order, 0, rows, :] = weight
-            weights[chunk][order, 1, rows, :] = jnp.where(is_low, weight, -weight)
-
-    for chunk in CHUNKS:
-        lax.fori_loop(
-            0, COLS[chunk] // 8, lambda tile, _, chunk=chunk: (tile_step(chunk, tile), 0)[1], 0
-        )
+            weights[order, 0, rows, :] = weight
+            weights[order, 1, rows, :] = jnp.where(is_low, weight, -weight)
+
+        return carry
+
+    lax.fori_loop(0, COLS[chunk] // 8, tile_step, 0, unroll=2)
 
 
 def table_kernel(place, first, after, hi0, hi1, lo0, lo1):
@@ -440,7 +446,6 @@
 
 def reconstruct(frames, phase_offset, order_gain, band_shift):
     base, first, odd = tables()
-    order_gain, band_shift = order_gain[0], band_shift[0]
     rank = lax.axis_index("row")
     place = rank.reshape(1).astype(jnp.int32)
 
@@ -451,45 +456,52 @@
         [bf16(PHASES, ROWS, PIX), f32(4, ROWS, PIX), f32(4, 8, 128)]
         + [bf16(PARTS, 2, ROWS, PIX)] * 2
         + [bf16(PARTS, 2 * MAIN[c], PIX) for c in CHUNKS for _ in range(2)],
-        [smem()] * 3 + [hbm(), hbm()],
-        scratch=[pltpu.VMEM(base.shape, jnp.bfloat16), pltpu.SemaphoreType.DMA((2,))],
+        [smem()] * 2 + [hbm()] * 3,
+        scratch=[
+            pltpu.VMEM(base.shape, jnp.bfloat16),
+            pltpu.VMEM((1, 2), jnp.int32),
+            pltpu.SemaphoreType.DMA((3,)),
+        ],
     )(
         place,
-        band_shift,
         phase_offset,
+        pltpu.with_memory_space_constraint(band_shift, pltpu.HBM),
         pltpu.with_memory_space_constraint(frames, pltpu.HBM),
         pltpu.with_memory_space_constraint(base, pltpu.HBM),
     )
     blocks = [f32(5, 2 * MAIN[c], ROWS) for c in CHUNKS]
-    *sent, band_hi, band_lo = call(
+    *far, band_hi, band_lo = call(
         forward_kernel,
-        [blocks[0]] * PARTS + [bf16(5 * ROWS, PIX)] * 2,
+        [blocks[0]] * 2 + [bf16(5 * ROWS, PIX)] * 2,
         [smem()] + [vmem()] * 9,
     )(place, *sums, turns, phases, frames, *x_parts[:2])
-    spectra = [from_partners(sent)]
-    sent = call(forward_rest_kernel, [blocks[1]] * PARTS, [smem()] + [vmem()] * 4)(
-        place, band_hi, band_lo, *x_parts[2:]
-    )
-    spectra.append(from_partners(sent))
-    weights = call(
-        weights_kernel,
-        [f32(5, 2, COLS[c], PIX) for c in CHUNKS],
-        [smem()] * 3 + [vmem()],
-        scratch=[pltpu.VMEM((5, 8, PIX), jnp.float32)] * 2,
-    )(place, order_gain, band_shift, sent[0])
+    sent = call(
+        forward_rest_kernel,
+        [blocks[0]] * 2 + [blocks[1]] * PARTS,
+        [smem()] + [vmem()] * 6,
+    )(place, band_hi, band_lo, *x_parts)
+    spectra = [from_partners([*sent[:2], *far]), from_partners(sent[2:])]
+    got = []
+    after = sent[0]
+    for c in CHUNKS:
+        weights = call(
+            functools.partial(weights_kernel, c),
+            f32(5, 2, COLS[c], PIX),
+            [smem()] * 3 + [vmem()],
+            scratch=[pltpu.VMEM((5, 8, PIX), jnp.float32)] * 2,
+        )(place, order_gain, band_shift, after)
+        sent = call(
+            functools.partial(middle_kernel, c),
+            [f32(2 * COLS[c], 2 * ROWS)] * PARTS,
+            [smem()] + [vmem()] * 8,
+        )(place, *spectra[c], weights, y_hi, y_lo, odd)
+        after = sent[0]
+        got.append(from_partners(sent))
     hi0, hi1, lo0, lo1 = call(
         table_kernel,
         [bf16(8 * COLS[c], GRID) for c in CHUNKS] * 2,
         [smem()] + [vmem()] * 2,
-    )(place, first, sent[0])
-    got = []
-    for c in CHUNKS:
-        sent = call(
-            functools.partial(middle_kernel, c),
-            [f32(2 * COLS[c], 2 * ROWS)] * PARTS,
-            [smem()] + [vmem()] * 8,
-        )(place, *spectra[c], weights[c], y_hi, y_lo, odd)
-        got.append(from_partners(sent))
+    )(place, first, after)
     part = call(part_kernel, f32(2 * ROWS, GRID), [vmem()] * 6)(*got[0], hi0, lo0)
     return call(
         final_kernel,

time: 50.1 us -> 50.6 us (level)
  waiting for transfers between devices: 9.48 us -> 10.3 us
  local copies, waits for them, and re-layouts: 0.67 us -> 0.02 us
    ppermute x15, waiting for transfers between devices: 9.48 us -> 10.3 us  [from_partners(): lax.ppermute(blocks[k], 'row', [(i, i ^ k) for i in range(PARTS)])]
    unnamed x8, local copies, waits for them, and re-layouts: 0.67 us -> 0.02 us
    pallas_call x3 -> x4, Pallas kernels: 5.79 us -> 6.11 us  [the longest x2 3.46 us: reconstruct(): call(functools.partial(weights_kernel, c), f32(5, 2, COLS[c], PIX), [smem...]
  transfers between devices with their start and end apart: 15 -> 15, of which waited for: 4 -> 4; matrix products, arithmetic and copies ran while one was open for 0% -> 0% of each run, Pallas kernels for 28% -> 26%
where the time goes in v4:
time: 50.6 us; the launch traced here: 50.5 us
  starting transfers between devices  20.5 us (41%)
  Pallas kernels  17.3 us (34%)
  waiting for transfers between devices  10.3 us (20%)
  other arithmetic  1.3 us (3%)
  between operations  0.99 us (2%)
    ppermute x15, starting transfers between devices, from_partners(): lax.ppermute(blocks[k], 'row', [(i, i ^ k) for i in range(PARTS)])  20.5 us
    ppermute x15, waiting for transfers between devices, from_partners(): lax.ppermute(blocks[k], 'row', [(i, i ^ k) for i in range(PARTS)])  10.3 us
    pallas_call x2, Pallas kernels, reconstruct(): call(functools.partial(middle_kernel, c), [f32(2 * COLS[c], 2 * ROWS)] *...  5.21 us
    pallas_call x2, Pallas kernels, reconstruct(): call(functools.partial(weights_kernel, c), f32(5, 2, COLS[c], PIX), [smem...  3.46 us
    pallas_call x1, Pallas kernels, reconstruct(): call(phase_kernel, [bf16(PHASES, ROWS, PIX), f32(4, ROWS, PIX), f32(4, 8,...  2.15 us
    pallas_call x1, Pallas kernels, reconstruct(): call(final_kernel, f32(2 * ROWS, GRID), [vmem()] * 7, hbm(), [pltpu.VMEM(...  1.51 us
    pallas_call x1, Pallas kernels, reconstruct(): call(forward_rest_kernel, [blocks[0]] * 2 + [blocks[1]] * PARTS, [smem()]...  1.4 us
    pallas_call x1, Pallas kernels, reconstruct(): call(part_kernel, f32(2 * ROWS, GRID), [vmem()] * 6)(*got[0], hi0, lo0)  1.32 us
  transfers between devices with their start and end apart: 15, of which 4 were waited for; matrix products, arithmetic and copies ran while one was open for 0% of the time, Pallas kernels for 26%

profile of v4, /device:TPU:1, one launch (start us, length us, event | category | flops | bytes accessed | tf_op | source)
XLA Modules:
  0.0 50.5 jit_solution(15044881617092014958)
XLA Ops:
  0.0 1.3 %convert_reduce_fusion = f32[5]{0:T(128)S(1)} fusion(bf16[1,5,128,512]{3,2,1,0:T(8,128)(2,1)} %source.1), kind=kLoop, calls=%fused_computation | loop fusion | flops 655355 | bytes 655380 | tf_op jit(solution)/shard_map/reduce_sum | solution.py:452
  1.3 4.3 %collective-permute-start.2 = (f32[1,5]{1,0:T(1,128)S(1)}, f32[1,5]{1,0:T(1,128)S(1)}, u32[]{:S(2)}, u32[]{:S(2)}) collective-permute-start(f32[1,5]{1,0:T(1,128)S(1)} %bitcast.2), channel_id=1, source_target_pairs={{0,3},{1,2},{2,1},{3,0},{4,7},{5,6},{6,5},{7,4},{8,11},{9,10},{10,... | collective-permute-start | bytes 68 | tf_op jit(solution)/shard_map/ppermute | solution.py:443
  5.6 1.8 %collective-permute-start.1 = (f32[1,5]{1,0:T(1,128)S(1)}, f32[1,5]{1,0:T(1,128)S(1)}, u32[]{:S(2)}, u32[]{:S(2)}) collective-permute-start(f32[1,5]{1,0:T(1,128)S(1)} %bitcast.3), channel_id=1, source_target_pairs={{0,2},{1,3},{2,0},{3,1},{4,6},{5,7},{6,4},{7,5},{8,10},{9,11},{10,... | collective-permute-start | bytes 68 | tf_op jit(solution)/shard_map/ppermute | solution.py:443
  7.4 0.0 collective-permute-start
  8.1 2.2 %shard_map.73 = (bf16[5,128,512]{2,1,0:T(8,128)(2,1)S(1)}, f32[4,128,512]{2,1,0:T(8,128)S(1)}, f32[4,8,128]{2,1,0:T(8,128)S(1)}, bf16[4,2,128,512]{3,2,1,0:T(8,1...) custom-call(s32[1]{0:T(128)} %bitcast.place, ...), custom_call_target="tpu_custom_call" | custom-call | tf_op jit(solution)/shard_map/pallas_call | solution.py:454
  10.2 0.0 collective-permute-done.2.sums3
  10.2 0.0 collective-permute-done.1.sums2
  10.2 0.0 collective-permute-done.sums1
  10.3 1.3 %shard_map.74 = (f32[5,80,128]{2,1,0:T(8,128)S(1)}, f32[5,80,128]{2,1,0:T(8,128)S(1)}, bf16[640,512]{1,0:T(8,128)(2,1)S(1)}, bf16[640,512]{1,0:T(8,128)(2,1)S(1)}) custom-call(s32[1]{0:T(128)} %bitcast.place, f32[1,5]{1,0:T(1,128)S(1)} %bitcast.5, f32[1,5]{1,0:T(1,128)S(1)} %collective-permute-done.sums1, f32[1,5]{1,0:T(1,128)S(1)} %collective-permute-done.1.sums2, ...), custom_call_target="tpu_custom_call" | custom-call | tf_op jit(solution)/shard_map/pallas_call | solution.py:473
  11.5 0.0 copy-start.2
  11.5 0.0 copy-start.3
  11.5 1.4 %shard_map.75 = (f32[5,80,128]{2,1,0:T(8,128)S(1)}, f32[5,80,128]{2,1,0:T(8,128)S(1)}, f32[5,48,128]{2,1,0:T(8,128)S(1)}, f32[5,48,128]{2,1,0:T(8,128)S(1)}, f32...) custom-call(s32[1]{0:T(128)} %bitcast.place, bf16[640,512]{1,0:T(8,128)(2,1)S(1)} %get-tuple-element.41.band_hi, ...), custom_call_target="tpu_custom_call" | custom-call | tf_op jit(solution)/shard_map/pallas_call | solution.py:478
  12.9 0.0 copy-start.1
  13.0 0.6 %collective-permute-start.6 = (f32[5,80,128]{2,1,0:T(8,128)S(1)}, f32[5,80,128]{2,1,0:T(8,128)S(1)}, u32[]{:S(2)}, u32[]{:S(2)}) collective-permute-start(f32[5,80,128]{2,1,0:T(8,128)S(1)} %get-tuple-element.50), channel_id=1, source_target_pairs={{0,1},{1,0},{2,3},{3,2},{4,5},{5,4},{6,7},{7,6},{8,9},{9,8},{10,11... | collective-permute-start | bytes 614408 | tf_op jit(solution)/shard_map/ppermute | solution.py:443
  13.6 1.2 %collective-permute-start.7 = (f32[5,80,128]{2,1,0:T(8,128)S(1)}, f32[5,80,128]{2,1,0:T(8,128)S(1)}, u32[]{:S(2)}, u32[]{:S(2)}) collective-permute-start(f32[5,80,128]{2,1,0:T(8,128)S(1)} %get-tuple-element.51), channel_id=1, source_target_pairs={{0,2},{1,3},{2,0},{3,1},{4,6},{5,7},{6,4},{7,5},{8,10},{9,11},{10,... | collective-permute-start | bytes 614408 | tf_op jit(solution)/shard_map/ppermute | solution.py:443
  14.8 2.0 %collective-permute-start.8 = (f32[5,80,128]{2,1,0:T(8,128)S(1)}, f32[5,80,128]{2,1,0:T(8,128)S(1)}, u32[]{:S(2)}, u32[]{:S(2)}) collective-permute-start(f32[5,80,128]{2,1,0:T(8,128)S(1)} %get-tuple-element.52), channel_id=1, source_target_pairs={{0,3},{1,2},{2,1},{3,0},{4,7},{5,6},{6,5},{7,4},{8,11},{9,10},{10,... | collective-permute-start | bytes 614408 | tf_op jit(solution)/shard_map/ppermute | solution.py:443
  16.8 0.1 collective-permute-start.3
  16.9 0.0 copy-done.2
  16.9 0.0 copy-done.3
  16.9 2.2 %shard_map.76.weights = f32[5,2,80,512]{3,2,1,0:T(8,128)S(1)} custom-call(s32[1]{0:T(128)} %bitcast.place, f32[1,5]{1,0:T(1,128)S(1)} %copy-done.3, s32[1,2]{1,0:T(1,128)S(1)} %copy-done.2, f32[5,80,128]{2,1,0:T(8,128)S(1)} %get-tuple-element.49.after.got0), custom_call_target="tpu_custom_call" | custom-call | tf_op jit(solution)/shard_map/pallas_call | solution.py:487
  19.2 0.0 collective-permute-done.6.got1
  19.2 2.4 %collective-permute-done.7.got2 = f32[5,80,128]{2,1,0:T(8,128)S(1)} collective-permute-done((f32[5,80,128]{2,1,0:T(8,128)S(1)}, f32[5,80,128]{2,1,0:T(8,128)S(1)}, u32[]{:S(2)}, u32[]{:S(2)}) %collective-permute-start.7) | collective-permute-done | bytes 204832 | tf_op jit(solution)/shard_map/ppermute | solution.py:443
  21.6 4.7 %collective-permute-done.8.got3 = f32[5,80,128]{2,1,0:T(8,128)S(1)} collective-permute-done((f32[5,80,128]{2,1,0:T(8,128)S(1)}, f32[5,80,128]{2,1,0:T(8,128)S(1)}, u32[]{:S(2)}, u32[]{:S(2)}) %collective-permute-start.8) | collective-permute-done | bytes 204832 | tf_op jit(solution)/shard_map/ppermute | solution.py:443
  26.3 0.0 copy-done.1
  26.3 2.9 %shard_map.77 = (f32[160,256]{1,0:T(8,128)S(1)}, f32[160,256]{1,0:T(8,128)S(1)}, f32[160,256]{1,0:T(8,128)S(1)}, f32[160,256]{1,0:T(8,128)S(1)}) custom-call(s32[1]{0:T(128)} %bitcast.place, f32[5,80,128]{2,1,0:T(8,128)S(1)} %get-tuple-element.49.after.got0, f32[5,80,128]{2,1,0:T(8,128)S(1)} %collective-permute-done.6.got1, ...), custom_call_target="tpu_custom_call" | custom-call | tf_op jit(solution)/shard_map/pallas_call | solution.py:493
  29.2 0.2 collective-permute-start.12
  29.4 1.2 %collective-permute-start.4 = (f32[5,48,128]{2,1,0:T(8,128)S(1)}, f32[5,48,128]{2,1,0:T(8,128)S(1)}, u32[]{:S(2)}, u32[]{:S(2)}) collective-permute-start(f32[5,48,128]{2,1,0:T(8,128)S(1)} %get-tuple-element.47), channel_id=1, source_target_pairs={{0,2},{1,3},{2,0},{3,1},{4,6},{5,7},{6,4},{7,5},{8,10},{9,11},{10,... | collective-permute-start | bytes 368648 | tf_op jit(solution)/shard_map/ppermute | solution.py:443
  30.6 2.3 %collective-permute-start.5 = (f32[5,48,128]{2,1,0:T(8,128)S(1)}, f32[5,48,128]{2,1,0:T(8,128)S(1)}, u32[]{:S(2)}, u32[]{:S(2)}) collective-permute-start(f32[5,48,128]{2,1,0:T(8,128)S(1)} %get-tuple-element.48), channel_id=1, source_target_pairs={{0,3},{1,2},{2,1},{3,0},{4,7},{5,6},{6,5},{7,4},{8,11},{9,10},{10,... | collective-permute-start | bytes 368648 | tf_op jit(solution)/shard_map/ppermute | solution.py:443
  32.9 1.2 %collective-permute-start.13 = (f32[160,256]{1,0:T(8,128)S(1)}, f32[160,256]{1,0:T(8,128)S(1)}, u32[]{:S(2)}, u32[]{:S(2)}) collective-permute-start(f32[160,256]{1,0:T(8,128)S(1)} %get-tuple-element.63), channel_id=1, source_target_pairs={{0,2},{1,3},{2,0},{3,1},{4,6},{5,7},{6,4},{7,5},{8,10},{9,11},{10,... | collective-permute-start | bytes 491528 | tf_op jit(solution)/shard_map/ppermute | solution.py:443
  34.1 0.0 collective-permute-done.3.got1
  34.1 1.8 %collective-permute-start.14 = (f32[160,256]{1,0:T(8,128)S(1)}, f32[160,256]{1,0:T(8,128)S(1)}, u32[]{:S(2)}, u32[]{:S(2)}) collective-permute-start(f32[160,256]{1,0:T(8,128)S(1)} %get-tuple-element.64), channel_id=1, source_target_pairs={{0,3},{1,2},{2,1},{3,0},{4,7},{5,6},{6,5},{7,4},{8,11},{9,10},{10,... | collective-permute-start | bytes 491528 | tf_op jit(solution)/shard_map/ppermute | solution.py:443
  35.9 1.2 %shard_map.78.weights = f32[5,2,32,512]{3,2,1,0:T(8,128)S(1)} custom-call(s32[1]{0:T(128)} %bitcast.place, f32[1,5]{1,0:T(1,128)S(1)} %copy-done.3, s32[1,2]{1,0:T(1,128)S(1)} %copy-done.2, f32[160,256]{1,0:T(8,128)S(1)} %get-tuple-element.55.after.got0), custom_call_target="tpu_custom_call" | custom-call | tf_op jit(solution)/shard_map/pallas_call | solution.py:487
  37.1 0.0 collective-permute-done.4.got2
  37.2 2.3 %collective-permute-done.5.got3 = f32[5,48,128]{2,1,0:T(8,128)S(1)} collective-permute-done((f32[5,48,128]{2,1,0:T(8,128)S(1)}, f32[5,48,128]{2,1,0:T(8,128)S(1)}, u32[]{:S(2)}, u32[]{:S(2)}) %collective-permute-start.5) | collective-permute-done | bytes 122912 | tf_op jit(solution)/shard_map/ppermute | solution.py:443
  39.4 2.3 %shard_map.79 = (f32[64,256]{1,0:T(8,128)S(1)}, f32[64,256]{1,0:T(8,128)S(1)}, f32[64,256]{1,0:T(8,128)S(1)}, f32[64,256]{1,0:T(8,128)S(1)}) custom-call(s32[1]{0:T(128)} %bitcast.place, f32[5,48,128]{2,1,0:T(8,128)S(1)} %get-tuple-element.45.got0, f32[5,48,128]{2,1,0:T(8,128)S(1)} %collective-permute-done.3.got1, ...), custom_call_target="tpu_custom_call" | custom-call | tf_op jit(solution)/shard_map/pallas_call | solution.py:493
  41.7 0.1 collective-permute-start.9
  41.8 0.7 %collective-permute-start.10 = (f32[64,256]{1,0:T(8,128)S(1)}, f32[64,256]{1,0:T(8,128)S(1)}, u32[]{:S(2)}, u32[]{:S(2)}) collective-permute-start(f32[64,256]{1,0:T(8,128)S(1)} %get-tuple-element.58), channel_id=1, source_target_pairs={{0,2},{1,3},{2,0},{3,1},{4,6},{5,7},{6,4},{7,5},{8,10},{9,11},{10,... | collective-permute-start | bytes 196616 | tf_op jit(solution)/shard_map/ppermute | solution.py:443
  42.6 0.0 collective-permute-done.12.got1
  42.6 2.9 %collective-permute-start.11 = (f32[64,256]{1,0:T(8,128)S(1)}, f32[64,256]{1,0:T(8,128)S(1)}, u32[]{:S(2)}, u32[]{:S(2)}) collective-permute-start(f32[64,256]{1,0:T(8,128)S(1)} %get-tuple-element.59), channel_id=1, source_target_pairs={{0,3},{1,2},{2,1},{3,0},{4,7},{5,6},{6,5},{7,4},{8,11},{9,10},{10,... | collective-permute-start | bytes 196616 | tf_op jit(solution)/shard_map/ppermute | solution.py:443
  45.5 0.0 copy-done
  45.5 1.0 %shard_map.80 = (bf16[640,1024]{1,0:T(8,128)(2,1)S(1)}, bf16[256,1024]{1,0:T(8,128)(2,1)S(1)}, bf16[640,1024]{1,0:T(8,128)(2,1)S(1)}, bf16[256,1024]{1,0:T(8,128)(2,1)S(1)}) custom-call(s32[1]{0:T(128)} %bitcast.place, f32[4,2,112,128]{3,2,1,0:T(8,128)S(1)} %copy-done, f32[64,256]{1,0:T(8,128)S(1)} %get-tuple-element.56.after.got0), custom_call_target="tpu_custom_call" | custom-call | tf_op jit(solution)/shard_map/pallas_call | solution.py:500
  46.5 0.0 collective-permute-done.13.got2
  46.5 0.0 collective-permute-done.14.got3
  46.5 1.3 %shard_map.81.part = f32[256,1024]{1,0:T(8,128)S(1)} custom-call(f32[160,256]{1,0:T(8,128)S(1)} %get-tuple-element.55.after.got0, f32[160,256]{1,0:T(8,128)S(1)} %collective-permute-done.12.got1, f32[160,256]{1,0:T(8,128)S(1)} %collective-permute-done.13.got2, f32[160,256]{1,0:T(8,128)S(1)} %collective-permute-done.14.got3, ...), custom_call_target="tpu_custom_call" | custom-call | tf_op jit(solution)/shard_map/pallas_call | solution.py:505
  47.8 0.0 collective-permute-done.9.got1
  47.8 0.0 collective-permute-done.10.got2
  47.9 1.0 %collective-permute-done.11.got3 = f32[64,256]{1,0:T(8,128)S(1)} collective-permute-done((f32[64,256]{1,0:T(8,128)S(1)}, f32[64,256]{1,0:T(8,128)S(1)}, u32[]{:S(2)}, u32[]{:S(2)}) %collective-permute-start.11) | collective-permute-done | bytes 65568 | tf_op jit(solution)/shard_map/ppermute | solution.py:443
  48.8 1.5 %shard_map.82 = f32[256,1024]{1,0:T(8,128)} custom-call(f32[64,256]{1,0:T(8,128)S(1)} %get-tuple-element.56.after.got0, f32[64,256]{1,0:T(8,128)S(1)} %collective-permute-done.9.got1, f32[64,256]{1,0:T(8,128)S(1)} %collective-permute-done.10.got2, f32[64,256]{1,0:T(8,128)S(1)} %collective-permute-done.11.got3, ...), custom_call_target="tpu_custom_call" | custom-call | tf_op jit(solution)/shard_map/pallas_call | solution.py:506
  (1 shorter events, 0.0 us)
Async XLA Ops:
  1.3 8.9 %collective-permute-start.2 = (f32[1,5]{1,0:T(1,128)S(1)}, f32[1,5]{1,0:T(1,128)S(1)}, u32[]{:S(2)}, u32[]{:S(2)}) collective-permute-start(f32[1,5]{1,0:T(1,128)S(1)} %bitcast.2), channel_id=1, source_target_pairs={{0,3},{1,2},{2,1},{3,0},{4,7},{5,6},{6,5},{7,4},{8,11},{9,10},{10,... | collective-permute-start | bytes 68 | tf_op jit(solution)/shard_map/ppermute | solution.py:443
  5.6 4.6 %collective-permute-start.1 = (f32[1,5]{1,0:T(1,128)S(1)}, f32[1,5]{1,0:T(1,128)S(1)}, u32[]{:S(2)}, u32[]{:S(2)}) collective-permute-start(f32[1,5]{1,0:T(1,128)S(1)} %bitcast.3), channel_id=1, source_target_pairs={{0,2},{1,3},{2,0},{3,1},{4,6},{5,7},{6,4},{7,5},{8,10},{9,11},{10,... | collective-permute-start | bytes 68 | tf_op jit(solution)/shard_map/ppermute | solution.py:443
  7.4 2.8 %collective-permute-start = (f32[1,5]{1,0:T(1,128)S(1)}, f32[1,5]{1,0:T(1,128)S(1)}, u32[]{:S(2)}, u32[]{:S(2)}) collective-permute-start(f32[1,5]{1,0:T(1,128)S(1)} %bitcast.4), channel_id=1, source_target_pairs={{0,1},{1,0},{2,3},{3,2},{4,5},{5,4},{6,7},{7,6},{8,9},{9,8},{10,11... | collective-permute-start | bytes 68 | tf_op jit(solution)/shard_map/ppermute | solution.py:443
  11.5 5.4 %copy-start.2 = (s32[1,2]{1,0:T(1,128)S(1)}, s32[1,2]{1,0:T(1,128)}, u32[]{:S(2)}) copy-start(s32[1,2]{1,0:T(1,128)} %shift.3) | copy-start | bytes 28
  11.5 5.4 %copy-start.3 = (f32[1,5]{1,0:T(1,128)S(1)}, f32[1,5]{1,0:T(1,128)}, u32[]{:S(2)}) copy-start(f32[1,5]{1,0:T(1,128)} %gains.3) | copy-start | bytes 64
  12.9 13.3 %copy-start.1 = (f32[2,512]{1,0:T(2,128)S(1)}, f32[2,512]{1,0:T(2,128)}, u32[]{:S(2)}) copy-start(f32[2,512]{1,0:T(2,128)} %constant.13.clone.odd) | copy-start | bytes 12292
  13.0 6.2 %collective-permute-start.6 = (f32[5,80,128]{2,1,0:T(8,128)S(1)}, f32[5,80,128]{2,1,0:T(8,128)S(1)}, u32[]{:S(2)}, u32[]{:S(2)}) collective-permute-start(f32[5,80,128]{2,1,0:T(8,128)S(1)} %get-tuple-element.50), channel_id=1, source_target_pairs={{0,1},{1,0},{2,3},{3,2},{4,5},{5,4},{6,7},{7,6},{8,9},{9,8},{10,11... | collective-permute-start | bytes 614408 | tf_op jit(solution)/shard_map/ppermute | solution.py:443
  13.6 8.0 %collective-permute-start.7 = (f32[5,80,128]{2,1,0:T(8,128)S(1)}, f32[5,80,128]{2,1,0:T(8,128)S(1)}, u32[]{:S(2)}, u32[]{:S(2)}) collective-permute-start(f32[5,80,128]{2,1,0:T(8,128)S(1)} %get-tuple-element.51), channel_id=1, source_target_pairs={{0,2},{1,3},{2,0},{3,1},{4,6},{5,7},{6,4},{7,5},{8,10},{9,11},{10,... | collective-permute-start | bytes 614408 | tf_op jit(solution)/shard_map/ppermute | solution.py:443
  14.8 11.5 %collective-permute-start.8 = (f32[5,80,128]{2,1,0:T(8,128)S(1)}, f32[5,80,128]{2,1,0:T(8,128)S(1)}, u32[]{:S(2)}, u32[]{:S(2)}) collective-permute-start(f32[5,80,128]{2,1,0:T(8,128)S(1)} %get-tuple-element.52), channel_id=1, source_target_pairs={{0,3},{1,2},{2,1},{3,0},{4,7},{5,6},{6,5},{7,4},{8,11},{9,10},{10,... | collective-permute-start | bytes 614408 | tf_op jit(solution)/shard_map/ppermute | solution.py:443
  16.8 17.3 %collective-permute-start.3 = (f32[5,48,128]{2,1,0:T(8,128)S(1)}, f32[5,48,128]{2,1,0:T(8,128)S(1)}, u32[]{:S(2)}, u32[]{:S(2)}) collective-permute-start(f32[5,48,128]{2,1,0:T(8,128)S(1)} %get-tuple-element.46), channel_id=1, source_target_pairs={{0,1},{1,0},{2,3},{3,2},{4,5},{5,4},{6,7},{7,6},{8,9},{9,8},{10,11... | collective-permute-start | bytes 368648 | tf_op jit(solution)/shard_map/ppermute | solution.py:443
  29.2 13.4 %collective-permute-start.12 = (f32[160,256]{1,0:T(8,128)S(1)}, f32[160,256]{1,0:T(8,128)S(1)}, u32[]{:S(2)}, u32[]{:S(2)}) collective-permute-start(f32[160,256]{1,0:T(8,128)S(1)} %get-tuple-element.62), channel_id=1, source_target_pairs={{0,1},{1,0},{2,3},{3,2},{4,5},{5,4},{6,7},{7,6},{8,9},{9,8},{10,11... | collective-permute-start | bytes 491528 | tf_op jit(solution)/shard_map/ppermute | solution.py:443
  29.4 7.8 %collective-permute-start.4 = (f32[5,48,128]{2,1,0:T(8,128)S(1)}, f32[5,48,128]{2,1,0:T(8,128)S(1)}, u32[]{:S(2)}, u32[]{:S(2)}) collective-permute-start(f32[5,48,128]{2,1,0:T(8,128)S(1)} %get-tuple-element.47), channel_id=1, source_target_pairs={{0,2},{1,3},{2,0},{3,1},{4,6},{5,7},{6,4},{7,5},{8,10},{9,11},{10,... | collective-permute-start | bytes 368648 | tf_op jit(solution)/shard_map/ppermute | solution.py:443
  30.6 8.8 %collective-permute-start.5 = (f32[5,48,128]{2,1,0:T(8,128)S(1)}, f32[5,48,128]{2,1,0:T(8,128)S(1)}, u32[]{:S(2)}, u32[]{:S(2)}) collective-permute-start(f32[5,48,128]{2,1,0:T(8,128)S(1)} %get-tuple-element.48), channel_id=1, source_target_pairs={{0,3},{1,2},{2,1},{3,0},{4,7},{5,6},{6,5},{7,4},{8,11},{9,10},{10,... | collective-permute-start | bytes 368648 | tf_op jit(solution)/shard_map/ppermute | solution.py:443
  32.9 13.6 %collective-permute-start.13 = (f32[160,256]{1,0:T(8,128)S(1)}, f32[160,256]{1,0:T(8,128)S(1)}, u32[]{:S(2)}, u32[]{:S(2)}) collective-permute-start(f32[160,256]{1,0:T(8,128)S(1)} %get-tuple-element.63), channel_id=1, source_target_pairs={{0,2},{1,3},{2,0},{3,1},{4,6},{5,7},{6,4},{7,5},{8,10},{9,11},{10,... | collective-permute-start | bytes 491528 | tf_op jit(solution)/shard_map/ppermute | solution.py:443
  34.1 12.4 %collective-permute-start.14 = (f32[160,256]{1,0:T(8,128)S(1)}, f32[160,256]{1,0:T(8,128)S(1)}, u32[]{:S(2)}, u32[]{:S(2)}) collective-permute-start(f32[160,256]{1,0:T(8,128)S(1)} %get-tuple-element.64), channel_id=1, source_target_pairs={{0,3},{1,2},{2,1},{3,0},{4,7},{5,6},{6,5},{7,4},{8,11},{9,10},{10,... | collective-permute-start | bytes 491528 | tf_op jit(solution)/shard_map/ppermute | solution.py:443
  39.4 6.0 %copy-start = (f32[4,2,112,128]{3,2,1,0:T(8,128)S(1)}, f32[4,2,112,128]{3,2,1,0:T(8,128)}, u32[]{:S(2)}) copy-start(f32[4,2,112,128]{3,2,1,0:T(8,128)} %constant.14.clone.first) | copy-start | bytes 1376260
  41.7 6.1 %collective-permute-start.9 = (f32[64,256]{1,0:T(8,128)S(1)}, f32[64,256]{1,0:T(8,128)S(1)}, u32[]{:S(2)}, u32[]{:S(2)}) collective-permute-start(f32[64,256]{1,0:T(8,128)S(1)} %get-tuple-element.57), channel_id=1, source_target_pairs={{0,1},{1,0},{2,3},{3,2},{4,5},{5,4},{6,7},{7,6},{8,9},{9,8},{10,11... | collective-permute-start | bytes 196616 | tf_op jit(solution)/shard_map/ppermute | solution.py:443
  41.8 6.0 %collective-permute-start.10 = (f32[64,256]{1,0:T(8,128)S(1)}, f32[64,256]{1,0:T(8,128)S(1)}, u32[]{:S(2)}, u32[]{:S(2)}) collective-permute-start(f32[64,256]{1,0:T(8,128)S(1)} %get-tuple-element.58), channel_id=1, source_target_pairs={{0,2},{1,3},{2,0},{3,1},{4,6},{5,7},{6,4},{7,5},{8,10},{9,11},{10,... | collective-permute-start | bytes 196616 | tf_op jit(solution)/shard_map/ppermute | solution.py:443
  42.6 6.2 %collective-permute-start.11 = (f32[64,256]{1,0:T(8,128)S(1)}, f32[64,256]{1,0:T(8,128)S(1)}, u32[]{:S(2)}, u32[]{:S(2)}) collective-permute-start(f32[64,256]{1,0:T(8,128)S(1)} %get-tuple-element.59), channel_id=1, source_target_pairs={{0,3},{1,2},{2,1},{3,0},{4,7},{5,6},{6,5},{7,4},{8,11},{9,10},{10,... | collective-permute-start | bytes 196616 | tf_op jit(solution)/shard_map/ppermute | solution.py:443

commit v5 on v4

--- a/solution.py
+++ b/solution.py
@@ -19,12 +19,12 @@
 PARTS = 4
 ROWS = PIX // PARTS
 CHUNKS = (0, 1)
-LOW = (24, 0)
-MAIN = (40, 24)
-FOLD_LOW = (24, 16)
-FOLD = (40, 8)
-COLS = (80, 32)
-EXT = (40, 32)
+LOW = (32, 0)
+MAIN = (32, 32)
+FOLD_LOW = (32, 16)
+FOLD = (32, 16)
+COLS = (64, 48)
+EXT = (32, 40)
 ORDERS = (0, 1, -1, 2, -2)
 ARC = (
     1.5707963050,
@@ -91,8 +91,46 @@
     return jnp.cos(angle), jnp.sin(angle)
 
 
-def phase_kernel(place, offset, shift_far, source, base_far, frames, turns, phases, *rest):
-    y_out, x_out, (base, shift, sems) = rest[0:2], (rest[2:4], rest[4:6]), rest[6:]
+def row_blocks(base, part, count):
+    lane = lax.broadcasted_iota(jnp.int32, (1, PIX), 1)
+    parity = lane % 2
+    sign = (1 - lane % 4 + parity).astype(jnp.float32)
+    quarter_re = jnp.where(parity == 0, sign, 0.0)
+    quarter_im = jnp.where(parity == 1, sign, 0.0)
+    half_turn = 1.0 - 2.0 * parity.astype(jnp.float32)
+    cosine, sine = base[part, 0].astype(jnp.float32), base[part, 1].astype(jnp.float32)
+    cos_re, cos_im = cosine * quarter_re, cosine * quarter_im
+    sin_re, sin_im = sine * quarter_re, sine * quarter_im
+    blocks = [(cosine, sine), (cos_re - sin_im, sin_re + cos_im)]
+    if count > 2:
+        blocks += [
+            (cosine * half_turn, sine * half_turn),
+            (cos_re + sin_im, sin_re - cos_im),
+        ]
+    return blocks, half_turn
+
+
+def x_rows(base, chunk, outs):
+    top = lax.broadcasted_iota(jnp.int32, (8, PIX), 0) == 0
+    for part in range(2):
+        blocks, half_turn = row_blocks(base, part, 2)
+        lone = half_turn if part == 0 else jnp.zeros_like(half_turn)
+        for d in range(PARTS):
+            pieces = []
+            for kind in range(2):
+                for l in range(LOW[chunk], LOW[chunk] + MAIN[chunk], 8):
+                    column = 64 * (l // 16) + 16 * d + l % 16
+                    s, t = column // ROWS, column % ROWS
+                    piece = blocks[s][kind][t : t + 8]
+                    if column == 0 and kind == 1:
+                        piece = jnp.where(top, lone, piece)
+                    pieces.append(piece)
+            outs[part][d] = jnp.concatenate(pieces, axis=0).astype(jnp.bfloat16)
+
+
+def phase_kernel(
+    place, offset, shift_far, source, base_far, frames, turns, phases, base, x_hi, x_lo, shift, sems
+):
     base_copy = pltpu.make_async_copy(base_far, base, sems.at[0])
     base_copy.start()
     shift_copy = pltpu.make_async_copy(shift_far, shift, sems.at[1])
@@ -106,40 +144,6 @@
     phases[1] = jnp.sin(phase_at)
     phases[2] = jnp.cos(2.0 * phase_at)
     phases[3] = jnp.sin(2.0 * phase_at)
-    lane = lax.broadcasted_iota(jnp.int32, (1, PIX), 1)
-    parity = lane % 2
-    sign = (1 - lane % 4 + parity).astype(jnp.float32)
-    quarter_re = jnp.where(parity == 0, sign, 0.0)
-    quarter_im = jnp.where(parity == 1, sign, 0.0)
-    half_turn = 1.0 - 2.0 * parity.astype(jnp.float32)
-    base_copy.wait()
-    for part in range(2):
-        cosine, sine = base[part, 0].astype(jnp.float32), base[part, 1].astype(jnp.float32)
-        cos_re, cos_im = cosine * quarter_re, cosine * quarter_im
-        sin_re, sin_im = sine * quarter_re, sine * quarter_im
-        blocks = [
-            (cosine, sine),
-            (cos_re - sin_im, sin_re + cos_im),
-            (cosine * half_turn, sine * half_turn),
-            (cos_re + sin_im, sin_re - cos_im),
-        ]
-        for s in range(PARTS):
-            for kind in range(2):
-                y_out[part][s, kind] = blocks[s][kind].astype(jnp.bfloat16)
-        lone = half_turn if part == 0 else jnp.zeros_like(half_turn)
-        top = lax.broadcasted_iota(jnp.int32, (8, PIX), 0) == 0
-        for chunk in CHUNKS:
-            for d in range(PARTS):
-                pieces = []
-                for kind in range(2):
-                    for l in range(LOW[chunk], LOW[chunk] + MAIN[chunk], 8):
-                        column = 64 * (l // 16) + 16 * d + l % 16
-                        s, t = column // ROWS, column % ROWS
-                        piece = blocks[s][kind][t : t + 8]
-                        if column == 0 and kind == 1:
-                            piece = jnp.where(top, lone, piece)
-                        pieces.append(piece)
-                x_out[chunk][part][d] = jnp.concatenate(pieces, axis=0).astype(jnp.bfloat16)
     shift_copy.wait()
     shift_y, shift_x = shift[0:1, 0:1], shift[0:1, 1:2]
     x_cos, x_sin = turn_pair(lax.broadcasted_iota(jnp.int32, (8, PIX), 1) * shift_x)
@@ -154,6 +158,8 @@
     turns[1] = turn_im
     turns[2] = turn_re * turn_re - turn_im * turn_im
     turns[3] = 2.0 * turn_re * turn_im
+    base_copy.wait()
+    x_rows(base, 0, (x_hi, x_lo))
     copy.wait()
 
 
@@ -196,10 +202,17 @@
     spectra_rows(place[0], 2 * MAIN[0], (2, 3), band, x_hi, x_lo, outs)
 
 
-def forward_rest_kernel(place, band_hi, band_lo, x_hi0, x_lo0, x_hi1, x_lo1, *outs):
+def forward_rest_kernel(place, band_hi, band_lo, x_hi0, x_lo0, base, *rest):
+    outs, (y_hi, y_lo, x_hi1, x_lo1) = rest[:6], rest[6:]
+    x_rows(base, 1, (x_hi1, x_lo1))
     band = (band_hi[...], band_lo[...])
     spectra_rows(place[0], 2 * MAIN[1], (0, 1, 2, 3), band, x_hi1, x_lo1, outs[2:])
     spectra_rows(place[0], 2 * MAIN[0], (0, 1), band, x_hi0, x_lo0, outs[:2])
+    for part, out in ((0, y_hi), (1, y_lo)):
+        blocks, _ = row_blocks(base, part, PARTS)
+        for s in range(PARTS):
+            for kind in range(2):
+                out[s, kind] = blocks[s][kind].astype(jnp.bfloat16)
 
 
 def root(value):
@@ -451,17 +464,13 @@
 
     sums = jnp.sum(frames.astype(jnp.float32), axis=(2, 3))
     sums = from_partners([sums] * PARTS)
-    frames, turns, phases, y_hi, y_lo, *x_parts = call(
+    table = bf16(PARTS, 2 * MAIN[0], PIX)
+    frames, turns, phases, near_base, *x_parts = call(
         phase_kernel,
-        [bf16(PHASES, ROWS, PIX), f32(4, ROWS, PIX), f32(4, 8, 128)]
-        + [bf16(PARTS, 2, ROWS, PIX)] * 2
-        + [bf16(PARTS, 2 * MAIN[c], PIX) for c in CHUNKS for _ in range(2)],
+        [bf16(PHASES, ROWS, PIX), f32(4, ROWS, PIX), f32(4, 8, 128), bf16(*base.shape)]
+        + [table] * 2,
         [smem()] * 2 + [hbm()] * 3,
-        scratch=[
-            pltpu.VMEM(base.shape, jnp.bfloat16),
-            pltpu.VMEM((1, 2), jnp.int32),
-            pltpu.SemaphoreType.DMA((3,)),
-        ],
+        scratch=[pltpu.VMEM((1, 2), jnp.int32), pltpu.SemaphoreType.DMA((3,))],
     )(
         place,
         phase_offset,
@@ -474,12 +483,13 @@
         forward_kernel,
         [blocks[0]] * 2 + [bf16(5 * ROWS, PIX)] * 2,
         [smem()] + [vmem()] * 9,
-    )(place, *sums, turns, phases, frames, *x_parts[:2])
-    sent = call(
+    )(place, *sums, turns, phases, frames, *x_parts)
+    *sent, y_hi, y_lo = call(
         forward_rest_kernel,
-        [blocks[0]] * 2 + [blocks[1]] * PARTS,
-        [smem()] + [vmem()] * 6,
-    )(place, band_hi, band_lo, *x_parts)
+        [blocks[0]] * 2 + [blocks[1]] * PARTS + [bf16(PARTS, 2, ROWS, PIX)] * 2,
+        [smem()] + [vmem()] * 5,
+        scratch=[pltpu.VMEM((PARTS, 2 * MAIN[1], PIX), jnp.bfloat16)] * 2,
+    )(place, band_hi, band_lo, *x_parts, near_base)
     spectra = [from_partners([*sent[:2], *far]), from_partners(sent[2:])]
     got = []
     after = sent[0]

time: 50.6 us -> 44.9 us (0.89)
  waiting for transfers between devices: 10.3 us -> 3.31 us
  starting transfers between devices: 20.5 us -> 21.9 us
    ppermute x15, waiting for transfers between devices: 10.3 us -> 3.31 us  [from_partners(): lax.ppermute(blocks[k], 'row', [(i, i ^ k) for i in range(PARTS)])]
    ppermute x15, starting transfers between devices: 20.5 us -> 21.9 us  [from_partners(): lax.ppermute(blocks[k], 'row', [(i, i ^ k) for i in range(PARTS)])]
  transfers between devices with their start and end apart: 15 -> 15, of which waited for: 4 -> 1; matrix products, arithmetic and copies ran while one was open for 0% -> 0% of each run, Pallas kernels for 26% -> 32%
where the time goes in v5:
time: 44.9 us; the launch traced here: 44.8 us
  starting transfers between devices  21.9 us (49%)
  Pallas kernels  17.2 us (38%)
  waiting for transfers between devices  3.31 us (7%)
  other arithmetic  1.3 us (3%)
  between operations  1.03 us (2%)
    ppermute x15, starting transfers between devices, from_partners(): lax.ppermute(blocks[k], 'row', [(i, i ^ k) for i in range(PARTS)])  21.9 us
    pallas_call x2, Pallas kernels, reconstruct(): call(functools.partial(middle_kernel, c), [f32(2 * COLS[c], 2 * ROWS)] *...  5.06 us
    pallas_call x2, Pallas kernels, reconstruct(): call(functools.partial(weights_kernel, c), f32(5, 2, COLS[c], PIX), [smem...  3.46 us
    ppermute x15, waiting for transfers between devices, from_partners(): lax.ppermute(blocks[k], 'row', [(i, i ^ k) for i in range(PARTS)])  3.31 us
    pallas_call x1, Pallas kernels, reconstruct(): call(forward_rest_kernel, [blocks[0]] * 2 + [blocks[1]] * PARTS + [bf16(P...  1.88 us
    pallas_call x1, Pallas kernels, reconstruct(): call(final_kernel, f32(2 * ROWS, GRID), [vmem()] * 7, hbm(), [pltpu.VMEM(...  1.79 us
    pallas_call x1, Pallas kernels, reconstruct(): call(phase_kernel, [bf16(PHASES, ROWS, PIX), f32(4, ROWS, PIX), f32(4, 8,...  1.65 us
    reduce_sum x1, other arithmetic, reconstruct(): sums = jnp.sum(frames.astype(jnp.float32), axis=(2, 3))  1.3 us
  transfers between devices with their start and end apart: 15, of which 1 were waited for; matrix products, arithmetic and copies ran while one was open for 0% of the time, Pallas kernels for 32%

profile of v5, /device:TPU:1, one launch (start us, length us, event | category | flops | bytes accessed | tf_op | source)
XLA Modules:
  0.0 44.8 jit_solution(17636416370404511460)
XLA Ops:
  0.0 1.3 %convert_reduce_fusion = f32[5]{0:T(128)S(1)} fusion(bf16[1,5,128,512]{3,2,1,0:T(8,128)(2,1)} %source.1), kind=kLoop, calls=%fused_computation | loop fusion | flops 655355 | bytes 655380 | tf_op jit(solution)/shard_map/reduce_sum | solution.py:465
  1.3 4.3 %collective-permute-start.2 = (f32[1,5]{1,0:T(1,128)S(1)}, f32[1,5]{1,0:T(1,128)S(1)}, u32[]{:S(2)}, u32[]{:S(2)}) collective-permute-start(f32[1,5]{1,0:T(1,128)S(1)} %bitcast.2), channel_id=1, source_target_pairs={{0,3},{1,2},{2,1},{3,0},{4,7},{5,6},{6,5},{7,4},{8,11},{9,10},{10,... | collective-permute-start | bytes 68 | tf_op jit(solution)/shard_map/ppermute | solution.py:456
  5.6 1.8 %collective-permute-start.1 = (f32[1,5]{1,0:T(1,128)S(1)}, f32[1,5]{1,0:T(1,128)S(1)}, u32[]{:S(2)}, u32[]{:S(2)}) collective-permute-start(f32[1,5]{1,0:T(1,128)S(1)} %bitcast.3), channel_id=1, source_target_pairs={{0,2},{1,3},{2,0},{3,1},{4,6},{5,7},{6,4},{7,5},{8,10},{9,11},{10,... | collective-permute-start | bytes 68 | tf_op jit(solution)/shard_map/ppermute | solution.py:456
  7.4 0.0 collective-permute-start
  8.1 1.6 %shard_map.73 = (bf16[5,128,512]{2,1,0:T(8,128)(2,1)S(1)}, f32[4,128,512]{2,1,0:T(8,128)S(1)}, f32[4,8,128]{2,1,0:T(8,128)S(1)}, bf16[2,2,128,512]{3,2,1,0:T(8,1...) custom-call(s32[1]{0:T(128)} %bitcast.place, f32[1]{0:T(128)S(6)} %copy.8.offset, ...), custom_call_target="tpu_custom_call" | custom-call | tf_op jit(solution)/shard_map/pallas_call | solution.py:468
  9.7 0.0 collective-permute-done.2.sums3
  9.7 0.0 collective-permute-done.1.sums2
  9.7 0.0 collective-permute-done.sums1
  9.8 1.3 %shard_map.74 = (f32[5,64,128]{2,1,0:T(8,128)S(1)}, f32[5,64,128]{2,1,0:T(8,128)S(1)}, bf16[640,512]{1,0:T(8,128)(2,1)S(1)}, bf16[640,512]{1,0:T(8,128)(2,1)S(1)}) custom-call(s32[1]{0:T(128)} %bitcast.place, f32[1,5]{1,0:T(1,128)S(1)} %bitcast.5, f32[1,5]{1,0:T(1,128)S(1)} %collective-permute-done.sums1, f32[1,5]{1,0:T(1,128)S(1)} %collective-permute-done.1.sums2, ...), custom_call_target="tpu_custom_call" | custom-call | tf_op jit(solution)/shard_map/pallas_call | solution.py:482
  11.0 0.0 copy-start.2
  11.0 0.0 copy-start.3
  11.0 1.7 %collective-permute-start.7 = (f32[5,64,128]{2,1,0:T(8,128)S(1)}, f32[5,64,128]{2,1,0:T(8,128)S(1)}, u32[]{:S(2)}, u32[]{:S(2)}) collective-permute-start(f32[5,64,128]{2,1,0:T(8,128)S(1)} %get-tuple-element.49), channel_id=1, source_target_pairs={{0,2},{1,3},{2,0},{3,1},{4,6},{5,7},{6,4},{7,5},{8,10},{9,11},{10,... | collective-permute-start | bytes 491528 | tf_op jit(solution)/shard_map/ppermute | solution.py:456
  12.7 2.4 %collective-permute-start.8 = (f32[5,64,128]{2,1,0:T(8,128)S(1)}, f32[5,64,128]{2,1,0:T(8,128)S(1)}, u32[]{:S(2)}, u32[]{:S(2)}) collective-permute-start(f32[5,64,128]{2,1,0:T(8,128)S(1)} %get-tuple-element.50), channel_id=1, source_target_pairs={{0,3},{1,2},{2,1},{3,0},{4,7},{5,6},{6,5},{7,4},{8,11},{9,10},{10,... | collective-permute-start | bytes 491528 | tf_op jit(solution)/shard_map/ppermute | solution.py:456
  15.1 1.9 %shard_map.75 = (f32[5,64,128]{2,1,0:T(8,128)S(1)}, f32[5,64,128]{2,1,0:T(8,128)S(1)}, f32[5,64,128]{2,1,0:T(8,128)S(1)}, f32[5,64,128]{2,1,0:T(8,128)S(1)}, f32...) custom-call(s32[1]{0:T(128)} %bitcast.place, ...), custom_call_target="tpu_custom_call" | custom-call | tf_op jit(solution)/shard_map/pallas_call | solution.py:487
  16.9 0.0 copy-start.1
  17.0 0.1 collective-permute-start.6
  17.1 0.5 %collective-permute-start.3 = (f32[5,64,128]{2,1,0:T(8,128)S(1)}, f32[5,64,128]{2,1,0:T(8,128)S(1)}, u32[]{:S(2)}, u32[]{:S(2)}) collective-permute-start(f32[5,64,128]{2,1,0:T(8,128)S(1)} %get-tuple-element.44), channel_id=1, source_target_pairs={{0,1},{1,0},{2,3},{3,2},{4,5},{5,4},{6,7},{7,6},{8,9},{9,8},{10,11... | collective-permute-start | bytes 491528 | tf_op jit(solution)/shard_map/ppermute | solution.py:456
  17.6 0.9 %collective-permute-start.4 = (f32[5,64,128]{2,1,0:T(8,128)S(1)}, f32[5,64,128]{2,1,0:T(8,128)S(1)}, u32[]{:S(2)}, u32[]{:S(2)}) collective-permute-start(f32[5,64,128]{2,1,0:T(8,128)S(1)} %get-tuple-element.45), channel_id=1, source_target_pairs={{0,2},{1,3},{2,0},{3,1},{4,6},{5,7},{6,4},{7,5},{8,10},{9,11},{10,... | collective-permute-start | bytes 491528 | tf_op jit(solution)/shard_map/ppermute | solution.py:456
  18.5 0.0 collective-permute-done.7.got2
  18.5 2.8 %collective-permute-start.5 = (f32[5,64,128]{2,1,0:T(8,128)S(1)}, f32[5,64,128]{2,1,0:T(8,128)S(1)}, u32[]{:S(2)}, u32[]{:S(2)}) collective-permute-start(f32[5,64,128]{2,1,0:T(8,128)S(1)} %get-tuple-element.46), channel_id=1, source_target_pairs={{0,3},{1,2},{2,1},{3,0},{4,7},{5,6},{6,5},{7,4},{8,11},{9,10},{10,... | collective-permute-start | bytes 491528 | tf_op jit(solution)/shard_map/ppermute | solution.py:456
  21.3 0.0 copy-done.2
  21.3 0.0 copy-done.3
  21.3 1.9 %shard_map.76.weights = f32[5,2,64,512]{3,2,1,0:T(8,128)S(1)} custom-call(s32[1]{0:T(128)} %bitcast.place, f32[1,5]{1,0:T(1,128)S(1)} %copy-done.3, s32[1,2]{1,0:T(1,128)S(1)} %copy-done.2, f32[5,64,128]{2,1,0:T(8,128)S(1)} %get-tuple-element.47.after.got0), custom_call_target="tpu_custom_call" | custom-call | tf_op jit(solution)/shard_map/pallas_call | solution.py:497
  23.2 0.0 collective-permute-done.8.got3
  23.2 0.0 collective-permute-done.6.got1
  23.2 0.0 copy-done.1
  23.2 2.4 %shard_map.77 = (f32[128,256]{1,0:T(8,128)S(1)}, f32[128,256]{1,0:T(8,128)S(1)}, f32[128,256]{1,0:T(8,128)S(1)}, f32[128,256]{1,0:T(8,128)S(1)}) custom-call(s32[1]{0:T(128)} %bitcast.place, f32[5,64,128]{2,1,0:T(8,128)S(1)} %get-tuple-element.47.after.got0, f32[5,64,128]{2,1,0:T(8,128)S(1)} %collective-permute-done.6.got1, ...), custom_call_target="tpu_custom_call" | custom-call | tf_op jit(solution)/shard_map/pallas_call | solution.py:503
  25.6 0.1 collective-permute-start.12
  25.7 2.1 %collective-permute-start.13 = (f32[128,256]{1,0:T(8,128)S(1)}, f32[128,256]{1,0:T(8,128)S(1)}, u32[]{:S(2)}, u32[]{:S(2)}) collective-permute-start(f32[128,256]{1,0:T(8,128)S(1)} %get-tuple-element.61), channel_id=1, source_target_pairs={{0,2},{1,3},{2,0},{3,1},{4,6},{5,7},{6,4},{7,5},{8,10},{9,11},{10,... | collective-permute-start | bytes 393224 | tf_op jit(solution)/shard_map/ppermute | solution.py:456
  27.9 0.0 collective-permute-done.3.got1
  27.9 1.5 %collective-permute-start.14 = (f32[128,256]{1,0:T(8,128)S(1)}, f32[128,256]{1,0:T(8,128)S(1)}, u32[]{:S(2)}, u32[]{:S(2)}) collective-permute-start(f32[128,256]{1,0:T(8,128)S(1)} %get-tuple-element.62), channel_id=1, source_target_pairs={{0,3},{1,2},{2,1},{3,0},{4,7},{5,6},{6,5},{7,4},{8,11},{9,10},{10,... | collective-permute-start | bytes 393224 | tf_op jit(solution)/shard_map/ppermute | solution.py:456
  29.4 1.6 %shard_map.78.weights = f32[5,2,48,512]{3,2,1,0:T(8,128)S(1)} custom-call(s32[1]{0:T(128)} %bitcast.place, f32[1,5]{1,0:T(1,128)S(1)} %copy-done.3, s32[1,2]{1,0:T(1,128)S(1)} %copy-done.2, f32[128,256]{1,0:T(8,128)S(1)} %get-tuple-element.53.after.got0), custom_call_target="tpu_custom_call" | custom-call | tf_op jit(solution)/shard_map/pallas_call | solution.py:497
  30.9 0.0 collective-permute-done.4.got2
  30.9 0.0 collective-permute-done.5.got3
  31.0 0.0 copy-start
  31.0 2.7 %shard_map.79 = (f32[96,256]{1,0:T(8,128)S(1)}, f32[96,256]{1,0:T(8,128)S(1)}, f32[96,256]{1,0:T(8,128)S(1)}, f32[96,256]{1,0:T(8,128)S(1)}) custom-call(s32[1]{0:T(128)} %bitcast.place, f32[5,64,128]{2,1,0:T(8,128)S(1)} %get-tuple-element.43.got0, f32[5,64,128]{2,1,0:T(8,128)S(1)} %collective-permute-done.3.got1, ...), custom_call_target="tpu_custom_call" | custom-call | tf_op jit(solution)/shard_map/pallas_call | solution.py:503
  33.7 0.1 collective-permute-start.9
  33.8 2.2 %collective-permute-start.10 = (f32[96,256]{1,0:T(8,128)S(1)}, f32[96,256]{1,0:T(8,128)S(1)}, u32[]{:S(2)}, u32[]{:S(2)}) collective-permute-start(f32[96,256]{1,0:T(8,128)S(1)} %get-tuple-element.56), channel_id=1, source_target_pairs={{0,2},{1,3},{2,0},{3,1},{4,6},{5,7},{6,4},{7,5},{8,10},{9,11},{10,... | collective-permute-start | bytes 294920 | tf_op jit(solution)/shard_map/ppermute | solution.py:456
  35.9 0.0 collective-permute-done.12.got1
  35.9 1.5 %collective-permute-start.11 = (f32[96,256]{1,0:T(8,128)S(1)}, f32[96,256]{1,0:T(8,128)S(1)}, u32[]{:S(2)}, u32[]{:S(2)}) collective-permute-start(f32[96,256]{1,0:T(8,128)S(1)} %get-tuple-element.57), channel_id=1, source_target_pairs={{0,3},{1,2},{2,1},{3,0},{4,7},{5,6},{6,5},{7,4},{8,11},{9,10},{10,... | collective-permute-start | bytes 294920 | tf_op jit(solution)/shard_map/ppermute | solution.py:456
  37.4 1.1 %shard_map.80 = (bf16[512,1024]{1,0:T(8,128)(2,1)S(1)}, bf16[384,1024]{1,0:T(8,128)(2,1)S(1)}, bf16[512,1024]{1,0:T(8,128)(2,1)S(1)}, bf16[384,1024]{1,0:T(8,128)(2,1)S(1)}) custom-call(s32[1]{0:T(128)} %bitcast.place, f32[4,2,112,128]{3,2,1,0:T(8,128)S(1)} %copy-done, f32[96,256]{1,0:T(8,128)S(1)} %get-tuple-element.54.after.got0), custom_call_target="tpu_custom_call" | custom-call | tf_op jit(solution)/shard_map/pallas_call | solution.py:510
  38.5 0.0 collective-permute-done.13.got2
  38.5 0.0 collective-permute-done.14.got3
  38.5 1.0 %shard_map.81.part = f32[256,1024]{1,0:T(8,128)S(1)} custom-call(f32[128,256]{1,0:T(8,128)S(1)} %get-tuple-element.53.after.got0, f32[128,256]{1,0:T(8,128)S(1)} %collective-permute-done.12.got1, f32[128,256]{1,0:T(8,128)S(1)} %collective-permute-done.13.got2, f32[128,256]{1,0:T(8,128)S(1)} %collective-permute-done.14.got3, ...), custom_call_target="tpu_custom_call" | custom-call | tf_op jit(solution)/shard_map/pallas_call | solution.py:515
  39.5 0.0 collective-permute-done.9.got1
  39.5 0.0 collective-permute-done.10.got2
  39.5 3.3 %collective-permute-done.11.got3 = f32[96,256]{1,0:T(8,128)S(1)} collective-permute-done((f32[96,256]{1,0:T(8,128)S(1)}, f32[96,256]{1,0:T(8,128)S(1)}, u32[]{:S(2)}, u32[]{:S(2)}) %collective-permute-start.11) | collective-permute-done | bytes 98336 | tf_op jit(solution)/shard_map/ppermute | solution.py:456
  42.8 1.8 %shard_map.82 = f32[256,1024]{1,0:T(8,128)} custom-call(f32[96,256]{1,0:T(8,128)S(1)} %get-tuple-element.54.after.got0, f32[96,256]{1,0:T(8,128)S(1)} %collective-permute-done.9.got1, f32[96,256]{1,0:T(8,128)S(1)} %collective-permute-done.10.got2, f32[96,256]{1,0:T(8,128)S(1)} %collective-permute-done.11.got3, ...), custom_call_target="tpu_custom_call" | custom-call | tf_op jit(solution)/shard_map/pallas_call | solution.py:516
  (1 shorter events, 0.0 us)
Async XLA Ops:
  1.3 8.4 %collective-permute-start.2 = (f32[1,5]{1,0:T(1,128)S(1)}, f32[1,5]{1,0:T(1,128)S(1)}, u32[]{:S(2)}, u32[]{:S(2)}) collective-permute-start(f32[1,5]{1,0:T(1,128)S(1)} %bitcast.2), channel_id=1, source_target_pairs={{0,3},{1,2},{2,1},{3,0},{4,7},{5,6},{6,5},{7,4},{8,11},{9,10},{10,... | collective-permute-start | bytes 68 | tf_op jit(solution)/shard_map/ppermute | solution.py:456
  5.6 4.1 %collective-permute-start.1 = (f32[1,5]{1,0:T(1,128)S(1)}, f32[1,5]{1,0:T(1,128)S(1)}, u32[]{:S(2)}, u32[]{:S(2)}) collective-permute-start(f32[1,5]{1,0:T(1,128)S(1)} %bitcast.3), channel_id=1, source_target_pairs={{0,2},{1,3},{2,0},{3,1},{4,6},{5,7},{6,4},{7,5},{8,10},{9,11},{10,... | collective-permute-start | bytes 68 | tf_op jit(solution)/shard_map/ppermute | solution.py:456
  7.4 2.3 %collective-permute-start = (f32[1,5]{1,0:T(1,128)S(1)}, f32[1,5]{1,0:T(1,128)S(1)}, u32[]{:S(2)}, u32[]{:S(2)}) collective-permute-start(f32[1,5]{1,0:T(1,128)S(1)} %bitcast.4), channel_id=1, source_target_pairs={{0,1},{1,0},{2,3},{3,2},{4,5},{5,4},{6,7},{7,6},{8,9},{9,8},{10,11... | collective-permute-start | bytes 68 | tf_op jit(solution)/shard_map/ppermute | solution.py:456
  11.0 10.3 %copy-start.2 = (s32[1,2]{1,0:T(1,128)S(1)}, s32[1,2]{1,0:T(1,128)}, u32[]{:S(2)}) copy-start(s32[1,2]{1,0:T(1,128)} %shift.3) | copy-start | bytes 28
  11.0 10.3 %copy-start.3 = (f32[1,5]{1,0:T(1,128)S(1)}, f32[1,5]{1,0:T(1,128)}, u32[]{:S(2)}) copy-start(f32[1,5]{1,0:T(1,128)} %gains.3) | copy-start | bytes 64
  11.0 7.4 %collective-permute-start.7 = (f32[5,64,128]{2,1,0:T(8,128)S(1)}, f32[5,64,128]{2,1,0:T(8,128)S(1)}, u32[]{:S(2)}, u32[]{:S(2)}) collective-permute-start(f32[5,64,128]{2,1,0:T(8,128)S(1)} %get-tuple-element.49), channel_id=1, source_target_pairs={{0,2},{1,3},{2,0},{3,1},{4,6},{5,7},{6,4},{7,5},{8,10},{9,11},{10,... | collective-permute-start | bytes 491528 | tf_op jit(solution)/shard_map/ppermute | solution.py:456
  12.7 10.5 %collective-permute-start.8 = (f32[5,64,128]{2,1,0:T(8,128)S(1)}, f32[5,64,128]{2,1,0:T(8,128)S(1)}, u32[]{:S(2)}, u32[]{:S(2)}) collective-permute-start(f32[5,64,128]{2,1,0:T(8,128)S(1)} %get-tuple-element.50), channel_id=1, source_target_pairs={{0,3},{1,2},{2,1},{3,0},{4,7},{5,6},{6,5},{7,4},{8,11},{9,10},{10,... | collective-permute-start | bytes 491528 | tf_op jit(solution)/shard_map/ppermute | solution.py:456
  16.9 6.3 %copy-start.1 = (f32[2,512]{1,0:T(2,128)S(1)}, f32[2,512]{1,0:T(2,128)}, u32[]{:S(2)}) copy-start(f32[2,512]{1,0:T(2,128)} %constant.13.clone.odd) | copy-start | bytes 12292
  17.0 6.3 %collective-permute-start.6 = (f32[5,64,128]{2,1,0:T(8,128)S(1)}, f32[5,64,128]{2,1,0:T(8,128)S(1)}, u32[]{:S(2)}, u32[]{:S(2)}) collective-permute-start(f32[5,64,128]{2,1,0:T(8,128)S(1)} %get-tuple-element.48), channel_id=1, source_target_pairs={{0,1},{1,0},{2,3},{3,2},{4,5},{5,4},{6,7},{7,6},{8,9},{9,8},{10,11... | collective-permute-start | bytes 491528 | tf_op jit(solution)/shard_map/ppermute | solution.py:456
  17.1 10.8 %collective-permute-start.3 = (f32[5,64,128]{2,1,0:T(8,128)S(1)}, f32[5,64,128]{2,1,0:T(8,128)S(1)}, u32[]{:S(2)}, u32[]{:S(2)}) collective-permute-start(f32[5,64,128]{2,1,0:T(8,128)S(1)} %get-tuple-element.44), channel_id=1, source_target_pairs={{0,1},{1,0},{2,3},{3,2},{4,5},{5,4},{6,7},{7,6},{8,9},{9,8},{10,11... | collective-permute-start | bytes 491528 | tf_op jit(solution)/shard_map/ppermute | solution.py:456
  17.6 13.4 %collective-permute-start.4 = (f32[5,64,128]{2,1,0:T(8,128)S(1)}, f32[5,64,128]{2,1,0:T(8,128)S(1)}, u32[]{:S(2)}, u32[]{:S(2)}) collective-permute-start(f32[5,64,128]{2,1,0:T(8,128)S(1)} %get-tuple-element.45), channel_id=1, source_target_pairs={{0,2},{1,3},{2,0},{3,1},{4,6},{5,7},{6,4},{7,5},{8,10},{9,11},{10,... | collective-permute-start | bytes 491528 | tf_op jit(solution)/shard_map/ppermute | solution.py:456
  18.5 12.5 %collective-permute-start.5 = (f32[5,64,128]{2,1,0:T(8,128)S(1)}, f32[5,64,128]{2,1,0:T(8,128)S(1)}, u32[]{:S(2)}, u32[]{:S(2)}) collective-permute-start(f32[5,64,128]{2,1,0:T(8,128)S(1)} %get-tuple-element.46), channel_id=1, source_target_pairs={{0,3},{1,2},{2,1},{3,0},{4,7},{5,6},{6,5},{7,4},{8,11},{9,10},{10,... | collective-permute-start | bytes 491528 | tf_op jit(solution)/shard_map/ppermute | solution.py:456
  25.6 10.3 %collective-permute-start.12 = (f32[128,256]{1,0:T(8,128)S(1)}, f32[128,256]{1,0:T(8,128)S(1)}, u32[]{:S(2)}, u32[]{:S(2)}) collective-permute-start(f32[128,256]{1,0:T(8,128)S(1)} %get-tuple-element.60), channel_id=1, source_target_pairs={{0,1},{1,0},{2,3},{3,2},{4,5},{5,4},{6,7},{7,6},{8,9},{9,8},{10,11... | collective-permute-start | bytes 393224 | tf_op jit(solution)/shard_map/ppermute | solution.py:456
  25.7 12.8 %collective-permute-start.13 = (f32[128,256]{1,0:T(8,128)S(1)}, f32[128,256]{1,0:T(8,128)S(1)}, u32[]{:S(2)}, u32[]{:S(2)}) collective-permute-start(f32[128,256]{1,0:T(8,128)S(1)} %get-tuple-element.61), channel_id=1, source_target_pairs={{0,2},{1,3},{2,0},{3,1},{4,6},{5,7},{6,4},{7,5},{8,10},{9,11},{10,... | collective-permute-start | bytes 393224 | tf_op jit(solution)/shard_map/ppermute | solution.py:456
  27.9 10.6 %collective-permute-start.14 = (f32[128,256]{1,0:T(8,128)S(1)}, f32[128,256]{1,0:T(8,128)S(1)}, u32[]{:S(2)}, u32[]{:S(2)}) collective-permute-start(f32[128,256]{1,0:T(8,128)S(1)} %get-tuple-element.62), channel_id=1, source_target_pairs={{0,3},{1,2},{2,1},{3,0},{4,7},{5,6},{6,5},{7,4},{8,11},{9,10},{10,... | collective-permute-start | bytes 393224 | tf_op jit(solution)/shard_map/ppermute | solution.py:456
  31.0 6.4 %copy-start = (f32[4,2,112,128]{3,2,1,0:T(8,128)S(1)}, f32[4,2,112,128]{3,2,1,0:T(8,128)}, u32[]{:S(2)}) copy-start(f32[4,2,112,128]{3,2,1,0:T(8,128)} %constant.14.clone.first) | copy-start | bytes 1376260
  33.7 5.9 %collective-permute-start.9 = (f32[96,256]{1,0:T(8,128)S(1)}, f32[96,256]{1,0:T(8,128)S(1)}, u32[]{:S(2)}, u32[]{:S(2)}) collective-permute-start(f32[96,256]{1,0:T(8,128)S(1)} %get-tuple-element.55), channel_id=1, source_target_pairs={{0,1},{1,0},{2,3},{3,2},{4,5},{5,4},{6,7},{7,6},{8,9},{9,8},{10,11... | collective-permute-start | bytes 294920 | tf_op jit(solution)/shard_map/ppermute | solution.py:456
  33.8 5.8 %collective-permute-start.10 = (f32[96,256]{1,0:T(8,128)S(1)}, f32[96,256]{1,0:T(8,128)S(1)}, u32[]{:S(2)}, u32[]{:S(2)}) collective-permute-start(f32[96,256]{1,0:T(8,128)S(1)} %get-tuple-element.56), channel_id=1, source_target_pairs={{0,2},{1,3},{2,0},{3,1},{4,6},{5,7},{6,4},{7,5},{8,10},{9,11},{10,... | collective-permute-start | bytes 294920 | tf_op jit(solution)/shard_map/ppermute | solution.py:456
  35.9 6.9 %collective-permute-start.11 = (f32[96,256]{1,0:T(8,128)S(1)}, f32[96,256]{1,0:T(8,128)S(1)}, u32[]{:S(2)}, u32[]{:S(2)}) collective-permute-start(f32[96,256]{1,0:T(8,128)S(1)} %get-tuple-element.57), channel_id=1, source_target_pairs={{0,3},{1,2},{2,1},{3,0},{4,7},{5,6},{6,5},{7,4},{8,11},{9,10},{10,... | collective-permute-start | bytes 294920 | tf_op jit(solution)/shard_map/ppermute | solution.py:456

commit v6 on v5

--- a/solution.py
+++ b/solution.py
@@ -19,12 +19,12 @@
 PARTS = 4
 ROWS = PIX // PARTS
 CHUNKS = (0, 1)
-LOW = (32, 0)
-MAIN = (32, 32)
-FOLD_LOW = (32, 16)
-FOLD = (32, 16)
-COLS = (64, 48)
-EXT = (32, 40)
+LOW = (24, 0)
+MAIN = (40, 24)
+FOLD_LOW = (24, 16)
+FOLD = (40, 8)
+COLS = (80, 32)
+EXT = (40, 32)
 ORDERS = (0, 1, -1, 2, -2)
 ARC = (
     1.5707963050,
@@ -389,20 +389,27 @@
 
 
 def gathered(blocks):
-    return split(jnp.concatenate([b[...] for b in blocks], axis=0))
-
-
-def part_kernel(got0, got1, got2, got3, final_hi, final_lo, part):
+    return split(jnp.concatenate([b[...] for b in blocks], axis=0).T)
+
+
+NEAR = 4 * COLS[1]
+
+
+def part_kernel(got0, got1, got2, got3, near0, near1, hi0, lo0, hi1, lo1, part):
     data = gathered((got0, got1, got2, got3))
-    part[...] = dot3(data, (final_hi[...], final_lo[...]), (0, 0))
-
-
-def final_kernel(got0, got1, got2, got3, final_hi, final_lo, part, out, woven, sems):
-    data = gathered((got0, got1, got2, got3))
+    near = gathered((near0, near1))
+    part[...] = dot3(data, (hi0[...], lo0[...]), (1, 0)) + dot3(
+        near, (hi1[:NEAR], lo1[:NEAR]), (1, 0)
+    )
+
+
+def final_kernel(got2, got3, final_hi, final_lo, part, out, woven, sems):
+    data = gathered((got2, got3))
     copies = []
     for strip in range(GRID // 256):
         lanes = slice(256 * strip, 256 * (strip + 1))
-        picture = part[:, lanes] + dot3(data, (final_hi[:, lanes], final_lo[:, lanes]), (0, 0))
+        table = (final_hi[NEAR:, lanes], final_lo[NEAR:, lanes])
+        picture = part[:, lanes] + dot3(data, table, (1, 0))
         for block in range(2):
             at = 2 * strip + block
             piece = slice(128 * block, 128 * (block + 1))
@@ -512,17 +519,19 @@
         [bf16(8 * COLS[c], GRID) for c in CHUNKS] * 2,
         [smem()] + [vmem()] * 2,
     )(place, first, after)
-    part = call(part_kernel, f32(2 * ROWS, GRID), [vmem()] * 6)(*got[0], hi0, lo0)
+    part = call(part_kernel, f32(2 * ROWS, GRID), [vmem()] * 10)(
+        *got[0], *got[1][:2], hi0, lo0, hi1, lo1
+    )
     return call(
         final_kernel,
         f32(2 * ROWS, GRID),
-        [vmem()] * 7,
+        [vmem()] * 5,
         hbm(),
         [
             pltpu.VMEM((GRID // 128, 2 * ROWS, 128), jnp.float32),
             pltpu.SemaphoreType.DMA((GRID // 128,)),
         ],
-    )(*got[1], hi1, lo1, part)
+    )(*got[1][2:], hi1, lo1, part)
 
 
 def solution(mesh):

time: 44.9 us -> 44.9 us (level)
  waiting for transfers between devices: 3.31 us -> 2.1 us
  starting transfers between devices: 21.9 us -> 22.8 us
    ppermute x15, waiting for transfers between devices: 3.31 us -> 2.1 us  [from_partners(): lax.ppermute(blocks[k], 'row', [(i, i ^ k) for i in range(PARTS)])]
    ppermute x15, starting transfers between devices: 21.9 us -> 22.8 us  [from_partners(): lax.ppermute(blocks[k], 'row', [(i, i ^ k) for i in range(PARTS)])]
  transfers between devices with their start and end apart: 15 -> 15, of which waited for: 1 -> 2; matrix products, arithmetic and copies ran while one was open for 0% -> 0% of each run, Pallas kernels for 32% -> 33%
where the time goes in v6:
time: 44.9 us; the launch traced here: 44.7 us
  starting transfers between devices  22.8 us (51%)
  Pallas kernels  17.5 us (39%)
  waiting for transfers between devices  2.1 us (5%)
  other arithmetic  1.3 us (3%)
  between operations  1.01 us (2%)
    ppermute x15, starting transfers between devices, from_partners(): lax.ppermute(blocks[k], 'row', [(i, i ^ k) for i in range(PARTS)])  22.8 us
    pallas_call x2, Pallas kernels, reconstruct(): call(functools.partial(middle_kernel, c), [f32(2 * COLS[c], 2 * ROWS)] *...  5.26 us
    pallas_call x2, Pallas kernels, reconstruct(): call(functools.partial(weights_kernel, c), f32(5, 2, COLS[c], PIX), [smem...  3.46 us
    ppermute x15, waiting for transfers between devices, from_partners(): lax.ppermute(blocks[k], 'row', [(i, i ^ k) for i in range(PARTS)])  2.1 us
    pallas_call x1, Pallas kernels, reconstruct(): call(forward_rest_kernel, [blocks[0]] * 2 + [blocks[1]] * PARTS + [bf16(P...  1.82 us
    pallas_call x1, Pallas kernels, reconstruct(): call(phase_kernel, [bf16(PHASES, ROWS, PIX), f32(4, ROWS, PIX), f32(4, 8,...  1.65 us
    pallas_call x1, Pallas kernels, reconstruct(): call(part_kernel, f32(2 * ROWS, GRID), [vmem()] * 10)  1.56 us
    pallas_call x1, Pallas kernels, reconstruct(): call(final_kernel, f32(2 * ROWS, GRID), [vmem()] * 5, hbm(), [pltpu.VMEM(...  1.38 us
  transfers between devices with their start and end apart: 15, of which 2 were waited for; matrix products, arithmetic and copies ran while one was open for 0% of the time, Pallas kernels for 33%

profile of v6, /device:TPU:1, one launch (start us, length us, event | category | flops | bytes accessed | tf_op | source)
XLA Modules:
  0.0 44.7 jit_solution(6704428351849943903)
XLA Ops:
  0.0 1.3 %convert_reduce_fusion = f32[5]{0:T(128)S(1)} fusion(bf16[1,5,128,512]{3,2,1,0:T(8,128)(2,1)} %source.1), kind=kLoop, calls=%fused_computation | loop fusion | flops 655355 | bytes 655380 | tf_op jit(solution)/shard_map/reduce_sum | solution.py:472
  1.3 4.3 %collective-permute-start.2 = (f32[1,5]{1,0:T(1,128)S(1)}, f32[1,5]{1,0:T(1,128)S(1)}, u32[]{:S(2)}, u32[]{:S(2)}) collective-permute-start(f32[1,5]{1,0:T(1,128)S(1)} %bitcast.2), channel_id=1, source_target_pairs={{0,3},{1,2},{2,1},{3,0},{4,7},{5,6},{6,5},{7,4},{8,11},{9,10},{10,... | collective-permute-start | bytes 68 | tf_op jit(solution)/shard_map/ppermute | solution.py:463
  5.6 1.8 %collective-permute-start.1 = (f32[1,5]{1,0:T(1,128)S(1)}, f32[1,5]{1,0:T(1,128)S(1)}, u32[]{:S(2)}, u32[]{:S(2)}) collective-permute-start(f32[1,5]{1,0:T(1,128)S(1)} %bitcast.3), channel_id=1, source_target_pairs={{0,2},{1,3},{2,0},{3,1},{4,6},{5,7},{6,4},{7,5},{8,10},{9,11},{10,... | collective-permute-start | bytes 68 | tf_op jit(solution)/shard_map/ppermute | solution.py:463
  7.4 0.0 collective-permute-start
  8.1 1.7 %shard_map.73 = (bf16[5,128,512]{2,1,0:T(8,128)(2,1)S(1)}, f32[4,128,512]{2,1,0:T(8,128)S(1)}, f32[4,8,128]{2,1,0:T(8,128)S(1)}, bf16[2,2,128,512]{3,2,1,0:T(8,1...) custom-call(s32[1]{0:T(128)} %bitcast.place, f32[1]{0:T(128)S(6)} %copy.8.offset, ...), custom_call_target="tpu_custom_call" | custom-call | tf_op jit(solution)/shard_map/pallas_call | solution.py:475
  9.7 0.0 collective-permute-done.2.sums3
  9.7 0.0 collective-permute-done.1.sums2
  9.7 0.0 collective-permute-done.sums1
  9.8 1.3 %shard_map.74 = (f32[5,80,128]{2,1,0:T(8,128)S(1)}, f32[5,80,128]{2,1,0:T(8,128)S(1)}, bf16[640,512]{1,0:T(8,128)(2,1)S(1)}, bf16[640,512]{1,0:T(8,128)(2,1)S(1)}) custom-call(s32[1]{0:T(128)} %bitcast.place, f32[1,5]{1,0:T(1,128)S(1)} %bitcast.5, f32[1,5]{1,0:T(1,128)S(1)} %collective-permute-done.sums1, f32[1,5]{1,0:T(1,128)S(1)} %collective-permute-done.1.sums2, ...), custom_call_target="tpu_custom_call" | custom-call | tf_op jit(solution)/shard_map/pallas_call | solution.py:489
  11.0 0.0 copy-start.2
  11.0 0.0 copy-start.3
  11.0 1.7 %collective-permute-start.7 = (f32[5,80,128]{2,1,0:T(8,128)S(1)}, f32[5,80,128]{2,1,0:T(8,128)S(1)}, u32[]{:S(2)}, u32[]{:S(2)}) collective-permute-start(f32[5,80,128]{2,1,0:T(8,128)S(1)} %get-tuple-element.49), channel_id=1, source_target_pairs={{0,2},{1,3},{2,0},{3,1},{4,6},{5,7},{6,4},{7,5},{8,10},{9,11},{10,... | collective-permute-start | bytes 614408 | tf_op jit(solution)/shard_map/ppermute | solution.py:463
  12.7 2.4 %collective-permute-start.8 = (f32[5,80,128]{2,1,0:T(8,128)S(1)}, f32[5,80,128]{2,1,0:T(8,128)S(1)}, u32[]{:S(2)}, u32[]{:S(2)}) collective-permute-start(f32[5,80,128]{2,1,0:T(8,128)S(1)} %get-tuple-element.50), channel_id=1, source_target_pairs={{0,3},{1,2},{2,1},{3,0},{4,7},{5,6},{6,5},{7,4},{8,11},{9,10},{10,... | collective-permute-start | bytes 614408 | tf_op jit(solution)/shard_map/ppermute | solution.py:463
  15.1 1.8 %shard_map.75 = (f32[5,80,128]{2,1,0:T(8,128)S(1)}, f32[5,80,128]{2,1,0:T(8,128)S(1)}, f32[5,48,128]{2,1,0:T(8,128)S(1)}, f32[5,48,128]{2,1,0:T(8,128)S(1)}, f32...) custom-call(s32[1]{0:T(128)} %bitcast.place, ...), custom_call_target="tpu_custom_call" | custom-call | tf_op jit(solution)/shard_map/pallas_call | solution.py:494
  16.9 0.0 copy-start.1
  16.9 0.1 collective-permute-start.6
  17.0 0.5 %collective-permute-start.3 = (f32[5,48,128]{2,1,0:T(8,128)S(1)}, f32[5,48,128]{2,1,0:T(8,128)S(1)}, u32[]{:S(2)}, u32[]{:S(2)}) collective-permute-start(f32[5,48,128]{2,1,0:T(8,128)S(1)} %get-tuple-element.44), channel_id=1, source_target_pairs={{0,1},{1,0},{2,3},{3,2},{4,5},{5,4},{6,7},{7,6},{8,9},{9,8},{10,11... | collective-permute-start | bytes 368648 | tf_op jit(solution)/shard_map/ppermute | solution.py:463
  17.5 0.9 %collective-permute-start.4 = (f32[5,48,128]{2,1,0:T(8,128)S(1)}, f32[5,48,128]{2,1,0:T(8,128)S(1)}, u32[]{:S(2)}, u32[]{:S(2)}) collective-permute-start(f32[5,48,128]{2,1,0:T(8,128)S(1)} %get-tuple-element.45), channel_id=1, source_target_pairs={{0,2},{1,3},{2,0},{3,1},{4,6},{5,7},{6,4},{7,5},{8,10},{9,11},{10,... | collective-permute-start | bytes 368648 | tf_op jit(solution)/shard_map/ppermute | solution.py:463
  18.4 0.0 collective-permute-done.7.got2
  18.5 3.7 %collective-permute-start.5 = (f32[5,48,128]{2,1,0:T(8,128)S(1)}, f32[5,48,128]{2,1,0:T(8,128)S(1)}, u32[]{:S(2)}, u32[]{:S(2)}) collective-permute-start(f32[5,48,128]{2,1,0:T(8,128)S(1)} %get-tuple-element.46), channel_id=1, source_target_pairs={{0,3},{1,2},{2,1},{3,0},{4,7},{5,6},{6,5},{7,4},{8,11},{9,10},{10,... | collective-permute-start | bytes 368648 | tf_op jit(solution)/shard_map/ppermute | solution.py:463
  22.2 0.0 copy-done.2
  22.2 0.0 copy-done.3
  22.2 2.2 %shard_map.76.weights = f32[5,2,80,512]{3,2,1,0:T(8,128)S(1)} custom-call(s32[1]{0:T(128)} %bitcast.place, f32[1,5]{1,0:T(1,128)S(1)} %copy-done.3, s32[1,2]{1,0:T(1,128)S(1)} %copy-done.2, f32[5,80,128]{2,1,0:T(8,128)S(1)} %get-tuple-element.47.after.got0), custom_call_target="tpu_custom_call" | custom-call | tf_op jit(solution)/shard_map/pallas_call | solution.py:504
  24.4 0.7 %collective-permute-done.8.got3 = f32[5,80,128]{2,1,0:T(8,128)S(1)} collective-permute-done((f32[5,80,128]{2,1,0:T(8,128)S(1)}, f32[5,80,128]{2,1,0:T(8,128)S(1)}, u32[]{:S(2)}, u32[]{:S(2)}) %collective-permute-start.8) | collective-permute-done | bytes 204832 | tf_op jit(solution)/shard_map/ppermute | solution.py:463
  25.1 0.0 collective-permute-done.6.got1
  25.1 2.9 %shard_map.77 = (f32[160,256]{1,0:T(8,128)S(1)}, f32[160,256]{1,0:T(8,128)S(1)}, f32[160,256]{1,0:T(8,128)S(1)}, f32[160,256]{1,0:T(8,128)S(1)}) custom-call(s32[1]{0:T(128)} %bitcast.place, f32[5,80,128]{2,1,0:T(8,128)S(1)} %get-tuple-element.47.after.got0, f32[5,80,128]{2,1,0:T(8,128)S(1)} %collective-permute-done.6.got1, ...), custom_call_target="tpu_custom_call" | custom-call | tf_op jit(solution)/shard_map/pallas_call | solution.py:510
  28.0 0.1 collective-permute-start.11
  28.1 1.5 %collective-permute-start.12 = (f32[160,256]{1,0:T(8,128)S(1)}, f32[160,256]{1,0:T(8,128)S(1)}, u32[]{:S(2)}, u32[]{:S(2)}) collective-permute-start(f32[160,256]{1,0:T(8,128)S(1)} %get-tuple-element.60), channel_id=1, source_target_pairs={{0,2},{1,3},{2,0},{3,1},{4,6},{5,7},{6,4},{7,5},{8,10},{9,11},{10,... | collective-permute-start | bytes 491528 | tf_op jit(solution)/shard_map/ppermute | solution.py:463
  29.6 0.0 collective-permute-done.3.got1
  29.6 2.1 %collective-permute-start.13 = (f32[160,256]{1,0:T(8,128)S(1)}, f32[160,256]{1,0:T(8,128)S(1)}, u32[]{:S(2)}, u32[]{:S(2)}) collective-permute-start(f32[160,256]{1,0:T(8,128)S(1)} %get-tuple-element.61), channel_id=1, source_target_pairs={{0,3},{1,2},{2,1},{3,0},{4,7},{5,6},{6,5},{7,4},{8,11},{9,10},{10,... | collective-permute-start | bytes 491528 | tf_op jit(solution)/shard_map/ppermute | solution.py:463
  31.8 1.2 %shard_map.78.weights = f32[5,2,32,512]{3,2,1,0:T(8,128)S(1)} custom-call(s32[1]{0:T(128)} %bitcast.place, f32[1,5]{1,0:T(1,128)S(1)} %copy-done.3, s32[1,2]{1,0:T(1,128)S(1)} %copy-done.2, f32[160,256]{1,0:T(8,128)S(1)} %get-tuple-element.53.after.got0), custom_call_target="tpu_custom_call" | custom-call | tf_op jit(solution)/shard_map/pallas_call | solution.py:504
  33.0 0.0 collective-permute-done.4.got2
  33.0 0.0 collective-permute-done.5.got3
  33.0 0.0 copy-start
  33.1 2.3 %shard_map.79 = (f32[64,256]{1,0:T(8,128)S(1)}, f32[64,256]{1,0:T(8,128)S(1)}, f32[64,256]{1,0:T(8,128)S(1)}, f32[64,256]{1,0:T(8,128)S(1)}) custom-call(s32[1]{0:T(128)} %bitcast.place, f32[5,48,128]{2,1,0:T(8,128)S(1)} %get-tuple-element.43.got0, f32[5,48,128]{2,1,0:T(8,128)S(1)} %collective-permute-done.3.got1, ...), custom_call_target="tpu_custom_call" | custom-call | tf_op jit(solution)/shard_map/pallas_call | solution.py:510
  35.4 0.1 collective-permute-start.14
  35.5 1.5 %collective-permute-start.9 = (f32[64,256]{1,0:T(8,128)S(1)}, f32[64,256]{1,0:T(8,128)S(1)}, u32[]{:S(2)}, u32[]{:S(2)}) collective-permute-start(f32[64,256]{1,0:T(8,128)S(1)} %get-tuple-element.54), channel_id=1, source_target_pairs={{0,2},{1,3},{2,0},{3,1},{4,6},{5,7},{6,4},{7,5},{8,10},{9,11},{10,... | collective-permute-start | bytes 196616 | tf_op jit(solution)/shard_map/ppermute | solution.py:463
  37.0 0.0 collective-permute-done.14.near1
  37.0 2.1 %collective-permute-start.10 = (f32[64,256]{1,0:T(8,128)S(1)}, f32[64,256]{1,0:T(8,128)S(1)}, u32[]{:S(2)}, u32[]{:S(2)}) collective-permute-start(f32[64,256]{1,0:T(8,128)S(1)} %get-tuple-element.55), channel_id=1, source_target_pairs={{0,3},{1,2},{2,1},{3,0},{4,7},{5,6},{6,5},{7,4},{8,11},{9,10},{10,... | collective-permute-start | bytes 196616 | tf_op jit(solution)/shard_map/ppermute | solution.py:463
  39.1 0.0 copy-done
  39.1 1.1 %shard_map.80 = (bf16[640,1024]{1,0:T(8,128)(2,1)S(1)}, bf16[256,1024]{1,0:T(8,128)(2,1)S(1)}, bf16[640,1024]{1,0:T(8,128)(2,1)S(1)}, bf16[256,1024]{1,0:T(8,128)(2,1)S(1)}) custom-call(s32[1]{0:T(128)} %bitcast.place, f32[4,2,112,128]{3,2,1,0:T(8,128)S(1)} %copy-done, f32[64,256]{1,0:T(8,128)S(1)} %get-tuple-element.56.after.near0), custom_call_target="tpu_custom_call" | custom-call | tf_op jit(solution)/shard_map/pallas_call | solution.py:517
  40.2 0.0 collective-permute-done.11.got1
  40.2 0.0 collective-permute-done.12.got2
  40.2 0.0 collective-permute-done.13.got3
  40.2 1.6 %shard_map.81.part = f32[256,1024]{1,0:T(8,128)S(1)} custom-call(f32[160,256]{1,0:T(8,128)S(1)} %get-tuple-element.53.after.got0, f32[160,256]{1,0:T(8,128)S(1)} %collective-permute-done.11.got1, f32[160,256]{1,0:T(8,128)S(1)} %collective-permute-done.12.got2, f32[160,256]{1,0:T(8,128)S(1)} %collective-permute-done.13.got3, ...), custom_call_target="tpu_custom_call" | custom-call | tf_op jit(solution)/shard_map/pallas_call | solution.py:522
  41.8 0.0 collective-permute-done.9.got2
  41.8 1.4 %collective-permute-done.10.got3 = f32[64,256]{1,0:T(8,128)S(1)} collective-permute-done((f32[64,256]{1,0:T(8,128)S(1)}, f32[64,256]{1,0:T(8,128)S(1)}, u32[]{:S(2)}, u32[]{:S(2)}) %collective-permute-start.10) | collective-permute-done | bytes 65568 | tf_op jit(solution)/shard_map/ppermute | solution.py:463
  43.2 1.4 %shard_map.82 = f32[256,1024]{1,0:T(8,128)} custom-call(f32[64,256]{1,0:T(8,128)S(1)} %collective-permute-done.9.got2, f32[64,256]{1,0:T(8,128)S(1)} %collective-permute-done.10.got3, bf16[256,1024]{1,0:T(8,128)(2,1)S(1)} %get-tuple-element.57.hi1.final_hi, bf16[256,1024]{1,0:T(8,128)(2,1)S(1)} %get-tuple-element.58.lo1.final_lo, f32[256,1024]{1,0:T(8,128)S(1)} %shard_map.81.part), custom_call_target="tpu_custom_call" | custom-call | tf_op jit(solution)/shard_map/pallas_call | solution.py:525
  (1 shorter events, 0.0 us)
Async XLA Ops:
  1.3 8.4 %collective-permute-start.2 = (f32[1,5]{1,0:T(1,128)S(1)}, f32[1,5]{1,0:T(1,128)S(1)}, u32[]{:S(2)}, u32[]{:S(2)}) collective-permute-start(f32[1,5]{1,0:T(1,128)S(1)} %bitcast.2), channel_id=1, source_target_pairs={{0,3},{1,2},{2,1},{3,0},{4,7},{5,6},{6,5},{7,4},{8,11},{9,10},{10,... | collective-permute-start | bytes 68 | tf_op jit(solution)/shard_map/ppermute | solution.py:463
  5.6 4.1 %collective-permute-start.1 = (f32[1,5]{1,0:T(1,128)S(1)}, f32[1,5]{1,0:T(1,128)S(1)}, u32[]{:S(2)}, u32[]{:S(2)}) collective-permute-start(f32[1,5]{1,0:T(1,128)S(1)} %bitcast.3), channel_id=1, source_target_pairs={{0,2},{1,3},{2,0},{3,1},{4,6},{5,7},{6,4},{7,5},{8,10},{9,11},{10,... | collective-permute-start | bytes 68 | tf_op jit(solution)/shard_map/ppermute | solution.py:463
  7.4 2.3 %collective-permute-start = (f32[1,5]{1,0:T(1,128)S(1)}, f32[1,5]{1,0:T(1,128)S(1)}, u32[]{:S(2)}, u32[]{:S(2)}) collective-permute-start(f32[1,5]{1,0:T(1,128)S(1)} %bitcast.4), channel_id=1, source_target_pairs={{0,1},{1,0},{2,3},{3,2},{4,5},{5,4},{6,7},{7,6},{8,9},{9,8},{10,11... | collective-permute-start | bytes 68 | tf_op jit(solution)/shard_map/ppermute | solution.py:463
  11.0 11.2 %copy-start.2 = (s32[1,2]{1,0:T(1,128)S(1)}, s32[1,2]{1,0:T(1,128)}, u32[]{:S(2)}) copy-start(s32[1,2]{1,0:T(1,128)} %shift.3) | copy-start | bytes 28
  11.0 11.2 %copy-start.3 = (f32[1,5]{1,0:T(1,128)S(1)}, f32[1,5]{1,0:T(1,128)}, u32[]{:S(2)}) copy-start(f32[1,5]{1,0:T(1,128)} %gains.3) | copy-start | bytes 64
  11.0 7.4 %collective-permute-start.7 = (f32[5,80,128]{2,1,0:T(8,128)S(1)}, f32[5,80,128]{2,1,0:T(8,128)S(1)}, u32[]{:S(2)}, u32[]{:S(2)}) collective-permute-start(f32[5,80,128]{2,1,0:T(8,128)S(1)} %get-tuple-element.49), channel_id=1, source_target_pairs={{0,2},{1,3},{2,0},{3,1},{4,6},{5,7},{6,4},{7,5},{8,10},{9,11},{10,... | collective-permute-start | bytes 614408 | tf_op jit(solution)/shard_map/ppermute | solution.py:463
  12.7 12.4 %collective-permute-start.8 = (f32[5,80,128]{2,1,0:T(8,128)S(1)}, f32[5,80,128]{2,1,0:T(8,128)S(1)}, u32[]{:S(2)}, u32[]{:S(2)}) collective-permute-start(f32[5,80,128]{2,1,0:T(8,128)S(1)} %get-tuple-element.50), channel_id=1, source_target_pairs={{0,3},{1,2},{2,1},{3,0},{4,7},{5,6},{6,5},{7,4},{8,11},{9,10},{10,... | collective-permute-start | bytes 614408 | tf_op jit(solution)/shard_map/ppermute | solution.py:463
  16.9 8.2 %copy-start.1 = (f32[2,512]{1,0:T(2,128)S(1)}, f32[2,512]{1,0:T(2,128)}, u32[]{:S(2)}) copy-start(f32[2,512]{1,0:T(2,128)} %constant.13.clone.odd) | copy-start | bytes 12292
  16.9 8.2 %collective-permute-start.6 = (f32[5,80,128]{2,1,0:T(8,128)S(1)}, f32[5,80,128]{2,1,0:T(8,128)S(1)}, u32[]{:S(2)}, u32[]{:S(2)}) collective-permute-start(f32[5,80,128]{2,1,0:T(8,128)S(1)} %get-tuple-element.48), channel_id=1, source_target_pairs={{0,1},{1,0},{2,3},{3,2},{4,5},{5,4},{6,7},{7,6},{8,9},{9,8},{10,11... | collective-permute-start | bytes 614408 | tf_op jit(solution)/shard_map/ppermute | solution.py:463
  17.0 12.6 %collective-permute-start.3 = (f32[5,48,128]{2,1,0:T(8,128)S(1)}, f32[5,48,128]{2,1,0:T(8,128)S(1)}, u32[]{:S(2)}, u32[]{:S(2)}) collective-permute-start(f32[5,48,128]{2,1,0:T(8,128)S(1)} %get-tuple-element.44), channel_id=1, source_target_pairs={{0,1},{1,0},{2,3},{3,2},{4,5},{5,4},{6,7},{7,6},{8,9},{9,8},{10,11... | collective-permute-start | bytes 368648 | tf_op jit(solution)/shard_map/ppermute | solution.py:463
  17.5 15.5 %collective-permute-start.4 = (f32[5,48,128]{2,1,0:T(8,128)S(1)}, f32[5,48,128]{2,1,0:T(8,128)S(1)}, u32[]{:S(2)}, u32[]{:S(2)}) collective-permute-start(f32[5,48,128]{2,1,0:T(8,128)S(1)} %get-tuple-element.45), channel_id=1, source_target_pairs={{0,2},{1,3},{2,0},{3,1},{4,6},{5,7},{6,4},{7,5},{8,10},{9,11},{10,... | collective-permute-start | bytes 368648 | tf_op jit(solution)/shard_map/ppermute | solution.py:463
  18.5 14.6 %collective-permute-start.5 = (f32[5,48,128]{2,1,0:T(8,128)S(1)}, f32[5,48,128]{2,1,0:T(8,128)S(1)}, u32[]{:S(2)}, u32[]{:S(2)}) collective-permute-start(f32[5,48,128]{2,1,0:T(8,128)S(1)} %get-tuple-element.46), channel_id=1, source_target_pairs={{0,3},{1,2},{2,1},{3,0},{4,7},{5,6},{6,5},{7,4},{8,11},{9,10},{10,... | collective-permute-start | bytes 368648 | tf_op jit(solution)/shard_map/ppermute | solution.py:463
  28.0 12.2 %collective-permute-start.11 = (f32[160,256]{1,0:T(8,128)S(1)}, f32[160,256]{1,0:T(8,128)S(1)}, u32[]{:S(2)}, u32[]{:S(2)}) collective-permute-start(f32[160,256]{1,0:T(8,128)S(1)} %get-tuple-element.59), channel_id=1, source_target_pairs={{0,1},{1,0},{2,3},{3,2},{4,5},{5,4},{6,7},{7,6},{8,9},{9,8},{10,11... | collective-permute-start | bytes 491528 | tf_op jit(solution)/shard_map/ppermute | solution.py:463
  28.1 12.1 %collective-permute-start.12 = (f32[160,256]{1,0:T(8,128)S(1)}, f32[160,256]{1,0:T(8,128)S(1)}, u32[]{:S(2)}, u32[]{:S(2)}) collective-permute-start(f32[160,256]{1,0:T(8,128)S(1)} %get-tuple-element.60), channel_id=1, source_target_pairs={{0,2},{1,3},{2,0},{3,1},{4,6},{5,7},{6,4},{7,5},{8,10},{9,11},{10,... | collective-permute-start | bytes 491528 | tf_op jit(solution)/shard_map/ppermute | solution.py:463
  29.6 10.6 %collective-permute-start.13 = (f32[160,256]{1,0:T(8,128)S(1)}, f32[160,256]{1,0:T(8,128)S(1)}, u32[]{:S(2)}, u32[]{:S(2)}) collective-permute-start(f32[160,256]{1,0:T(8,128)S(1)} %get-tuple-element.61), channel_id=1, source_target_pairs={{0,3},{1,2},{2,1},{3,0},{4,7},{5,6},{6,5},{7,4},{8,11},{9,10},{10,... | collective-permute-start | bytes 491528 | tf_op jit(solution)/shard_map/ppermute | solution.py:463
  33.0 6.1 %copy-start = (f32[4,2,112,128]{3,2,1,0:T(8,128)S(1)}, f32[4,2,112,128]{3,2,1,0:T(8,128)}, u32[]{:S(2)}) copy-start(f32[4,2,112,128]{3,2,1,0:T(8,128)} %constant.14.clone.first) | copy-start | bytes 1376260
  35.4 1.6 %collective-permute-start.14 = (f32[64,256]{1,0:T(8,128)S(1)}, f32[64,256]{1,0:T(8,128)S(1)}, u32[]{:S(2)}, u32[]{:S(2)}) collective-permute-start(f32[64,256]{1,0:T(8,128)S(1)} %get-tuple-element.62), channel_id=1, source_target_pairs={{0,1},{1,0},{2,3},{3,2},{4,5},{5,4},{6,7},{7,6},{8,9},{9,8},{10,11... | collective-permute-start | bytes 196616 | tf_op jit(solution)/shard_map/ppermute | solution.py:463
  35.5 6.3 %collective-permute-start.9 = (f32[64,256]{1,0:T(8,128)S(1)}, f32[64,256]{1,0:T(8,128)S(1)}, u32[]{:S(2)}, u32[]{:S(2)}) collective-permute-start(f32[64,256]{1,0:T(8,128)S(1)} %get-tuple-element.54), channel_id=1, source_target_pairs={{0,2},{1,3},{2,0},{3,1},{4,6},{5,7},{6,4},{7,5},{8,10},{9,11},{10,... | collective-permute-start | bytes 196616 | tf_op jit(solution)/shard_map/ppermute | solution.py:463
  37.0 6.2 %collective-permute-start.10 = (f32[64,256]{1,0:T(8,128)S(1)}, f32[64,256]{1,0:T(8,128)S(1)}, u32[]{:S(2)}, u32[]{:S(2)}) collective-permute-start(f32[64,256]{1,0:T(8,128)S(1)} %get-tuple-element.55), channel_id=1, source_target_pairs={{0,3},{1,2},{2,1},{3,0},{4,7},{5,6},{6,5},{7,4},{8,11},{9,10},{10,... | collective-permute-start | bytes 196616 | tf_op jit(solution)/shard_map/ppermute | solution.py:463

commit v7 on v6

--- a/solution.py
+++ b/solution.py
@@ -19,12 +19,12 @@
 PARTS = 4
 ROWS = PIX // PARTS
 CHUNKS = (0, 1)
-LOW = (24, 0)
-MAIN = (40, 24)
-FOLD_LOW = (24, 16)
-FOLD = (40, 8)
-COLS = (80, 32)
-EXT = (40, 32)
+LOW = (32, 0)
+MAIN = (32, 32)
+FOLD_LOW = (32, 16)
+FOLD = (32, 16)
+COLS = (64, 48)
+EXT = (32, 40)
 ORDERS = (0, 1, -1, 2, -2)
 ARC = (
     1.5707963050,
@@ -278,7 +278,7 @@
 
         return carry
 
-    lax.fori_loop(0, COLS[chunk] // 8, tile_step, 0, unroll=2)
+    lax.fori_loop(0, COLS[chunk] // 8, tile_step, 0, unroll=4 - chunk)
 
 
 def table_kernel(place, first, after, hi0, hi1, lo0, lo1):

time: 44.9 us -> 48.1 us (1.071)
  waiting for transfers between devices: 2.1 us -> 6.45 us
  starting transfers between devices: 22.8 us -> 21.6 us
    ppermute x15, waiting for transfers between devices: 2.1 us -> 6.45 us  [from_partners(): lax.ppermute(blocks[k], 'row', [(i, i ^ k) for i in range(PARTS)])]
    ppermute x15, starting transfers between devices: 22.8 us -> 21.6 us  [from_partners(): lax.ppermute(blocks[k], 'row', [(i, i ^ k) for i in range(PARTS)])]
  transfers between devices with their start and end apart: 15 -> 15, of which waited for: 2 -> 3; matrix products, arithmetic and copies ran while one was open for 0% -> 0% of each run, Pallas kernels for 33% -> 25%
where the time goes in v7:
time: 48.1 us; the launch traced here: 47.9 us
  starting transfers between devices  21.6 us (45%)
  Pallas kernels  17.6 us (37%)
  waiting for transfers between devices  6.45 us (13%)
  other arithmetic  1.3 us (3%)
  between operations  1 us (2%)
    ppermute x15, starting transfers between devices, from_partners(): lax.ppermute(blocks[k], 'row', [(i, i ^ k) for i in range(PARTS)])  21.6 us
    ppermute x15, waiting for transfers between devices, from_partners(): lax.ppermute(blocks[k], 'row', [(i, i ^ k) for i in range(PARTS)])  6.45 us
    pallas_call x2, Pallas kernels, reconstruct(): call(functools.partial(middle_kernel, c), [f32(2 * COLS[c], 2 * ROWS)] *...  5.05 us
    pallas_call x2, Pallas kernels, reconstruct(): call(functools.partial(weights_kernel, c), f32(5, 2, COLS[c], PIX), [smem...  3.46 us
    pallas_call x1, Pallas kernels, reconstruct(): call(forward_rest_kernel, [blocks[0]] * 2 + [blocks[1]] * PARTS + [bf16(P...  1.88 us
    pallas_call x1, Pallas kernels, reconstruct(): call(final_kernel, f32(2 * ROWS, GRID), [vmem()] * 5, hbm(), [pltpu.VMEM(...  1.66 us
    pallas_call x1, Pallas kernels, reconstruct(): call(phase_kernel, [bf16(PHASES, ROWS, PIX), f32(4, ROWS, PIX), f32(4, 8,...  1.62 us
    pallas_call x1, Pallas kernels, reconstruct(): call(part_kernel, f32(2 * ROWS, GRID), [vmem()] * 10)  1.57 us
  transfers between devices with their start and end apart: 15, of which 3 were waited for; matrix products, arithmetic and copies ran while one was open for 0% of the time, Pallas kernels for 25%

profile of v7, /device:TPU:1, one launch (start us, length us, event | category | flops | bytes accessed | tf_op | source)
XLA Modules:
  0.0 47.9 jit_solution(1640346367360103218)
XLA Ops:
  0.0 1.3 %convert_reduce_fusion = f32[5]{0:T(128)S(1)} fusion(bf16[1,5,128,512]{3,2,1,0:T(8,128)(2,1)} %source.1), kind=kLoop, calls=%fused_computation | loop fusion | flops 655355 | bytes 655380 | tf_op jit(solution)/shard_map/reduce_sum | solution.py:472
  1.3 4.3 %collective-permute-start.2 = (f32[1,5]{1,0:T(1,128)S(1)}, f32[1,5]{1,0:T(1,128)S(1)}, u32[]{:S(2)}, u32[]{:S(2)}) collective-permute-start(f32[1,5]{1,0:T(1,128)S(1)} %bitcast.2), channel_id=1, source_target_pairs={{0,3},{1,2},{2,1},{3,0},{4,7},{5,6},{6,5},{7,4},{8,11},{9,10},{10,... | collective-permute-start | bytes 68 | tf_op jit(solution)/shard_map/ppermute | solution.py:463
  5.6 1.8 %collective-permute-start.1 = (f32[1,5]{1,0:T(1,128)S(1)}, f32[1,5]{1,0:T(1,128)S(1)}, u32[]{:S(2)}, u32[]{:S(2)}) collective-permute-start(f32[1,5]{1,0:T(1,128)S(1)} %bitcast.3), channel_id=1, source_target_pairs={{0,2},{1,3},{2,0},{3,1},{4,6},{5,7},{6,4},{7,5},{8,10},{9,11},{10,... | collective-permute-start | bytes 68 | tf_op jit(solution)/shard_map/ppermute | solution.py:463
  7.4 0.0 collective-permute-start
  8.1 1.6 %shard_map.73 = (bf16[5,128,512]{2,1,0:T(8,128)(2,1)S(1)}, f32[4,128,512]{2,1,0:T(8,128)S(1)}, f32[4,8,128]{2,1,0:T(8,128)S(1)}, bf16[2,2,128,512]{3,2,1,0:T(8,1...) custom-call(s32[1]{0:T(128)} %bitcast.place, f32[1]{0:T(128)S(6)} %copy.8.offset, ...), custom_call_target="tpu_custom_call" | custom-call | tf_op jit(solution)/shard_map/pallas_call | solution.py:475
  9.7 0.0 collective-permute-done.2.sums3
  9.7 0.0 collective-permute-done.1.sums2
  9.7 0.0 collective-permute-done.sums1
  9.7 1.3 %shard_map.74 = (f32[5,64,128]{2,1,0:T(8,128)S(1)}, f32[5,64,128]{2,1,0:T(8,128)S(1)}, bf16[640,512]{1,0:T(8,128)(2,1)S(1)}, bf16[640,512]{1,0:T(8,128)(2,1)S(1)}) custom-call(s32[1]{0:T(128)} %bitcast.place, f32[1,5]{1,0:T(1,128)S(1)} %bitcast.5, f32[1,5]{1,0:T(1,128)S(1)} %collective-permute-done.sums1, f32[1,5]{1,0:T(1,128)S(1)} %collective-permute-done.1.sums2, ...), custom_call_target="tpu_custom_call" | custom-call | tf_op jit(solution)/shard_map/pallas_call | solution.py:489
  11.0 0.0 copy-start.2
  11.0 0.0 copy-start.3
  11.0 1.7 %collective-permute-start.7 = (f32[5,64,128]{2,1,0:T(8,128)S(1)}, f32[5,64,128]{2,1,0:T(8,128)S(1)}, u32[]{:S(2)}, u32[]{:S(2)}) collective-permute-start(f32[5,64,128]{2,1,0:T(8,128)S(1)} %get-tuple-element.49), channel_id=1, source_target_pairs={{0,2},{1,3},{2,0},{3,1},{4,6},{5,7},{6,4},{7,5},{8,10},{9,11},{10,... | collective-permute-start | bytes 491528 | tf_op jit(solution)/shard_map/ppermute | solution.py:463
  12.7 2.4 %collective-permute-start.8 = (f32[5,64,128]{2,1,0:T(8,128)S(1)}, f32[5,64,128]{2,1,0:T(8,128)S(1)}, u32[]{:S(2)}, u32[]{:S(2)}) collective-permute-start(f32[5,64,128]{2,1,0:T(8,128)S(1)} %get-tuple-element.50), channel_id=1, source_target_pairs={{0,3},{1,2},{2,1},{3,0},{4,7},{5,6},{6,5},{7,4},{8,11},{9,10},{10,... | collective-permute-start | bytes 491528 | tf_op jit(solution)/shard_map/ppermute | solution.py:463
  15.1 1.9 %shard_map.75 = (f32[5,64,128]{2,1,0:T(8,128)S(1)}, f32[5,64,128]{2,1,0:T(8,128)S(1)}, f32[5,64,128]{2,1,0:T(8,128)S(1)}, f32[5,64,128]{2,1,0:T(8,128)S(1)}, f32...) custom-call(s32[1]{0:T(128)} %bitcast.place, ...), custom_call_target="tpu_custom_call" | custom-call | tf_op jit(solution)/shard_map/pallas_call | solution.py:494
  16.9 0.0 copy-start.1
  17.0 0.1 collective-permute-start.6
  17.1 0.5 %collective-permute-start.3 = (f32[5,64,128]{2,1,0:T(8,128)S(1)}, f32[5,64,128]{2,1,0:T(8,128)S(1)}, u32[]{:S(2)}, u32[]{:S(2)}) collective-permute-start(f32[5,64,128]{2,1,0:T(8,128)S(1)} %get-tuple-element.44), channel_id=1, source_target_pairs={{0,1},{1,0},{2,3},{3,2},{4,5},{5,4},{6,7},{7,6},{8,9},{9,8},{10,11... | collective-permute-start | bytes 491528 | tf_op jit(solution)/shard_map/ppermute | solution.py:463
  17.6 0.9 %collective-permute-start.4 = (f32[5,64,128]{2,1,0:T(8,128)S(1)}, f32[5,64,128]{2,1,0:T(8,128)S(1)}, u32[]{:S(2)}, u32[]{:S(2)}) collective-permute-start(f32[5,64,128]{2,1,0:T(8,128)S(1)} %get-tuple-element.45), channel_id=1, source_target_pairs={{0,2},{1,3},{2,0},{3,1},{4,6},{5,7},{6,4},{7,5},{8,10},{9,11},{10,... | collective-permute-start | bytes 491528 | tf_op jit(solution)/shard_map/ppermute | solution.py:463
  18.4 0.0 collective-permute-done.7.got2
  18.4 2.8 %collective-permute-start.5 = (f32[5,64,128]{2,1,0:T(8,128)S(1)}, f32[5,64,128]{2,1,0:T(8,128)S(1)}, u32[]{:S(2)}, u32[]{:S(2)}) collective-permute-start(f32[5,64,128]{2,1,0:T(8,128)S(1)} %get-tuple-element.46), channel_id=1, source_target_pairs={{0,3},{1,2},{2,1},{3,0},{4,7},{5,6},{6,5},{7,4},{8,11},{9,10},{10,... | collective-permute-start | bytes 491528 | tf_op jit(solution)/shard_map/ppermute | solution.py:463
  21.3 0.0 copy-done.2
  21.3 0.0 copy-done.3
  21.3 1.9 %shard_map.76.weights = f32[5,2,64,512]{3,2,1,0:T(8,128)S(1)} custom-call(s32[1]{0:T(128)} %bitcast.place, f32[1,5]{1,0:T(1,128)S(1)} %copy-done.3, s32[1,2]{1,0:T(1,128)S(1)} %copy-done.2, f32[5,64,128]{2,1,0:T(8,128)S(1)} %get-tuple-element.47.after.got0), custom_call_target="tpu_custom_call" | custom-call | tf_op jit(solution)/shard_map/pallas_call | solution.py:504
  23.2 0.0 collective-permute-done.8.got3
  23.2 0.0 collective-permute-done.6.got1
  23.2 0.0 copy-done.1
  23.2 2.4 %shard_map.77 = (f32[128,256]{1,0:T(8,128)S(1)}, f32[128,256]{1,0:T(8,128)S(1)}, f32[128,256]{1,0:T(8,128)S(1)}, f32[128,256]{1,0:T(8,128)S(1)}) custom-call(s32[1]{0:T(128)} %bitcast.place, f32[5,64,128]{2,1,0:T(8,128)S(1)} %get-tuple-element.47.after.got0, f32[5,64,128]{2,1,0:T(8,128)S(1)} %collective-permute-done.6.got1, ...), custom_call_target="tpu_custom_call" | custom-call | tf_op jit(solution)/shard_map/pallas_call | solution.py:510
  25.6 1.6 %shard_map.78.weights = f32[5,2,48,512]{3,2,1,0:T(8,128)S(1)} custom-call(s32[1]{0:T(128)} %bitcast.place, f32[1,5]{1,0:T(1,128)S(1)} %copy-done.3, s32[1,2]{1,0:T(1,128)S(1)} %copy-done.2, f32[128,256]{1,0:T(8,128)S(1)} %get-tuple-element.53.after.got0), custom_call_target="tpu_custom_call" | custom-call | tf_op jit(solution)/shard_map/pallas_call | solution.py:504
  27.2 0.0 collective-permute-done.3.got1
  27.2 0.0 collective-permute-done.4.got2
  27.2 1.9 %collective-permute-done.5.got3 = f32[5,64,128]{2,1,0:T(8,128)S(1)} collective-permute-done((f32[5,64,128]{2,1,0:T(8,128)S(1)}, f32[5,64,128]{2,1,0:T(8,128)S(1)}, u32[]{:S(2)}, u32[]{:S(2)}) %collective-permute-start.5) | collective-permute-done | bytes 163872 | tf_op jit(solution)/shard_map/ppermute | solution.py:463
  29.1 2.7 %shard_map.79 = (f32[96,256]{1,0:T(8,128)S(1)}, f32[96,256]{1,0:T(8,128)S(1)}, f32[96,256]{1,0:T(8,128)S(1)}, f32[96,256]{1,0:T(8,128)S(1)}) custom-call(s32[1]{0:T(128)} %bitcast.place, f32[5,64,128]{2,1,0:T(8,128)S(1)} %get-tuple-element.43.got0, f32[5,64,128]{2,1,0:T(8,128)S(1)} %collective-permute-done.3.got1, ...), custom_call_target="tpu_custom_call" | custom-call | tf_op jit(solution)/shard_map/pallas_call | solution.py:510
  31.7 0.2 collective-permute-start.14
  32.0 0.4 collective-permute-start.11
  32.3 1.6 %collective-permute-start.12 = (f32[128,256]{1,0:T(8,128)S(1)}, f32[128,256]{1,0:T(8,128)S(1)}, u32[]{:S(2)}, u32[]{:S(2)}) collective-permute-start(f32[128,256]{1,0:T(8,128)S(1)} %get-tuple-element.60), channel_id=1, source_target_pairs={{0,2},{1,3},{2,0},{3,1},{4,6},{5,7},{6,4},{7,5},{8,10},{9,11},{10,... | collective-permute-start | bytes 393224 | tf_op jit(solution)/shard_map/ppermute | solution.py:463
  34.0 1.7 %collective-permute-start.13 = (f32[128,256]{1,0:T(8,128)S(1)}, f32[128,256]{1,0:T(8,128)S(1)}, u32[]{:S(2)}, u32[]{:S(2)}) collective-permute-start(f32[128,256]{1,0:T(8,128)S(1)} %get-tuple-element.61), channel_id=1, source_target_pairs={{0,3},{1,2},{2,1},{3,0},{4,7},{5,6},{6,5},{7,4},{8,11},{9,10},{10,... | collective-permute-start | bytes 393224 | tf_op jit(solution)/shard_map/ppermute | solution.py:463
  35.6 1.6 %collective-permute-start.9 = (f32[96,256]{1,0:T(8,128)S(1)}, f32[96,256]{1,0:T(8,128)S(1)}, u32[]{:S(2)}, u32[]{:S(2)}) collective-permute-start(f32[96,256]{1,0:T(8,128)S(1)} %get-tuple-element.54), channel_id=1, source_target_pairs={{0,2},{1,3},{2,0},{3,1},{4,6},{5,7},{6,4},{7,5},{8,10},{9,11},{10,... | collective-permute-start | bytes 294920 | tf_op jit(solution)/shard_map/ppermute | solution.py:463
  37.2 0.0 collective-permute-done.14.near1
  37.2 1.6 %collective-permute-start.10 = (f32[96,256]{1,0:T(8,128)S(1)}, f32[96,256]{1,0:T(8,128)S(1)}, u32[]{:S(2)}, u32[]{:S(2)}) collective-permute-start(f32[96,256]{1,0:T(8,128)S(1)} %get-tuple-element.55), channel_id=1, source_target_pairs={{0,3},{1,2},{2,1},{3,0},{4,7},{5,6},{6,5},{7,4},{8,11},{9,10},{10,... | collective-permute-start | bytes 294920 | tf_op jit(solution)/shard_map/ppermute | solution.py:463
  38.9 0.0 copy-done
  38.9 1.1 %shard_map.80 = (bf16[512,1024]{1,0:T(8,128)(2,1)S(1)}, bf16[384,1024]{1,0:T(8,128)(2,1)S(1)}, bf16[512,1024]{1,0:T(8,128)(2,1)S(1)}, bf16[384,1024]{1,0:T(8,128)(2,1)S(1)}) custom-call(s32[1]{0:T(128)} %bitcast.place, f32[4,2,112,128]{3,2,1,0:T(8,128)S(1)} %copy-done, f32[96,256]{1,0:T(8,128)S(1)} %get-tuple-element.56.after.near0), custom_call_target="tpu_custom_call" | custom-call | tf_op jit(solution)/shard_map/pallas_call | solution.py:517
  39.9 0.0 collective-permute-done.11.got1
  40.0 0.0 collective-permute-done.12.got2
  40.0 2.5 %collective-permute-done.13.got3 = f32[128,256]{1,0:T(8,128)S(1)} collective-permute-done((f32[128,256]{1,0:T(8,128)S(1)}, f32[128,256]{1,0:T(8,128)S(1)}, u32[]{:S(2)}, u32[]{:S(2)}) %collective-permute-start.13) | collective-permute-done | bytes 131104 | tf_op jit(solution)/shard_map/ppermute | solution.py:463
  42.5 1.6 %shard_map.81.part = f32[256,1024]{1,0:T(8,128)S(1)} custom-call(f32[128,256]{1,0:T(8,128)S(1)} %get-tuple-element.53.after.got0, f32[128,256]{1,0:T(8,128)S(1)} %collective-permute-done.11.got1, f32[128,256]{1,0:T(8,128)S(1)} %collective-permute-done.12.got2, f32[128,256]{1,0:T(8,128)S(1)} %collective-permute-done.13.got3, ...), custom_call_target="tpu_custom_call" | custom-call | tf_op jit(solution)/shard_map/pallas_call | solution.py:522
  44.0 0.0 collective-permute-done.9.got2
  44.1 2.0 %collective-permute-done.10.got3 = f32[96,256]{1,0:T(8,128)S(1)} collective-permute-done((f32[96,256]{1,0:T(8,128)S(1)}, f32[96,256]{1,0:T(8,128)S(1)}, u32[]{:S(2)}, u32[]{:S(2)}) %collective-permute-start.10) | collective-permute-done | bytes 98336 | tf_op jit(solution)/shard_map/ppermute | solution.py:463
  46.1 1.7 %shard_map.82 = f32[256,1024]{1,0:T(8,128)} custom-call(f32[96,256]{1,0:T(8,128)S(1)} %collective-permute-done.9.got2, f32[96,256]{1,0:T(8,128)S(1)} %collective-permute-done.10.got3, bf16[384,1024]{1,0:T(8,128)(2,1)S(1)} %get-tuple-element.57.hi1.final_hi, bf16[384,1024]{1,0:T(8,128)(2,1)S(1)} %get-tuple-element.58.lo1.final_lo, f32[256,1024]{1,0:T(8,128)S(1)} %shard_map.81.part), custom_call_target="tpu_custom_call" | custom-call | tf_op jit(solution)/shard_map/pallas_call | solution.py:525
  (1 shorter events, 0.0 us)
Async XLA Ops:
  1.3 8.4 %collective-permute-start.2 = (f32[1,5]{1,0:T(1,128)S(1)}, f32[1,5]{1,0:T(1,128)S(1)}, u32[]{:S(2)}, u32[]{:S(2)}) collective-permute-start(f32[1,5]{1,0:T(1,128)S(1)} %bitcast.2), channel_id=1, source_target_pairs={{0,3},{1,2},{2,1},{3,0},{4,7},{5,6},{6,5},{7,4},{8,11},{9,10},{10,... | collective-permute-start | bytes 68 | tf_op jit(solution)/shard_map/ppermute | solution.py:463
  5.6 4.1 %collective-permute-start.1 = (f32[1,5]{1,0:T(1,128)S(1)}, f32[1,5]{1,0:T(1,128)S(1)}, u32[]{:S(2)}, u32[]{:S(2)}) collective-permute-start(f32[1,5]{1,0:T(1,128)S(1)} %bitcast.3), channel_id=1, source_target_pairs={{0,2},{1,3},{2,0},{3,1},{4,6},{5,7},{6,4},{7,5},{8,10},{9,11},{10,... | collective-permute-start | bytes 68 | tf_op jit(solution)/shard_map/ppermute | solution.py:463
  7.4 2.3 %collective-permute-start = (f32[1,5]{1,0:T(1,128)S(1)}, f32[1,5]{1,0:T(1,128)S(1)}, u32[]{:S(2)}, u32[]{:S(2)}) collective-permute-start(f32[1,5]{1,0:T(1,128)S(1)} %bitcast.4), channel_id=1, source_target_pairs={{0,1},{1,0},{2,3},{3,2},{4,5},{5,4},{6,7},{7,6},{8,9},{9,8},{10,11... | collective-permute-start | bytes 68 | tf_op jit(solution)/shard_map/ppermute | solution.py:463
  11.0 10.3 %copy-start.2 = (s32[1,2]{1,0:T(1,128)S(1)}, s32[1,2]{1,0:T(1,128)}, u32[]{:S(2)}) copy-start(s32[1,2]{1,0:T(1,128)} %shift.3) | copy-start | bytes 28
  11.0 10.3 %copy-start.3 = (f32[1,5]{1,0:T(1,128)S(1)}, f32[1,5]{1,0:T(1,128)}, u32[]{:S(2)}) copy-start(f32[1,5]{1,0:T(1,128)} %gains.3) | copy-start | bytes 64
  11.0 7.4 %collective-permute-start.7 = (f32[5,64,128]{2,1,0:T(8,128)S(1)}, f32[5,64,128]{2,1,0:T(8,128)S(1)}, u32[]{:S(2)}, u32[]{:S(2)}) collective-permute-start(f32[5,64,128]{2,1,0:T(8,128)S(1)} %get-tuple-element.49), channel_id=1, source_target_pairs={{0,2},{1,3},{2,0},{3,1},{4,6},{5,7},{6,4},{7,5},{8,10},{9,11},{10,... | collective-permute-start | bytes 491528 | tf_op jit(solution)/shard_map/ppermute | solution.py:463
  12.7 10.5 %collective-permute-start.8 = (f32[5,64,128]{2,1,0:T(8,128)S(1)}, f32[5,64,128]{2,1,0:T(8,128)S(1)}, u32[]{:S(2)}, u32[]{:S(2)}) collective-permute-start(f32[5,64,128]{2,1,0:T(8,128)S(1)} %get-tuple-element.50), channel_id=1, source_target_pairs={{0,3},{1,2},{2,1},{3,0},{4,7},{5,6},{6,5},{7,4},{8,11},{9,10},{10,... | collective-permute-start | bytes 491528 | tf_op jit(solution)/shard_map/ppermute | solution.py:463
  16.9 6.2 %copy-start.1 = (f32[2,512]{1,0:T(2,128)S(1)}, f32[2,512]{1,0:T(2,128)}, u32[]{:S(2)}) copy-start(f32[2,512]{1,0:T(2,128)} %constant.13.clone.odd) | copy-start | bytes 12292
  17.0 6.2 %collective-permute-start.6 = (f32[5,64,128]{2,1,0:T(8,128)S(1)}, f32[5,64,128]{2,1,0:T(8,128)S(1)}, u32[]{:S(2)}, u32[]{:S(2)}) collective-permute-start(f32[5,64,128]{2,1,0:T(8,128)S(1)} %get-tuple-element.48), channel_id=1, source_target_pairs={{0,1},{1,0},{2,3},{3,2},{4,5},{5,4},{6,7},{7,6},{8,9},{9,8},{10,11... | collective-permute-start | bytes 491528 | tf_op jit(solution)/shard_map/ppermute | solution.py:463
  17.1 10.1 %collective-permute-start.3 = (f32[5,64,128]{2,1,0:T(8,128)S(1)}, f32[5,64,128]{2,1,0:T(8,128)S(1)}, u32[]{:S(2)}, u32[]{:S(2)}) collective-permute-start(f32[5,64,128]{2,1,0:T(8,128)S(1)} %get-tuple-element.44), channel_id=1, source_target_pairs={{0,1},{1,0},{2,3},{3,2},{4,5},{5,4},{6,7},{7,6},{8,9},{9,8},{10,11... | collective-permute-start | bytes 491528 | tf_op jit(solution)/shard_map/ppermute | solution.py:463
  17.6 9.6 %collective-permute-start.4 = (f32[5,64,128]{2,1,0:T(8,128)S(1)}, f32[5,64,128]{2,1,0:T(8,128)S(1)}, u32[]{:S(2)}, u32[]{:S(2)}) collective-permute-start(f32[5,64,128]{2,1,0:T(8,128)S(1)} %get-tuple-element.45), channel_id=1, source_target_pairs={{0,2},{1,3},{2,0},{3,1},{4,6},{5,7},{6,4},{7,5},{8,10},{9,11},{10,... | collective-permute-start | bytes 491528 | tf_op jit(solution)/shard_map/ppermute | solution.py:463
  18.4 10.6 %collective-permute-start.5 = (f32[5,64,128]{2,1,0:T(8,128)S(1)}, f32[5,64,128]{2,1,0:T(8,128)S(1)}, u32[]{:S(2)}, u32[]{:S(2)}) collective-permute-start(f32[5,64,128]{2,1,0:T(8,128)S(1)} %get-tuple-element.46), channel_id=1, source_target_pairs={{0,3},{1,2},{2,1},{3,0},{4,7},{5,6},{6,5},{7,4},{8,11},{9,10},{10,... | collective-permute-start | bytes 491528 | tf_op jit(solution)/shard_map/ppermute | solution.py:463
  29.1 9.8 %copy-start = (f32[4,2,112,128]{3,2,1,0:T(8,128)S(1)}, f32[4,2,112,128]{3,2,1,0:T(8,128)}, u32[]{:S(2)}) copy-start(f32[4,2,112,128]{3,2,1,0:T(8,128)} %constant.14.clone.first) | copy-start | bytes 1376260
  31.7 5.5 %collective-permute-start.14 = (f32[96,256]{1,0:T(8,128)S(1)}, f32[96,256]{1,0:T(8,128)S(1)}, u32[]{:S(2)}, u32[]{:S(2)}) collective-permute-start(f32[96,256]{1,0:T(8,128)S(1)} %get-tuple-element.62), channel_id=1, source_target_pairs={{0,1},{1,0},{2,3},{3,2},{4,5},{5,4},{6,7},{7,6},{8,9},{9,8},{10,11... | collective-permute-start | bytes 294920 | tf_op jit(solution)/shard_map/ppermute | solution.py:463
  32.0 8.0 %collective-permute-start.11 = (f32[128,256]{1,0:T(8,128)S(1)}, f32[128,256]{1,0:T(8,128)S(1)}, u32[]{:S(2)}, u32[]{:S(2)}) collective-permute-start(f32[128,256]{1,0:T(8,128)S(1)} %get-tuple-element.59), channel_id=1, source_target_pairs={{0,1},{1,0},{2,3},{3,2},{4,5},{5,4},{6,7},{7,6},{8,9},{9,8},{10,11... | collective-permute-start | bytes 393224 | tf_op jit(solution)/shard_map/ppermute | solution.py:463
  32.3 7.6 %collective-permute-start.12 = (f32[128,256]{1,0:T(8,128)S(1)}, f32[128,256]{1,0:T(8,128)S(1)}, u32[]{:S(2)}, u32[]{:S(2)}) collective-permute-start(f32[128,256]{1,0:T(8,128)S(1)} %get-tuple-element.60), channel_id=1, source_target_pairs={{0,2},{1,3},{2,0},{3,1},{4,6},{5,7},{6,4},{7,5},{8,10},{9,11},{10,... | collective-permute-start | bytes 393224 | tf_op jit(solution)/shard_map/ppermute | solution.py:463
  34.0 8.5 %collective-permute-start.13 = (f32[128,256]{1,0:T(8,128)S(1)}, f32[128,256]{1,0:T(8,128)S(1)}, u32[]{:S(2)}, u32[]{:S(2)}) collective-permute-start(f32[128,256]{1,0:T(8,128)S(1)} %get-tuple-element.61), channel_id=1, source_target_pairs={{0,3},{1,2},{2,1},{3,0},{4,7},{5,6},{6,5},{7,4},{8,11},{9,10},{10,... | collective-permute-start | bytes 393224 | tf_op jit(solution)/shard_map/ppermute | solution.py:463
  35.6 8.4 %collective-permute-start.9 = (f32[96,256]{1,0:T(8,128)S(1)}, f32[96,256]{1,0:T(8,128)S(1)}, u32[]{:S(2)}, u32[]{:S(2)}) collective-permute-start(f32[96,256]{1,0:T(8,128)S(1)} %get-tuple-element.54), channel_id=1, source_target_pairs={{0,2},{1,3},{2,0},{3,1},{4,6},{5,7},{6,4},{7,5},{8,10},{9,11},{10,... | collective-permute-start | bytes 294920 | tf_op jit(solution)/shard_map/ppermute | solution.py:463
  37.2 8.9 %collective-permute-start.10 = (f32[96,256]{1,0:T(8,128)S(1)}, f32[96,256]{1,0:T(8,128)S(1)}, u32[]{:S(2)}, u32[]{:S(2)}) collective-permute-start(f32[96,256]{1,0:T(8,128)S(1)} %get-tuple-element.55), channel_id=1, source_target_pairs={{0,3},{1,2},{2,1},{3,0},{4,7},{5,6},{6,5},{7,4},{8,11},{9,10},{10,... | collective-permute-start | bytes 294920 | tf_op jit(solution)/shard_map/ppermute | solution.py:463
